TPU v7x, 32 devices: a whole 2x2x4 slice. The times are simulated.
32 devices in a mesh: slab: 16 (over z, x, core), grp: 2 (over y).
Axes of the slice: x: 2, y: 2, z: 4, core: 2. Of those that a mesh axis runs over, the one named last changes fastest.
Arguments:
- capture: float32 [2, 262144], P(None, ('slab', 'grp')), may hold values from -6 to 6
- dropped: int32 [16], P('slab'), may hold values from 0 to 8191
Outputs:
- max_held: float32 [128, 128, 128], P('slab', 'grp')
- coherent: float32 [2, 128, 128, 128], P(None, 'slab', 'grp')
All inputs are finite; a program needn't handle non-finite values.
Results may differ from a plain program's by a relative error of at most 0.0001.
Values sent between devices are 32-bit elements; how exact they have to be, the bound alone decides.
No kernel may reach another device: no remote copies, remote signals or barrier semaphores. Data moves between devices by JAX's collectives and lax.ppermute only.
A program may use at most 128 MiB of HBM per device.

v0:
```python
import math

import jax
import jax.numpy as jnp
import ml_dtypes
import numpy as np
from jax import lax
from jax.experimental import pallas as pl
from jax.experimental.pallas import tpu as pltpu
from jax.sharding import PartitionSpec as P


NCH = 256
HOP = 64
KW = 128
LW = 128
Q = 128
BLOCKS = 2
PERIOD = Q * HOP
TURN = 2 * PERIOD
LANES = 128
PAD = 8


def halves(table):
    high = table.astype(ml_dtypes.bfloat16)
    low = (table - high.astype(np.float64)).astype(ml_dtypes.bfloat16)
    return high, low


def lower_order(width):
    quarter = width // 4
    return np.concatenate([4 * np.arange(quarter) + kappa for kappa in (0, 2, 1, 3)])


def upper_order():
    return np.concatenate([np.arange(0, LW, 2), np.arange(1, LW, 2)])


def window_rows():
    taps = np.arange(NCH)
    window = 0.5 - 0.5 * np.cos(2.0 * np.pi * taps / NCH)
    scaled = window / np.sqrt(np.sum(window * window))
    rows = np.zeros((8, LANES))
    for lag in range(NCH // HOP):
        piece = scaled[lag * HOP : (lag + 1) * HOP]
        rows[lag] = np.concatenate([piece, piece])
    return rows.astype(np.float32)


def channel_tables(groups):
    width = KW // groups
    half = width // 2
    taps = np.arange(NCH // 2)
    even = np.zeros((groups, NCH, NCH))
    odd = np.zeros((groups, NCH, NCH))

    def columns(channels):
        turns = 2.0 * np.pi * (taps[:, None] * channels[None, :] % NCH) / NCH
        cosine, sine = np.cos(turns), np.sin(turns)
        real = np.concatenate([cosine[:HOP], sine[:HOP], cosine[HOP:], sine[HOP:]])
        imag = np.concatenate([-sine[:HOP], cosine[:HOP], -sine[HOP:], cosine[HOP:]])
        return real, imag

    upper = KW + upper_order()
    for group in range(groups):
        lower = group * width + lower_order(width)
        real, imag = columns(upper[: LW // 2])
        even[group, :, 0:64], even[group, :, 64:128] = real, imag
        real, imag = columns(upper[LW // 2 :])
        odd[group, :, 0:64], odd[group, :, 64:128] = imag, real
        real, imag = columns(lower[:half])
        even[group, :, 128 : 128 + half] = real
        even[group, :, 192 : 192 + half] = imag
        real, imag = columns(lower[half:])
        odd[group, :, 128 + half : 128 + width] = real
        odd[group, :, 192 + half : 192 + width] = imag
    return halves(even) + halves(odd)


def turn_tables(bins, width):
    pairs = bins // 2
    rows = -(-(6 + pairs) // 8) * 8
    frame = np.arange(LANES)
    fixed = np.zeros((3, rows, LANES), np.int64)
    ticks = np.zeros((3, rows, LANES), np.int64)
    for place, kappa in enumerate((0, 2, 1, 3)):
        ticks[0, place] = bins - 1
        ticks[1, place] = 2 * bins
        fixed[0, place] = (bins - 1) * HOP * frame + (TURN // 4) * kappa * frame
        fixed[1, place] = 2 * bins * HOP * frame
    for pair in range(pairs):
        ticks[0, 4 + pair] = 2 * pair + 1
        fixed[0, 4 + pair] = (2 * pair + 1) * HOP * frame
    order = lower_order(width)
    scale = TURN // NCH
    ticks[0, 4 + pairs] = scale * np.concatenate([order, order])
    ticks[2, 4 + pairs] = scale * width
    ticks[0, 5 + pairs] = scale * (KW + upper_order())
    return fixed.astype(np.int32), ticks.astype(np.int32)


def cos_sin(angle):
    shifted = angle + TURN // 8
    quadrant = lax.shift_right_logical(shifted, int(math.log2(TURN // 4))) & 3
    remain = (shifted & (TURN // 4 - 1)) - TURN // 8
    x = remain.astype(jnp.float32) * np.float32(2.0 * math.pi / TURN)
    y = x * x
    sine = x * (1.0 + y * (-1.0 / 6 + y * (1.0 / 120 + y * (-1.0 / 5040 + y * (1.0 / 362880)))))
    cosine = 1.0 + y * (-0.5 + y * (1.0 / 24 + y * (-1.0 / 720 + y * (1.0 / 40320))))
    swap = (quadrant & 1) == 1
    out_cos = jnp.where(swap, sine, cosine)
    out_sin = jnp.where(swap, cosine, sine)
    out_cos = jnp.where((quadrant == 1) | (quadrant == 2), -out_cos, out_cos)
    out_sin = jnp.where(quadrant >= 2, -out_sin, out_sin)
    return out_cos, out_sin


def split(value):
    high = value.astype(jnp.bfloat16)
    low = (value - high.astype(jnp.float32)).astype(jnp.bfloat16)
    return high, low


def dot32(left, right):
    return lax.dot_general(
        left, right, (((1,), (0,)), ((), ())), preferred_element_type=jnp.float32
    )


def dot3(left, right):
    return dot32(left[0], right[0]) + dot32(left[1], right[0]) + dot32(left[0], right[1])


def small_table(width):
    order = KW + upper_order()
    phase = (np.arange(8)[:, None] * order[None, :]) % 4
    quarter_cos = np.array([1.0, 0.0, -1.0, 0.0])[phase]
    quarter_sin = np.array([0.0, 1.0, 0.0, -1.0])[phase]
    sign = np.where(np.arange(LANES) < width, 1.0, -1.0)[None, :]
    parts = [window_rows(), quarter_cos, quarter_sin, np.tile(sign, (8, 1))]
    return np.concatenate(parts).astype(np.float32)


def surfaces(plan, spots, pieces, slabs, groups, count, notes=(), carried=None):
    piece_at, note_at, tail_at, first_block = spots
    bins = Q // slabs
    pairs = bins // 2
    width = KW // groups
    quarter = width // 4
    blocks = slabs * BLOCKS
    fixed, ticks = turn_tables(bins, width)
    rows = fixed.shape[1]
    weights = channel_tables(groups)
    small = small_table(width)
    arrays = len(pieces)
    depth = pieces[0].shape[0]
    norm = 1.0 / math.sqrt(Q)
    blend = 1.0 / math.sqrt(slabs * BLOCKS)
    opening = carried is None
    inputs = arrays + len(notes) + (0 if opening else 6)
    outputs = 6 if opening else 2

    def kernel(plan_ref, fixed_ref, ticks_ref, small_ref, even_h, even_l, odd_h, odd_l, *rest):
        piece_refs = rest[:arrays]
        note_refs = rest[arrays : arrays + len(notes)]
        out_refs = rest[inputs : inputs + outputs]
        rest = rest[inputs + outputs :] if opening else rest[arrays:]
        if opening:
            acc_re, acc_im, acc_sq, cos_ref, sin_ref, tails = out_refs
            frames, drops = rest[:2]
            scratch = rest[2:]
        else:
            old_re, old_im, old_sq, cos_ref, sin_ref, tails = rest[:6]
            held_ref, coherent_ref = out_refs
            frames, acc_re, acc_im, acc_sq = rest[8:12]
            scratch = rest[12:]
        slots = ((scratch[0:4], scratch[4:8]), (scratch[8:12], scratch[12:16]))
        slab = plan_ref[0]
        group = plan_ref[1]
        frames[pl.ds(0, PAD), :] = jnp.zeros((PAD, LANES), jnp.float32)
        for array in range(arrays):
            for item in range(depth):
                place = plan_ref[piece_at + array * depth + item]
                start = pl.multiple_of(PAD + place * Q, 8)
                frames[pl.ds(start, Q), :] = piece_refs[array][item, pl.ds(0, Q), :]
                if opening:
                    start = pl.multiple_of((place // BLOCKS) * PAD, 8)
                    drops[pl.ds(start, PAD), :] = piece_refs[array][item, pl.ds(Q, PAD), :]
        for array in range(len(notes)):
            for item in range(depth):
                place = plan_ref[note_at + array * depth + item]
                tile = note_refs[array][item]
                frames[pl.ds(pl.multiple_of((place + 1) * Q, 8), PAD), :] = tile
                drops[pl.ds(pl.multiple_of((place // BLOCKS) * PAD, 8), PAD), :] = tile
        for item in range(depth):
            at = pl.ds(pl.multiple_of((plan_ref[tail_at + item] + 1) * Q, 8), PAD)
            if opening:
                tails[item] = frames[at, :]
            else:
                frames[at, :] = tails[item]

        def make_turns():
            base = fixed_ref[0] + slab * fixed_ref[1] + group * fixed_ref[2]
            rate = ticks_ref[0] + slab * ticks_ref[1] + group * ticks_ref[2]

            def stamp_step(n, total):
                dropped = drops[pl.ds(pl.multiple_of(n * PAD, 8), PAD), :][0:1]
                dropped = jnp.broadcast_to(dropped, (PAD, LANES)).astype(jnp.int32)
                total = (total + dropped) & (PERIOD - 1)
                wide = jnp.concatenate([total] * (rows // PAD), axis=0)
                cosine, sine = cos_sin((base + rate * wide) & (TURN - 1))
                at = pl.ds(pl.multiple_of(n * rows, 8), rows)
                cos_ref[at, :] = cosine
                sin_ref[at, :] = sine
                return total

            start = jnp.zeros((PAD, LANES), jnp.int32)
            lax.fori_loop(0, slabs, stamp_step, start, unroll=min(slabs, 16))

        if opening:
            acc_re[...] = jnp.zeros_like(acc_re)
            acc_im[...] = jnp.zeros_like(acc_im)
            acc_sq[...] = jnp.zeros_like(acc_sq)
            make_turns()
        else:
            acc_re[...] = old_re[...]
            acc_im[...] = old_im[...]
            acc_sq[...] = old_sq[...]
        lane = lax.broadcasted_iota(jnp.int32, (Q, LANES), 1)
        left_half = lane < LANES // 2

        def channelize(places, targets):
            evens = []
            odds = []
            for place in places:
                start = pl.multiple_of(place * Q, Q)
                lags = [
                    frames[pl.ds(start + (PAD - 3 + lag), Q), :] * small_ref[lag : lag + 1]
                    for lag in range(4)
                ]
                evens.append(jnp.concatenate([lags[0] + lags[2], lags[1] + lags[3]], axis=1))
                odds.append(jnp.concatenate([lags[0] - lags[2], lags[1] - lags[3]], axis=1))
            both_even = split(jnp.concatenate(evens, axis=0))
            both_odd = split(jnp.concatenate(odds, axis=0))
            from_even = dot3(both_even, (even_h[group], even_l[group]))
            from_odd = dot3(both_odd, (odd_h[group], odd_l[group]))
            for index, (place, slot) in enumerate(zip(places, targets)):
                part = slice(index * Q, (index + 1) * Q)
                finish(place, slot, from_even[part], from_odd[part])

        def finish(place, slot, from_even, from_odd):
            rhs_h, rhs_l, center_re, center_im = slot
            turn = pl.multiple_of((place // BLOCKS) * rows, 8)
            cos_rows = cos_ref[pl.ds(turn, rows), :]
            sin_rows = sin_ref[pl.ds(turn, rows), :]
            row_k, row_l = 4 + pairs, 5 + pairs
            low_cos = cos_rows[row_k : row_k + 1]
            low_sin = sin_rows[row_k : row_k + 1] * small_ref[24:25]
            up_cos = cos_rows[row_l : row_l + 1]
            up_sin = sin_rows[row_l : row_l + 1]
            table_cos = small_ref[8:16] * up_cos - small_ref[16:24] * up_sin
            table_sin = small_ref[16:24] * up_cos + small_ref[8:16] * up_sin
            table_cos = jnp.concatenate([table_cos] * (Q // 8), axis=0)
            table_sin = jnp.concatenate([table_sin] * (Q // 8), axis=0)
            up_even, up_odd = from_even[:, :LANES], from_odd[:, :LANES]
            up_re = jnp.where(left_half, up_even, up_odd)
            up_im = pltpu.roll(jnp.where(left_half, up_odd, up_even), LANES // 2, 1)
            re_h, re_l = split(up_re * table_cos + up_im * table_sin)
            im_h, im_l = split(up_im * table_cos - up_re * table_sin)
            for ref, real, imag in ((rhs_h, re_h, im_h), (rhs_l, re_l, im_l)):
                ref[0:Q, 0:LW] = real
                ref[0:Q, LW : 2 * LW] = -imag
                ref[Q : 2 * Q, 0:LW] = imag
                ref[Q : 2 * Q, LW : 2 * LW] = real
            low = from_even[:, LANES:] + from_odd[:, LANES:]
            low = low * low_cos + pltpu.roll(low, LANES // 2, 1) * low_sin
            low = low.T * norm
            low_re, low_im = low[:width], low[width:]
            for part in range(4):
                at = slice(part * quarter, (part + 1) * quarter)
                c = cos_rows[part : part + 1]
                s = sin_rows[part : part + 1]
                center_re[at] = low_re[at] * c + low_im[at] * s
                center_im[at] = low_im[at] * c - low_re[at] * s

        def correlate(place, slot):
            rhs_h, rhs_l, center_re, center_im = slot
            turn = pl.multiple_of((place // BLOCKS) * rows, 8)
            cos_rows = cos_ref[pl.ds(turn, rows), :]
            sin_rows = sin_ref[pl.ds(turn, rows), :]
            right = (rhs_h[...], rhs_l[...])
            group_size = min(pairs, 4)
            for base_pair in range(0, pairs, group_size):
                parts = []
                for pair in range(base_pair, base_pair + group_size):
                    c = cos_rows[4 + pair : 5 + pair]
                    s = sin_rows[4 + pair : 5 + pair]
                    t1 = center_re[...] * c
                    t2 = center_im[...] * s
                    t3 = center_im[...] * c
                    t4 = center_re[...] * s
                    parts.append(jnp.concatenate([t1 + t2, t3 - t4], axis=1))
                    parts.append(jnp.concatenate([t1 - t2, t3 + t4], axis=1))
                left = split(jnp.concatenate(parts, axis=0))
                total = dot3(left, right)
                for index in range(2 * group_size):
                    pair = base_pair + index // 2
                    at = (pairs - 1 - pair if index % 2 else pairs + pair) * width
                    put = slice(at, at + width)
                    re = total[index * width : (index + 1) * width, :LW]
                    im = total[index * width : (index + 1) * width, LW:]
                    acc_re[put] = acc_re[put] + re
                    acc_im[put] = acc_im[put] + im
                    acc_sq[put] = jnp.maximum(acc_sq[put], re * re + im * im)

        def block_at(index):
            return plan_ref[first_block + index]

        def work(first, side, more):
            if more:
                channelize((block_at(first + 2), block_at(first + 3)), slots[1 - side])
            for item in range(2):
                correlate(block_at(first + item), slots[side][item])

        def step(index, carry):
            work(4 * index, 0, True)
            work(4 * index + 2, 1, True)
            return carry

        channelize((block_at(0), block_at(1)), slots[0])
        lax.fori_loop(0, count // 4 - 1, step, 0)
        work(count - 4, 0, True)
        work(count - 2, 1, False)
        if opening:
            return
        lanes = lax.broadcasted_iota(jnp.int32, (quarter, LW), 1)
        source = lax.shift_right_logical(lanes, 1) + (LW // 2) * (lanes & 1)

        def natural(value):
            return jnp.take_along_axis(value, source, axis=1, mode="promise_in_bounds")

        for bin_index in range(bins):
            for part, kappa in enumerate((0, 2, 1, 3)):
                first = bin_index * width + part * quarter
                take = slice(first, first + quarter)
                put = pl.ds(kappa, quarter, stride=4)
                held_ref[bin_index, put, :] = natural(jnp.sqrt(acc_sq[take]))
                coherent_ref[0, bin_index, put, :] = natural(acc_re[take] * blend)
                coherent_ref[1, bin_index, put, :] = natural(acc_im[take] * blend)

    vmem = pl.BlockSpec(memory_space=pltpu.VMEM)
    slot = [
        pltpu.VMEM((2 * Q, 2 * LW), jnp.bfloat16),
        pltpu.VMEM((2 * Q, 2 * LW), jnp.bfloat16),
        pltpu.VMEM((width, Q), jnp.float32),
        pltpu.VMEM((width, Q), jnp.float32),
    ]
    sums = [(bins * width, LW)] * 3
    if opening:
        shapes = sums + [(slabs * rows, LANES)] * 2 + [(depth, PAD, LANES)]
        scratch = [(PAD + blocks * Q, LANES), (slabs * PAD, LANES)]
    else:
        shapes = [(bins, width, LW), (2, bins, width, LW)]
        scratch = [(PAD + blocks * Q, LANES)] + sums
    work = 2 * 3 * count * NCH * NCH * (2 * Q + 2 * bins * width // 2)
    return pl.pallas_call(
        kernel,
        in_specs=[pl.BlockSpec(memory_space=pltpu.SMEM)] + [vmem] * (7 + inputs),
        out_specs=[vmem] * outputs,
        scratch_shapes=[pltpu.VMEM(shape, jnp.float32) for shape in scratch] + slot * 4,
        out_shape=[jax.ShapeDtypeStruct(shape, jnp.float32) for shape in shapes],
        compiler_params=pltpu.CompilerParams(vmem_limit_bytes=(PAD + blocks * Q) * 4 * LANES + 12 * 1024 * 1024),
        cost_estimate=pl.CostEstimate(flops=work, transcendentals=0, bytes_accessed=4 * 1024 * 1024),
        name="surfaces_first" if opening else "surfaces_last",
    )(
        plan,
        jnp.asarray(fixed),
        jnp.asarray(ticks),
        jnp.asarray(small),
        *[jnp.asarray(table) for table in weights],
        *pieces,
        *notes,
        *(() if opening else carried),
    )


def on_device(capture, dropped):
    slabs = lax.axis_size("slab")
    groups = lax.axis_size("grp")
    slab = lax.axis_index("slab")
    group = lax.axis_index("grp")
    axes = ("slab", "grp")
    total = slabs * groups
    outer = slabs // 4
    hops = capture.shape[1] // HOP
    own = capture.reshape(2, hops, HOP).transpose(1, 0, 2).reshape(hops, 2 * HOP)
    lead = NCH // HOP - 1
    ticks = jnp.broadcast_to(dropped.astype(jnp.float32)[:, None], (PAD - lead, LANES))
    own = jnp.concatenate([own, ticks, own[hops - lead :]], axis=0)[None]

    def split_index(flat):
        return flat // (4 * groups), (flat // (2 * groups)) % 2, (flat // groups) % 2, flat % groups

    def joined(far, side, core, member):
        return ((far * 2 + side) * 2 + core) * groups + member

    def moved(array, by):
        pairs = []
        for flat in range(total):
            far, side, core, member = split_index(flat)
            target = joined(
                (far + by[0]) % outer, (side + by[1]) % 2, (core + by[2]) % 2, (member + by[3]) % groups
            )
            pairs.append((flat, target))
        return lax.ppermute(array, axes, pairs)

    line = [own] + [moved(own, (step, 0, 0, 0)) for step in range(1, outer)]
    line = jnp.concatenate(line, axis=0)
    tiles = line[:, hops:, :]
    note_steps = [(1, core, member) for core in range(2) for member in range(groups)]
    notes = []
    for by in note_steps:
        notes.append(moved(tiles, (0,) + by))
    near = [line] + [moved(line, (0, 0, 0, member)) for member in range(1, groups)]
    far = [moved(line, (0, 1, 0, 0))]
    far += [moved(piece, (0, 1, 0, 0)) for piece in near[1:]]
    near_steps = [(0, 0, member) for member in range(groups)]
    far_steps = [(1, 0, member) for member in range(groups)]
    cores = []
    for piece in near:
        cores.append(moved(piece, (0, 0, 1, 0)))
    near += cores
    near_steps += [(side, 1, member) for side, _, member in near_steps]
    me_far, me_side, me_core, me_member = split_index(slab * groups + group)

    def places(steps):
        return [
            joined(
                (me_far - step) % outer,
                (me_side - side) % 2,
                (me_core - core) % 2,
                (me_member - member) % groups,
            )
            for side, core, member in steps
            for step in range(outer)
        ]

    first_blocks = []
    last_blocks = []
    for step in range(outer):
        for core in range(2):
            for member in range(groups):
                first_blocks.append(joined(step, me_side, core, member))
                last_blocks.append(joined(step, 1 - me_side, core, member))
    tail_places = [joined(step, me_side, 1, groups - 1) for step in range(outer)]
    far_steps += [(side, 1, member) for side, _, member in far_steps]
    parts = [places(near_steps), places(far_steps), places(note_steps), tail_places]
    parts += [first_blocks, last_blocks]
    begins = np.cumsum([2] + [len(part) for part in parts])
    near_at, far_at, note_at, tail_at, first_at, last_at = (int(at) for at in begins[:-1])
    plan = [slab, group] + sum(parts, [])
    plan = jnp.stack([jnp.asarray(value, jnp.int32) for value in plan])
    spots = (near_at, note_at, tail_at, first_at)
    carried = surfaces(plan, spots, near, slabs, groups, len(first_blocks), notes=notes)
    far += [moved(far[0], (0, 0, 1, 0))]
    far += [moved(piece, (0, 0, 1, 0)) for piece in far[1:groups]]
    spots = (far_at, note_at, tail_at, last_at)
    held, coherent = surfaces(
        plan, spots, far, slabs, groups, len(last_blocks), carried=carried
    )
    return held, coherent


def solution(mesh):
    in_specs = (P(None, ("slab", "grp")), P("slab"))
    out_specs = (P("slab", "grp", None), P(None, "slab", "grp", None))

    return jax.shard_map(
        on_device, mesh=mesh, in_specs=in_specs, out_specs=out_specs, check_vma=False
    )
```

profile of v0, /device:TPU:0, one launch (start us, length us, event | category | flops | bytes accessed | tf_op | source)
XLA Modules:
  0.0 57.7 jit_solution(4906739236654462706)
XLA Ops:
  0.6 1.0 %reshape.12 = f32[2,128,64]{2,1,0:T(8,128)S(1)} reshape(f32[2,8192]{1,0:T(2,128)} %param.16) | data formatting | bytes 131072 | tf_op jit(solution)/shard_map/reshape | solution.py:397
  1.6 0.1 copy.19
  1.7 0.1 copy.21
  1.8 0.1 slice.10
  2.6 0.1 maximum_bitcast_fusion
  2.7 3.1 %collective-permute-start = (f32[1,136,128]{2,1,0:T(8,128)S(1)}, f32[1,136,128]{2,1,0:T(8,128)S(1)}, u32[]{:S(2)}, u32[]{:S(2)}) collective-permute-start(f32[1,136,128]{2,1,0:T(8,128)S(1)} %maximum_bitcast_fusion), channel_id=1, source_target_pairs={{0,8},{1,9},{2,10},{3,11},{4,12},{5,13},{6,14},{7,15},{8,16},{9,17... | collective-permute-start | bytes 208904 | tf_op jit(solution)/shard_map/ppermute | solution.py:416
  5.8 2.6 %collective-permute-start.1 = (f32[1,136,128]{2,1,0:T(8,128)S(1)}, f32[1,136,128]{2,1,0:T(8,128)S(1)}, u32[]{:S(2)}, u32[]{:S(2)}) collective-permute-start(f32[1,136,128]{2,1,0:T(8,128)S(1)} %maximum_bitcast_fusion), channel_id=1, source_target_pairs={{0,16},{1,17},{2,18},{3,19},{4,20},{5,21},{6,22},{7,23},{8,24},{9,... | collective-permute-start | bytes 208904 | tf_op jit(solution)/shard_map/ppermute | solution.py:416
  8.4 1.3 %collective-permute-start.2 = (f32[1,136,128]{2,1,0:T(8,128)S(1)}, f32[1,136,128]{2,1,0:T(8,128)S(1)}, u32[]{:S(2)}, u32[]{:S(2)}) collective-permute-start(f32[1,136,128]{2,1,0:T(8,128)S(1)} %maximum_bitcast_fusion), channel_id=1, source_target_pairs={{0,24},{1,25},{2,26},{3,27},{4,28},{5,29},{6,30},{7,31},{8,0},{9,1... | collective-permute-start | bytes 208904 | tf_op jit(solution)/shard_map/ppermute | solution.py:416
  9.7 0.6 %collective-permute-done = f32[1,136,128]{2,1,0:T(8,128)S(1)} collective-permute-done((f32[1,136,128]{2,1,0:T(8,128)S(1)}, f32[1,136,128]{2,1,0:T(8,128)S(1)}, u32[]{:S(2)}, u32[]{:S(2)}) %collective-permute-start) | collective-permute-done | bytes 69664 | tf_op jit(solution)/shard_map/ppermute | solution.py:416
  10.3 2.7 %collective-permute-done.1 = f32[1,136,128]{2,1,0:T(8,128)S(1)} collective-permute-done((f32[1,136,128]{2,1,0:T(8,128)S(1)}, f32[1,136,128]{2,1,0:T(8,128)S(1)}, u32[]{:S(2)}, u32[]{:S(2)}) %collective-permute-start.1) | collective-permute-done | bytes 69664 | tf_op jit(solution)/shard_map/ppermute | solution.py:416
  13.1 0.2 collective-permute-done.2
  13.3 1.6 %collective-permute-start.4 = (f32[4,136,128]{2,1,0:T(8,128)S(1)}, f32[4,136,128]{2,1,0:T(8,128)S(1)}, u32[]{:S(2)}, u32[]{:S(2)}) collective-permute-start(f32[4,136,128]{2,1,0:T(8,128)S(1)} %pad_maximum_fusion.rest_0_), channel_id=1, source_target_pairs={{0,1},{1,0},{2,3},{3,2},{4,5},{5,4},{6,7},{7,6},{8,9},{9,8},{10,11... | collective-permute-start | bytes 835592 | tf_op jit(solution)/shard_map/ppermute | solution.py:416
  14.9 1.5 %collective-permute-start.3 = (f32[4,136,128]{2,1,0:T(8,128)S(1)}, f32[4,136,128]{2,1,0:T(8,128)S(1)}, u32[]{:S(2)}, u32[]{:S(2)}) collective-permute-start(f32[4,136,128]{2,1,0:T(8,128)S(1)} %pad_maximum_fusion.rest_0_), channel_id=1, source_target_pairs={{0,4},{1,5},{2,6},{3,7},{4,0},{5,1},{6,2},{7,3},{8,12},{9,13},{10,... | collective-permute-start | bytes 835592 | tf_op jit(solution)/shard_map/ppermute | solution.py:416
  16.4 5.2 %collective-permute-done.4.rest_1_ = f32[4,136,128]{2,1,0:T(8,128)S(1)} collective-permute-done((f32[4,136,128]{2,1,0:T(8,128)S(1)}, f32[4,136,128]{2,1,0:T(8,128)S(1)}, u32[]{:S(2)}, u32[]{:S(2)}) %collective-permute-start.4) | collective-permute-done | bytes 278560 | tf_op jit(solution)/shard_map/ppermute | solution.py:416
  21.6 1.3 %collective-permute-start.5 = (f32[4,136,128]{2,1,0:T(8,128)S(1)}, f32[4,136,128]{2,1,0:T(8,128)S(1)}, u32[]{:S(2)}, u32[]{:S(2)}) collective-permute-start(f32[4,136,128]{2,1,0:T(8,128)S(1)} %collective-permute-done.4.rest_1_), channel_id=1, source_target_pairs={{0,4},{1,5},{2,6},{3,7},{4,0},{5,1},{6,2},{7,3},{8,12},{9,13},{10,... | collective-permute-start | bytes 835592 | tf_op jit(solution)/shard_map/ppermute | solution.py:416
  22.9 0.5 collective-permute-start.9
  23.4 0.8 %collective-permute-start.10 = (f32[4,8,128]{2,1,0:T(8,128)S(1)}, f32[4,8,128]{2,1,0:T(8,128)S(1)}, u32[]{:S(2)}, u32[]{:S(2)}) collective-permute-start(f32[4,8,128]{2,1,0:T(8,128)S(1)} %slice.13), channel_id=1, source_target_pairs={{0,4},{1,5},{2,6},{3,7},{4,0},{5,1},{6,2},{7,3},{8,12},{9,13},{10,... | collective-permute-start | bytes 49160 | tf_op jit(solution)/shard_map/ppermute | solution.py:416
  24.2 5.2 %collective-permute-done.10.rest_4_ = f32[4,8,128]{2,1,0:T(8,128)S(1)} collective-permute-done((f32[4,8,128]{2,1,0:T(8,128)S(1)}, f32[4,8,128]{2,1,0:T(8,128)S(1)}, u32[]{:S(2)}, u32[]{:S(2)}) %collective-permute-start.10) | collective-permute-done | bytes 16416 | tf_op jit(solution)/shard_map/ppermute | solution.py:416
  29.3 2.0 %collective-permute-start.11 = (f32[4,8,128]{2,1,0:T(8,128)S(1)}, f32[4,8,128]{2,1,0:T(8,128)S(1)}, u32[]{:S(2)}, u32[]{:S(2)}) collective-permute-start(f32[4,8,128]{2,1,0:T(8,128)S(1)} %slice.13), channel_id=1, source_target_pairs={{0,5},{1,4},{2,7},{3,6},{4,1},{5,0},{6,3},{7,2},{8,13},{9,12},{10,... | collective-permute-start | bytes 49160 | tf_op jit(solution)/shard_map/ppermute | solution.py:416
  31.4 2.6 %collective-permute-done.11.rest_5_ = f32[4,8,128]{2,1,0:T(8,128)S(1)} collective-permute-done((f32[4,8,128]{2,1,0:T(8,128)S(1)}, f32[4,8,128]{2,1,0:T(8,128)S(1)}, u32[]{:S(2)}, u32[]{:S(2)}) %collective-permute-start.11) | collective-permute-done | bytes 16416 | tf_op jit(solution)/shard_map/ppermute | solution.py:416
  34.0 0.0 collective-permute-start.12
  34.0 3.2 %collective-permute-done.12.rest_6_ = f32[4,8,128]{2,1,0:T(8,128)S(1)} collective-permute-done((f32[4,8,128]{2,1,0:T(8,128)S(1)}, f32[4,8,128]{2,1,0:T(8,128)S(1)}, u32[]{:S(2)}, u32[]{:S(2)}) %collective-permute-start.12) | collective-permute-done | bytes 16416 | tf_op jit(solution)/shard_map/ppermute | solution.py:416
  37.1 0.5 collective-permute-start.13
  37.7 0.2 stack.287.plan_ref
  37.9 1.7 %collective-permute-start.6 = (f32[4,136,128]{2,1,0:T(8,128)S(1)}, f32[4,136,128]{2,1,0:T(8,128)S(1)}, u32[]{:S(2)}, u32[]{:S(2)}) collective-permute-start(f32[4,136,128]{2,1,0:T(8,128)S(1)} %collective-permute-done.3.rest_0_), channel_id=1, source_target_pairs={{0,2},{1,3},{2,0},{3,1},{4,6},{5,7},{6,4},{7,5},{8,10},{9,11},{10,... | collective-permute-start | bytes 835592 | tf_op jit(solution)/shard_map/ppermute | solution.py:416
  39.5 0.0 collective-permute-done.5.rest_1_
  39.5 0.1 collective-permute-start.7
  39.6 1.6 %collective-permute-done.13.rest_7_ = f32[4,8,128]{2,1,0:T(8,128)S(1)} collective-permute-done((f32[4,8,128]{2,1,0:T(8,128)S(1)}, f32[4,8,128]{2,1,0:T(8,128)S(1)}, u32[]{:S(2)}, u32[]{:S(2)}) %collective-permute-start.13) | collective-permute-done | bytes 16416 | tf_op jit(solution)/shard_map/ppermute | solution.py:416
  41.2 0.0 collective-permute-done.8.rest_2_
  41.2 0.0 collective-permute-done.9.rest_3_
  41.3 7.9 %surfaces_first.1 = (f32[512,128]{1,0:T(8,128)S(1)}, f32[512,128]{1,0:T(8,128)S(1)}, f32[512,128]{1,0:T(8,128)S(1)}, f32[256,128]{1,0:T(8,128)S(1)}, f32[256,128]{1,0:T(8,128)S(1)}, /*index=5*/f32[4,8,128]{2,1,0:T(8,128)S(1)}) custom-call(s32[86]{0:T(128)S(1)} %stack.287.plan_ref, s32[3,16,128]{2,1,0:T(8,128)S(1)} %copy-done.4, s32[3,16,128]{2,1,0:T(8,128)S(1)} %copy-done.5, ...), custom_call_target="tpu_custom_call" | custom-call | flops 4831838208 | bytes 4194304 | tf_op jit(solution)/shard_map/surfaces_first/pallas_call | solution.py:367
  49.2 8.5 %surfaces_last.1 = (f32[8,64,128]{2,1,0:T(8,128)}, f32[2,8,64,128]{3,2,1,0:T(8,128)}) custom-call(s32[86]{0:T(128)S(1)} %stack.287.plan_ref, s32[3,16,128]{2,1,0:T(8,128)S(1)} %copy-done.4, s32[3,16,128]{2,1,0:T(8,128)S(1)} %copy-done.5, f32[32,128]{1,0:T(8,128)S(1)} %copy-done.6, bf16[2,256,256]{2,1,0:T(8,128)(2,1)S(1)} %copy-done, ...), custom_call_target="tpu_custom_call" | custom-call | flops 4831838208 | bytes 4194304 | tf_op jit(solution)/shard_map/surfaces_last/pallas_call | solution.py:367
  (24 shorter events, 0.1 us)
Async XLA Ops:
  2.7 7.7 %collective-permute-start = (f32[1,136,128]{2,1,0:T(8,128)S(1)}, f32[1,136,128]{2,1,0:T(8,128)S(1)}, u32[]{:S(2)}, u32[]{:S(2)}) collective-permute-start(f32[1,136,128]{2,1,0:T(8,128)S(1)} %maximum_bitcast_fusion), channel_id=1, source_target_pairs={{0,8},{1,9},{2,10},{3,11},{4,12},{5,13},{6,14},{7,15},{8,16},{9,17... | collective-permute-start | bytes 208904 | tf_op jit(solution)/shard_map/ppermute | solution.py:416
  5.8 7.3 %collective-permute-start.1 = (f32[1,136,128]{2,1,0:T(8,128)S(1)}, f32[1,136,128]{2,1,0:T(8,128)S(1)}, u32[]{:S(2)}, u32[]{:S(2)}) collective-permute-start(f32[1,136,128]{2,1,0:T(8,128)S(1)} %maximum_bitcast_fusion), channel_id=1, source_target_pairs={{0,16},{1,17},{2,18},{3,19},{4,20},{5,21},{6,22},{7,23},{8,24},{9,... | collective-permute-start | bytes 208904 | tf_op jit(solution)/shard_map/ppermute | solution.py:416
  8.4 4.9 %collective-permute-start.2 = (f32[1,136,128]{2,1,0:T(8,128)S(1)}, f32[1,136,128]{2,1,0:T(8,128)S(1)}, u32[]{:S(2)}, u32[]{:S(2)}) collective-permute-start(f32[1,136,128]{2,1,0:T(8,128)S(1)} %maximum_bitcast_fusion), channel_id=1, source_target_pairs={{0,24},{1,25},{2,26},{3,27},{4,28},{5,29},{6,30},{7,31},{8,0},{9,1... | collective-permute-start | bytes 208904 | tf_op jit(solution)/shard_map/ppermute | solution.py:416
  13.3 27.9 %copy-start.3 = (bf16[2,256,256]{2,1,0:T(8,128)(2,1)S(1)}, bf16[2,256,256]{2,1,0:T(8,128)(2,1)}, u32[]{:S(2)}) copy-start(bf16[2,256,256]{2,1,0:T(8,128)(2,1)} %constant.512.clone.odd_l) | copy-start | bytes 786436
  13.3 27.9 %copy-start.6 = (f32[32,128]{1,0:T(8,128)S(1)}, f32[32,128]{1,0:T(8,128)}, u32[]{:S(2)}) copy-start(f32[32,128]{1,0:T(8,128)} %constant.508.clone.small_ref) | copy-start | bytes 49156
  13.3 8.3 %collective-permute-start.4 = (f32[4,136,128]{2,1,0:T(8,128)S(1)}, f32[4,136,128]{2,1,0:T(8,128)S(1)}, u32[]{:S(2)}, u32[]{:S(2)}) collective-permute-start(f32[4,136,128]{2,1,0:T(8,128)S(1)} %pad_maximum_fusion.rest_0_), channel_id=1, source_target_pairs={{0,1},{1,0},{2,3},{3,2},{4,5},{5,4},{6,7},{7,6},{8,9},{9,8},{10,11... | collective-permute-start | bytes 835592 | tf_op jit(solution)/shard_map/ppermute | solution.py:416
  14.9 22.9 %collective-permute-start.3 = (f32[4,136,128]{2,1,0:T(8,128)S(1)}, f32[4,136,128]{2,1,0:T(8,128)S(1)}, u32[]{:S(2)}, u32[]{:S(2)}) collective-permute-start(f32[4,136,128]{2,1,0:T(8,128)S(1)} %pad_maximum_fusion.rest_0_), channel_id=1, source_target_pairs={{0,4},{1,5},{2,6},{3,7},{4,0},{5,1},{6,2},{7,3},{8,12},{9,13},{10,... | collective-permute-start | bytes 835592 | tf_op jit(solution)/shard_map/ppermute | solution.py:416
  21.6 17.9 %collective-permute-start.5 = (f32[4,136,128]{2,1,0:T(8,128)S(1)}, f32[4,136,128]{2,1,0:T(8,128)S(1)}, u32[]{:S(2)}, u32[]{:S(2)}) collective-permute-start(f32[4,136,128]{2,1,0:T(8,128)S(1)} %collective-permute-done.4.rest_1_), channel_id=1, source_target_pairs={{0,4},{1,5},{2,6},{3,7},{4,0},{5,1},{6,2},{7,3},{8,12},{9,13},{10,... | collective-permute-start | bytes 835592 | tf_op jit(solution)/shard_map/ppermute | solution.py:416
  22.9 18.3 %collective-permute-start.8 = (f32[4,136,128]{2,1,0:T(8,128)S(1)}, f32[4,136,128]{2,1,0:T(8,128)S(1)}, u32[]{:S(2)}, u32[]{:S(2)}) collective-permute-start(f32[4,136,128]{2,1,0:T(8,128)S(1)} %pad_maximum_fusion.rest_0_), channel_id=1, source_target_pairs={{0,2},{1,3},{2,0},{3,1},{4,6},{5,7},{6,4},{7,5},{8,10},{9,11},{10,... | collective-permute-start | bytes 835592 | tf_op jit(solution)/shard_map/ppermute | solution.py:416
  22.9 18.3 %collective-permute-start.9 = (f32[4,136,128]{2,1,0:T(8,128)S(1)}, f32[4,136,128]{2,1,0:T(8,128)S(1)}, u32[]{:S(2)}, u32[]{:S(2)}) collective-permute-start(f32[4,136,128]{2,1,0:T(8,128)S(1)} %collective-permute-done.4.rest_1_), channel_id=1, source_target_pairs={{0,2},{1,3},{2,0},{3,1},{4,6},{5,7},{6,4},{7,5},{8,10},{9,11},{10,... | collective-permute-start | bytes 835592 | tf_op jit(solution)/shard_map/ppermute | solution.py:416
  23.4 17.8 %copy-start.4 = (s32[3,16,128]{2,1,0:T(8,128)S(1)}, s32[3,16,128]{2,1,0:T(8,128)}, u32[]{:S(2)}) copy-start(s32[3,16,128]{2,1,0:T(8,128)} %constant.506.clone.fixed_ref) | copy-start | bytes 73732
  23.4 17.8 %copy-start.5 = (s32[3,16,128]{2,1,0:T(8,128)S(1)}, s32[3,16,128]{2,1,0:T(8,128)}, u32[]{:S(2)}) copy-start(s32[3,16,128]{2,1,0:T(8,128)} %constant.507.clone.ticks_ref) | copy-start | bytes 73732
  23.4 5.9 %collective-permute-start.10 = (f32[4,8,128]{2,1,0:T(8,128)S(1)}, f32[4,8,128]{2,1,0:T(8,128)S(1)}, u32[]{:S(2)}, u32[]{:S(2)}) collective-permute-start(f32[4,8,128]{2,1,0:T(8,128)S(1)} %slice.13), channel_id=1, source_target_pairs={{0,4},{1,5},{2,6},{3,7},{4,0},{5,1},{6,2},{7,3},{8,12},{9,13},{10,... | collective-permute-start | bytes 49160 | tf_op jit(solution)/shard_map/ppermute | solution.py:416
  29.3 4.6 %collective-permute-start.11 = (f32[4,8,128]{2,1,0:T(8,128)S(1)}, f32[4,8,128]{2,1,0:T(8,128)S(1)}, u32[]{:S(2)}, u32[]{:S(2)}) collective-permute-start(f32[4,8,128]{2,1,0:T(8,128)S(1)} %slice.13), channel_id=1, source_target_pairs={{0,5},{1,4},{2,7},{3,6},{4,1},{5,0},{6,3},{7,2},{8,13},{9,12},{10,... | collective-permute-start | bytes 49160 | tf_op jit(solution)/shard_map/ppermute | solution.py:416
  34.0 3.2 %collective-permute-start.12 = (f32[4,8,128]{2,1,0:T(8,128)S(1)}, f32[4,8,128]{2,1,0:T(8,128)S(1)}, u32[]{:S(2)}, u32[]{:S(2)}) collective-permute-start(f32[4,8,128]{2,1,0:T(8,128)S(1)} %slice.13), channel_id=1, source_target_pairs={{0,6},{1,7},{2,4},{3,5},{4,2},{5,3},{6,0},{7,1},{8,14},{9,15},{10,... | collective-permute-start | bytes 49160 | tf_op jit(solution)/shard_map/ppermute | solution.py:416
  34.0 7.3 %copy-start.2 = (bf16[2,256,256]{2,1,0:T(8,128)(2,1)S(1)}, bf16[2,256,256]{2,1,0:T(8,128)(2,1)}, u32[]{:S(2)}) copy-start(bf16[2,256,256]{2,1,0:T(8,128)(2,1)} %constant.511.clone.odd_h) | copy-start | bytes 786436
  37.1 4.1 %collective-permute-start.13 = (f32[4,8,128]{2,1,0:T(8,128)S(1)}, f32[4,8,128]{2,1,0:T(8,128)S(1)}, u32[]{:S(2)}, u32[]{:S(2)}) collective-permute-start(f32[4,8,128]{2,1,0:T(8,128)S(1)} %slice.13), channel_id=1, source_target_pairs={{0,7},{1,6},{2,5},{3,4},{4,3},{5,2},{6,1},{7,0},{8,15},{9,14},{10,... | collective-permute-start | bytes 49160 | tf_op jit(solution)/shard_map/ppermute | solution.py:416
  37.7 3.6 %copy-start.1 = (bf16[2,256,256]{2,1,0:T(8,128)(2,1)S(1)}, bf16[2,256,256]{2,1,0:T(8,128)(2,1)}, u32[]{:S(2)}) copy-start(bf16[2,256,256]{2,1,0:T(8,128)(2,1)} %constant.510.clone.even_l) | copy-start | bytes 786436
  37.7 3.6 %copy-start = (bf16[2,256,256]{2,1,0:T(8,128)(2,1)S(1)}, bf16[2,256,256]{2,1,0:T(8,128)(2,1)}, u32[]{:S(2)}) copy-start(bf16[2,256,256]{2,1,0:T(8,128)(2,1)} %constant.509.clone.even_h) | copy-start | bytes 786436
  37.9 11.3 %collective-permute-start.6 = (f32[4,136,128]{2,1,0:T(8,128)S(1)}, f32[4,136,128]{2,1,0:T(8,128)S(1)}, u32[]{:S(2)}, u32[]{:S(2)}) collective-permute-start(f32[4,136,128]{2,1,0:T(8,128)S(1)} %collective-permute-done.3.rest_0_), channel_id=1, source_target_pairs={{0,2},{1,3},{2,0},{3,1},{4,6},{5,7},{6,4},{7,5},{8,10},{9,11},{10,... | collective-permute-start | bytes 835592 | tf_op jit(solution)/shard_map/ppermute | solution.py:416
  39.5 9.6 %collective-permute-start.7 = (f32[4,136,128]{2,1,0:T(8,128)S(1)}, f32[4,136,128]{2,1,0:T(8,128)S(1)}, u32[]{:S(2)}, u32[]{:S(2)}) collective-permute-start(f32[4,136,128]{2,1,0:T(8,128)S(1)} %collective-permute-done.5.rest_1_), channel_id=1, source_target_pairs={{0,2},{1,3},{2,0},{3,1},{4,6},{5,7},{6,4},{7,5},{8,10},{9,11},{10,... | collective-permute-start | bytes 835592 | tf_op jit(solution)/shard_map/ppermute | solution.py:416
where the time goes:
time: 57.9 us; the launch traced here: 57.7 us
  waiting for transfers between devices  21.4 us (37%)
  starting transfers between devices  16.9 us (29%)
  Pallas kernels  16.4 us (28%)
  local copies, waits for them, and re-layouts  1.44 us (2%)
  between operations  1.44 us (2%)
    ppermute x14, waiting for transfers between devices, moved(): return lax.ppermute(array, axes, pairs)  21.4 us
    ppermute x14, starting transfers between devices, moved(): return lax.ppermute(array, axes, pairs)  16.9 us
    pallas_call x2, Pallas kernels, surfaces(): pl.pallas_call(kernel, in_specs=[pl.BlockSpec(memory_space=pltpu.SMEM)] +...  16.4 us
  transfers between devices with their start and end apart: 14, of which 8 were waited for; matrix products, arithmetic and copies ran while one was open for 0% of the time, Pallas kernels for 14%

commit v1 on v0

--- a/solution.py
+++ b/solution.py
@@ -395,9 +395,9 @@
     outer = slabs // 4
     hops = capture.shape[1] // HOP
     own = capture.reshape(2, hops, HOP).transpose(1, 0, 2).reshape(hops, 2 * HOP)
+    ticks = jnp.broadcast_to(dropped.astype(jnp.float32)[:, None], (PAD, LANES))
+    own = jnp.concatenate([own, ticks], axis=0)[None]
     lead = NCH // HOP - 1
-    ticks = jnp.broadcast_to(dropped.astype(jnp.float32)[:, None], (PAD - lead, LANES))
-    own = jnp.concatenate([own, ticks, own[hops - lead :]], axis=0)[None]
 
     def split_index(flat):
         return flat // (4 * groups), (flat // (2 * groups)) % 2, (flat // groups) % 2, flat % groups
@@ -415,16 +415,20 @@
             pairs.append((flat, target))
         return lax.ppermute(array, axes, pairs)
 
-    line = [own] + [moved(own, (step, 0, 0, 0)) for step in range(1, outer)]
+    line = [own]
+    for step in range(1, outer):
+        line.append(moved(own, (step, 0, 0, 0)))
     line = jnp.concatenate(line, axis=0)
-    tiles = line[:, hops:, :]
+    tiles = jnp.concatenate([line[:, hops : hops + PAD - lead], line[:, hops - lead : hops]], axis=1)
+    notes = []
+    for member in range(groups):
+        notes.append(moved(tiles, (0, 1, 0, member)))
+    notes += [moved(note, (0, 0, 1, 0)) for note in notes]
     note_steps = [(1, core, member) for core in range(2) for member in range(groups)]
-    notes = []
-    for by in note_steps:
-        notes.append(moved(tiles, (0,) + by))
     near = [line] + [moved(line, (0, 0, 0, member)) for member in range(1, groups)]
-    far = [moved(line, (0, 1, 0, 0))]
-    far += [moved(piece, (0, 1, 0, 0)) for piece in near[1:]]
+    far = []
+    for member in range(groups):
+        far.append(moved(line, (0, 1, 0, member)))
     near_steps = [(0, 0, member) for member in range(groups)]
     far_steps = [(1, 0, member) for member in range(groups)]
     cores = []

time: 57.9 us -> 56.5 us (0.976)
  starting transfers between devices: 16.9 us -> 14.4 us
  waiting for transfers between devices: 21.4 us -> 22.6 us
    ppermute x14, starting transfers between devices: 16.9 us -> 14.4 us  [moved(): return lax.ppermute(array, axes, pairs)]
    ppermute x14, waiting for transfers between devices: 21.4 us -> 22.6 us  [moved(): return lax.ppermute(array, axes, pairs)]
  transfers between devices with their start and end apart: 14 -> 14, of which waited for: 8 -> 7; matrix products, arithmetic and copies ran while one was open for 0% -> 0% of each run, Pallas kernels for 14% -> 14%
where the time goes in v1:
time: 56.5 us; the launch traced here: 56.3 us
  waiting for transfers between devices  22.6 us (40%)
  Pallas kernels  16.4 us (29%)
  starting transfers between devices  14.4 us (25%)
  between operations  1.44 us (3%)
  local copies, waits for them, and re-layouts  1.37 us (2%)
    ppermute x14, waiting for transfers between devices, moved(): return lax.ppermute(array, axes, pairs)  22.6 us
    pallas_call x2, Pallas kernels, surfaces(): pl.pallas_call(kernel, in_specs=[pl.BlockSpec(memory_space=pltpu.SMEM)] +...  16.4 us
    ppermute x14, starting transfers between devices, moved(): return lax.ppermute(array, axes, pairs)  14.4 us
  transfers between devices with their start and end apart: 14, of which 7 were waited for; matrix products, arithmetic and copies ran while one was open for 0% of the time, Pallas kernels for 14%

profile of v1, /device:TPU:0, one launch (start us, length us, event | category | flops | bytes accessed | tf_op | source)
XLA Modules:
  0.0 56.3 jit_solution(1047111237495420930)
XLA Ops:
  1.3 1.0 %reshape.11 = f32[2,128,64]{2,1,0:T(8,128)S(1)} reshape(f32[2,8192]{1,0:T(2,128)} %param.16) | data formatting | bytes 131072 | tf_op jit(solution)/shard_map/reshape | solution.py:397
  2.3 0.1 copy.19
  2.3 0.1 copy.20
  2.5 5.1 %collective-permute-start.2 = (f32[1,136,128]{2,1,0:T(8,128)S(1)}, f32[1,136,128]{2,1,0:T(8,128)S(1)}, u32[]{:S(2)}, u32[]{:S(2)}) collective-permute-start(f32[1,136,128]{2,1,0:T(8,128)S(1)} %pad_bitcast_fusion), channel_id=1, source_target_pairs={{0,24},{1,25},{2,26},{3,27},{4,28},{5,29},{6,30},{7,31},{8,0},{9,1... | collective-permute-start | bytes 208904 | tf_op jit(solution)/shard_map/ppermute | solution.py:416
  7.6 0.0 collective-permute-start.1
  7.6 1.0 %collective-permute-start = (f32[1,136,128]{2,1,0:T(8,128)S(1)}, f32[1,136,128]{2,1,0:T(8,128)S(1)}, u32[]{:S(2)}, u32[]{:S(2)}) collective-permute-start(f32[1,136,128]{2,1,0:T(8,128)S(1)} %pad_bitcast_fusion), channel_id=1, source_target_pairs={{0,8},{1,9},{2,10},{3,11},{4,12},{5,13},{6,14},{7,15},{8,16},{9,17... | collective-permute-start | bytes 208904 | tf_op jit(solution)/shard_map/ppermute | solution.py:416
  8.6 1.6 %collective-permute-done.2 = f32[1,136,128]{2,1,0:T(8,128)S(1)} collective-permute-done((f32[1,136,128]{2,1,0:T(8,128)S(1)}, f32[1,136,128]{2,1,0:T(8,128)S(1)}, u32[]{:S(2)}, u32[]{:S(2)}) %collective-permute-start.2) | collective-permute-done | bytes 69664 | tf_op jit(solution)/shard_map/ppermute | solution.py:416
  10.2 4.2 %collective-permute-done.1 = f32[1,136,128]{2,1,0:T(8,128)S(1)} collective-permute-done((f32[1,136,128]{2,1,0:T(8,128)S(1)}, f32[1,136,128]{2,1,0:T(8,128)S(1)}, u32[]{:S(2)}, u32[]{:S(2)}) %collective-permute-start.1) | collective-permute-done | bytes 69664 | tf_op jit(solution)/shard_map/ppermute | solution.py:416
  14.4 1.6 %collective-permute-start.7 = (f32[4,136,128]{2,1,0:T(8,128)S(1)}, f32[4,136,128]{2,1,0:T(8,128)S(1)}, u32[]{:S(2)}, u32[]{:S(2)}) collective-permute-start(f32[4,136,128]{2,1,0:T(8,128)S(1)} %pad_maximum_fusion.rest_0_), channel_id=1, source_target_pairs={{0,1},{1,0},{2,3},{3,2},{4,5},{5,4},{6,7},{7,6},{8,9},{9,8},{10,11... | collective-permute-start | bytes 835592 | tf_op jit(solution)/shard_map/ppermute | solution.py:416
  16.0 1.4 %collective-permute-start.4 = (f32[4,136,128]{2,1,0:T(8,128)S(1)}, f32[4,136,128]{2,1,0:T(8,128)S(1)}, u32[]{:S(2)}, u32[]{:S(2)}) collective-permute-start(f32[4,136,128]{2,1,0:T(8,128)S(1)} %pad_maximum_fusion.rest_0_), channel_id=1, source_target_pairs={{0,5},{1,4},{2,7},{3,6},{4,1},{5,0},{6,3},{7,2},{8,13},{9,12},{10,... | collective-permute-start | bytes 835592 | tf_op jit(solution)/shard_map/ppermute | solution.py:416
  17.4 0.5 collective-permute-start.3
  18.0 0.0 collective-permute-start.8
  18.0 11.0 %collective-permute-done.7.rest_1_ = f32[4,136,128]{2,1,0:T(8,128)S(1)} collective-permute-done((f32[4,136,128]{2,1,0:T(8,128)S(1)}, f32[4,136,128]{2,1,0:T(8,128)S(1)}, u32[]{:S(2)}, u32[]{:S(2)}) %collective-permute-start.7) | collective-permute-done | bytes 278560 | tf_op jit(solution)/shard_map/ppermute | solution.py:416
  28.9 0.0 collective-permute-start.9
  29.0 0.0 copy-start.6
  29.0 0.0 copy-start.4
  29.0 0.0 copy-start.5
  29.0 2.5 %collective-permute-start.11 = (f32[4,8,128]{2,1,0:T(8,128)S(1)}, f32[4,8,128]{2,1,0:T(8,128)S(1)}, u32[]{:S(2)}, u32[]{:S(2)}) collective-permute-start(f32[4,8,128]{2,1,0:T(8,128)S(1)} %pad_maximum_fusion.1), channel_id=1, source_target_pairs={{0,5},{1,4},{2,7},{3,6},{4,1},{5,0},{6,3},{7,2},{8,13},{9,12},{10,... | collective-permute-start | bytes 49160 | tf_op jit(solution)/shard_map/ppermute | solution.py:416
  31.5 2.2 %collective-permute-done.11.rest_5_ = f32[4,8,128]{2,1,0:T(8,128)S(1)} collective-permute-done((f32[4,8,128]{2,1,0:T(8,128)S(1)}, f32[4,8,128]{2,1,0:T(8,128)S(1)}, u32[]{:S(2)}, u32[]{:S(2)}) %collective-permute-start.11) | collective-permute-done | bytes 16416 | tf_op jit(solution)/shard_map/ppermute | solution.py:416
  33.7 1.5 %collective-permute-start.10 = (f32[4,8,128]{2,1,0:T(8,128)S(1)}, f32[4,8,128]{2,1,0:T(8,128)S(1)}, u32[]{:S(2)}, u32[]{:S(2)}) collective-permute-start(f32[4,8,128]{2,1,0:T(8,128)S(1)} %pad_maximum_fusion.1), channel_id=1, source_target_pairs={{0,4},{1,5},{2,6},{3,7},{4,0},{5,1},{6,2},{7,3},{8,12},{9,13},{10,... | collective-permute-start | bytes 49160 | tf_op jit(solution)/shard_map/ppermute | solution.py:416
  35.2 2.2 %collective-permute-done.10.rest_4_ = f32[4,8,128]{2,1,0:T(8,128)S(1)} collective-permute-done((f32[4,8,128]{2,1,0:T(8,128)S(1)}, f32[4,8,128]{2,1,0:T(8,128)S(1)}, u32[]{:S(2)}, u32[]{:S(2)}) %collective-permute-start.10) | collective-permute-done | bytes 16416 | tf_op jit(solution)/shard_map/ppermute | solution.py:416
  37.5 1.2 %collective-permute-done.13.rest_7_ = f32[4,8,128]{2,1,0:T(8,128)S(1)} collective-permute-done((f32[4,8,128]{2,1,0:T(8,128)S(1)}, f32[4,8,128]{2,1,0:T(8,128)S(1)}, u32[]{:S(2)}, u32[]{:S(2)}) %collective-permute-start.13) | collective-permute-done | bytes 16416 | tf_op jit(solution)/shard_map/ppermute | solution.py:416
  38.7 0.2 collective-permute-start.12
  38.8 0.2 stack.287.plan_ref
  39.0 0.0 collective-permute-done.4.rest_1_
  39.0 0.4 collective-permute-start.6
  39.4 0.2 collective-permute-start.5
  39.6 0.2 collective-permute-done.12.rest_6_
  39.8 0.0 collective-permute-done.8.rest_2_
  39.8 0.0 collective-permute-done.9.rest_3_
  39.9 7.9 %surfaces_first.1 = (f32[512,128]{1,0:T(8,128)S(1)}, f32[512,128]{1,0:T(8,128)S(1)}, f32[512,128]{1,0:T(8,128)S(1)}, f32[256,128]{1,0:T(8,128)S(1)}, f32[256,128]{1,0:T(8,128)S(1)}, /*index=5*/f32[4,8,128]{2,1,0:T(8,128)S(1)}) custom-call(s32[86]{0:T(128)S(1)} %stack.287.plan_ref, s32[3,16,128]{2,1,0:T(8,128)S(1)} %copy-done.5, s32[3,16,128]{2,1,0:T(8,128)S(1)} %copy-done.4, ...), custom_call_target="tpu_custom_call" | custom-call | flops 4831838208 | bytes 4194304 | tf_op jit(solution)/shard_map/surfaces_first/pallas_call | solution.py:367
  47.8 8.5 %surfaces_last.1 = (f32[8,64,128]{2,1,0:T(8,128)}, f32[2,8,64,128]{3,2,1,0:T(8,128)}) custom-call(s32[86]{0:T(128)S(1)} %stack.287.plan_ref, s32[3,16,128]{2,1,0:T(8,128)S(1)} %copy-done.5, s32[3,16,128]{2,1,0:T(8,128)S(1)} %copy-done.4, f32[32,128]{1,0:T(8,128)S(1)} %copy-done.6, bf16[2,256,256]{2,1,0:T(8,128)(2,1)S(1)} %copy-done.3, ...), custom_call_target="tpu_custom_call" | custom-call | flops 4831838208 | bytes 4194304 | tf_op jit(solution)/shard_map/surfaces_last/pallas_call | solution.py:367
  (21 shorter events, 0.1 us)
Async XLA Ops:
  2.5 7.7 %collective-permute-start.2 = (f32[1,136,128]{2,1,0:T(8,128)S(1)}, f32[1,136,128]{2,1,0:T(8,128)S(1)}, u32[]{:S(2)}, u32[]{:S(2)}) collective-permute-start(f32[1,136,128]{2,1,0:T(8,128)S(1)} %pad_bitcast_fusion), channel_id=1, source_target_pairs={{0,24},{1,25},{2,26},{3,27},{4,28},{5,29},{6,30},{7,31},{8,0},{9,1... | collective-permute-start | bytes 208904 | tf_op jit(solution)/shard_map/ppermute | solution.py:416
  7.6 6.8 %collective-permute-start.1 = (f32[1,136,128]{2,1,0:T(8,128)S(1)}, f32[1,136,128]{2,1,0:T(8,128)S(1)}, u32[]{:S(2)}, u32[]{:S(2)}) collective-permute-start(f32[1,136,128]{2,1,0:T(8,128)S(1)} %pad_bitcast_fusion), channel_id=1, source_target_pairs={{0,16},{1,17},{2,18},{3,19},{4,20},{5,21},{6,22},{7,23},{8,24},{9,... | collective-permute-start | bytes 208904 | tf_op jit(solution)/shard_map/ppermute | solution.py:416
  7.6 6.8 %collective-permute-start = (f32[1,136,128]{2,1,0:T(8,128)S(1)}, f32[1,136,128]{2,1,0:T(8,128)S(1)}, u32[]{:S(2)}, u32[]{:S(2)}) collective-permute-start(f32[1,136,128]{2,1,0:T(8,128)S(1)} %pad_bitcast_fusion), channel_id=1, source_target_pairs={{0,8},{1,9},{2,10},{3,11},{4,12},{5,13},{6,14},{7,15},{8,16},{9,17... | collective-permute-start | bytes 208904 | tf_op jit(solution)/shard_map/ppermute | solution.py:416
  14.4 25.5 %copy-start.3 = (bf16[2,256,256]{2,1,0:T(8,128)(2,1)S(1)}, bf16[2,256,256]{2,1,0:T(8,128)(2,1)}, u32[]{:S(2)}) copy-start(bf16[2,256,256]{2,1,0:T(8,128)(2,1)} %constant.509.clone.even_h) | copy-start | bytes 786436
  14.4 14.6 %collective-permute-start.7 = (f32[4,136,128]{2,1,0:T(8,128)S(1)}, f32[4,136,128]{2,1,0:T(8,128)S(1)}, u32[]{:S(2)}, u32[]{:S(2)}) collective-permute-start(f32[4,136,128]{2,1,0:T(8,128)S(1)} %pad_maximum_fusion.rest_0_), channel_id=1, source_target_pairs={{0,1},{1,0},{2,3},{3,2},{4,5},{5,4},{6,7},{7,6},{8,9},{9,8},{10,11... | collective-permute-start | bytes 835592 | tf_op jit(solution)/shard_map/ppermute | solution.py:416
  16.0 23.0 %collective-permute-start.4 = (f32[4,136,128]{2,1,0:T(8,128)S(1)}, f32[4,136,128]{2,1,0:T(8,128)S(1)}, u32[]{:S(2)}, u32[]{:S(2)}) collective-permute-start(f32[4,136,128]{2,1,0:T(8,128)S(1)} %pad_maximum_fusion.rest_0_), channel_id=1, source_target_pairs={{0,5},{1,4},{2,7},{3,6},{4,1},{5,0},{6,3},{7,2},{8,13},{9,12},{10,... | collective-permute-start | bytes 835592 | tf_op jit(solution)/shard_map/ppermute | solution.py:416
  17.4 22.0 %collective-permute-start.3 = (f32[4,136,128]{2,1,0:T(8,128)S(1)}, f32[4,136,128]{2,1,0:T(8,128)S(1)}, u32[]{:S(2)}, u32[]{:S(2)}) collective-permute-start(f32[4,136,128]{2,1,0:T(8,128)S(1)} %pad_maximum_fusion.rest_0_), channel_id=1, source_target_pairs={{0,4},{1,5},{2,6},{3,7},{4,0},{5,1},{6,2},{7,3},{8,12},{9,13},{10,... | collective-permute-start | bytes 835592 | tf_op jit(solution)/shard_map/ppermute | solution.py:416
  18.0 21.9 %collective-permute-start.8 = (f32[4,136,128]{2,1,0:T(8,128)S(1)}, f32[4,136,128]{2,1,0:T(8,128)S(1)}, u32[]{:S(2)}, u32[]{:S(2)}) collective-permute-start(f32[4,136,128]{2,1,0:T(8,128)S(1)} %pad_maximum_fusion.rest_0_), channel_id=1, source_target_pairs={{0,2},{1,3},{2,0},{3,1},{4,6},{5,7},{6,4},{7,5},{8,10},{9,11},{10,... | collective-permute-start | bytes 835592 | tf_op jit(solution)/shard_map/ppermute | solution.py:416
  28.9 10.9 %collective-permute-start.9 = (f32[4,136,128]{2,1,0:T(8,128)S(1)}, f32[4,136,128]{2,1,0:T(8,128)S(1)}, u32[]{:S(2)}, u32[]{:S(2)}) collective-permute-start(f32[4,136,128]{2,1,0:T(8,128)S(1)} %collective-permute-done.7.rest_1_), channel_id=1, source_target_pairs={{0,2},{1,3},{2,0},{3,1},{4,6},{5,7},{6,4},{7,5},{8,10},{9,11},{10,... | collective-permute-start | bytes 835592 | tf_op jit(solution)/shard_map/ppermute | solution.py:416
  29.0 10.9 %copy-start.6 = (f32[32,128]{1,0:T(8,128)S(1)}, f32[32,128]{1,0:T(8,128)}, u32[]{:S(2)}) copy-start(f32[32,128]{1,0:T(8,128)} %constant.508.clone.small_ref) | copy-start | bytes 49156
  29.0 10.9 %copy-start.4 = (s32[3,16,128]{2,1,0:T(8,128)S(1)}, s32[3,16,128]{2,1,0:T(8,128)}, u32[]{:S(2)}) copy-start(s32[3,16,128]{2,1,0:T(8,128)} %constant.507.clone.ticks_ref) | copy-start | bytes 73732
  29.0 10.9 %copy-start.5 = (s32[3,16,128]{2,1,0:T(8,128)S(1)}, s32[3,16,128]{2,1,0:T(8,128)}, u32[]{:S(2)}) copy-start(s32[3,16,128]{2,1,0:T(8,128)} %constant.506.clone.fixed_ref) | copy-start | bytes 73732
  29.0 4.7 %collective-permute-start.11 = (f32[4,8,128]{2,1,0:T(8,128)S(1)}, f32[4,8,128]{2,1,0:T(8,128)S(1)}, u32[]{:S(2)}, u32[]{:S(2)}) collective-permute-start(f32[4,8,128]{2,1,0:T(8,128)S(1)} %pad_maximum_fusion.1), channel_id=1, source_target_pairs={{0,5},{1,4},{2,7},{3,6},{4,1},{5,0},{6,3},{7,2},{8,13},{9,12},{10,... | collective-permute-start | bytes 49160 | tf_op jit(solution)/shard_map/ppermute | solution.py:416
  33.7 3.7 %collective-permute-start.10 = (f32[4,8,128]{2,1,0:T(8,128)S(1)}, f32[4,8,128]{2,1,0:T(8,128)S(1)}, u32[]{:S(2)}, u32[]{:S(2)}) collective-permute-start(f32[4,8,128]{2,1,0:T(8,128)S(1)} %pad_maximum_fusion.1), channel_id=1, source_target_pairs={{0,4},{1,5},{2,6},{3,7},{4,0},{5,1},{6,2},{7,3},{8,12},{9,13},{10,... | collective-permute-start | bytes 49160 | tf_op jit(solution)/shard_map/ppermute | solution.py:416
  37.5 1.2 %collective-permute-start.13 = (f32[4,8,128]{2,1,0:T(8,128)S(1)}, f32[4,8,128]{2,1,0:T(8,128)S(1)}, u32[]{:S(2)}, u32[]{:S(2)}) collective-permute-start(f32[4,8,128]{2,1,0:T(8,128)S(1)} %collective-permute-done.11.rest_5_), channel_id=1, source_target_pairs={{0,2},{1,3},{2,0},{3,1},{4,6},{5,7},{6,4},{7,5},{8,10},{9,11},{10,... | collective-permute-start | bytes 49160 | tf_op jit(solution)/shard_map/ppermute | solution.py:416
  37.5 2.4 %copy-start.2 = (bf16[2,256,256]{2,1,0:T(8,128)(2,1)S(1)}, bf16[2,256,256]{2,1,0:T(8,128)(2,1)}, u32[]{:S(2)}) copy-start(bf16[2,256,256]{2,1,0:T(8,128)(2,1)} %constant.510.clone.even_l) | copy-start | bytes 786436
  38.7 1.2 %collective-permute-start.12 = (f32[4,8,128]{2,1,0:T(8,128)S(1)}, f32[4,8,128]{2,1,0:T(8,128)S(1)}, u32[]{:S(2)}, u32[]{:S(2)}) collective-permute-start(f32[4,8,128]{2,1,0:T(8,128)S(1)} %collective-permute-done.10.rest_4_), channel_id=1, source_target_pairs={{0,2},{1,3},{2,0},{3,1},{4,6},{5,7},{6,4},{7,5},{8,10},{9,11},{10,... | collective-permute-start | bytes 49160 | tf_op jit(solution)/shard_map/ppermute | solution.py:416
  38.8 1.1 %copy-start.1 = (bf16[2,256,256]{2,1,0:T(8,128)(2,1)S(1)}, bf16[2,256,256]{2,1,0:T(8,128)(2,1)}, u32[]{:S(2)}) copy-start(bf16[2,256,256]{2,1,0:T(8,128)(2,1)} %constant.511.clone.odd_h) | copy-start | bytes 786436
  38.8 1.1 %copy-start = (bf16[2,256,256]{2,1,0:T(8,128)(2,1)S(1)}, bf16[2,256,256]{2,1,0:T(8,128)(2,1)}, u32[]{:S(2)}) copy-start(bf16[2,256,256]{2,1,0:T(8,128)(2,1)} %constant.512.clone.odd_l) | copy-start | bytes 786436
  39.0 8.8 %collective-permute-start.6 = (f32[4,136,128]{2,1,0:T(8,128)S(1)}, f32[4,136,128]{2,1,0:T(8,128)S(1)}, u32[]{:S(2)}, u32[]{:S(2)}) collective-permute-start(f32[4,136,128]{2,1,0:T(8,128)S(1)} %collective-permute-done.4.rest_1_), channel_id=1, source_target_pairs={{0,2},{1,3},{2,0},{3,1},{4,6},{5,7},{6,4},{7,5},{8,10},{9,11},{10,... | collective-permute-start | bytes 835592 | tf_op jit(solution)/shard_map/ppermute | solution.py:416
  39.4 8.4 %collective-permute-start.5 = (f32[4,136,128]{2,1,0:T(8,128)S(1)}, f32[4,136,128]{2,1,0:T(8,128)S(1)}, u32[]{:S(2)}, u32[]{:S(2)}) collective-permute-start(f32[4,136,128]{2,1,0:T(8,128)S(1)} %collective-permute-done.3.rest_0_), channel_id=1, source_target_pairs={{0,2},{1,3},{2,0},{3,1},{4,6},{5,7},{6,4},{7,5},{8,10},{9,11},{10,... | collective-permute-start | bytes 835592 | tf_op jit(solution)/shard_map/ppermute | solution.py:416

commit v2 on v0

--- a/solution.py
+++ b/solution.py
@@ -395,9 +395,9 @@
     outer = slabs // 4
     hops = capture.shape[1] // HOP
     own = capture.reshape(2, hops, HOP).transpose(1, 0, 2).reshape(hops, 2 * HOP)
+    ticks = jnp.broadcast_to(dropped.astype(jnp.float32)[:, None], (PAD, LANES))
+    own = jnp.concatenate([own, ticks], axis=0)[None]
     lead = NCH // HOP - 1
-    ticks = jnp.broadcast_to(dropped.astype(jnp.float32)[:, None], (PAD - lead, LANES))
-    own = jnp.concatenate([own, ticks, own[hops - lead :]], axis=0)[None]
 
     def split_index(flat):
         return flat // (4 * groups), (flat // (2 * groups)) % 2, (flat // groups) % 2, flat % groups
@@ -415,9 +415,11 @@
             pairs.append((flat, target))
         return lax.ppermute(array, axes, pairs)
 
-    line = [own] + [moved(own, (step, 0, 0, 0)) for step in range(1, outer)]
+    line = [own]
+    for step in range(1, outer):
+        line.append(moved(own, (step, 0, 0, 0)))
     line = jnp.concatenate(line, axis=0)
-    tiles = line[:, hops:, :]
+    tiles = jnp.concatenate([line[:, hops : hops + PAD - lead], line[:, hops - lead : hops]], axis=1)
     note_steps = [(1, core, member) for core in range(2) for member in range(groups)]
     notes = []
     for by in note_steps:

time: 57.9 us -> 57.7 us (level)
  no operation moved by 1% of the time
where the time goes in v2:
time: 57.7 us; the launch traced here: 57.5 us
  waiting for transfers between devices  21.3 us (37%)
  starting transfers between devices  17 us (29%)
  Pallas kernels  16.4 us (28%)
  between operations  1.44 us (2%)
  local copies, waits for them, and re-layouts  1.36 us (2%)
    ppermute x14, waiting for transfers between devices, moved(): return lax.ppermute(array, axes, pairs)  21.3 us
    ppermute x14, starting transfers between devices, moved(): return lax.ppermute(array, axes, pairs)  17 us
    pallas_call x2, Pallas kernels, surfaces(): pl.pallas_call(kernel, in_specs=[pl.BlockSpec(memory_space=pltpu.SMEM)] +...  16.4 us
  transfers between devices with their start and end apart: 14, of which 8 were waited for; matrix products, arithmetic and copies ran while one was open for 0% of the time, Pallas kernels for 14%

profile of v2, /device:TPU:0, one launch (start us, length us, event | category | flops | bytes accessed | tf_op | source)
XLA Modules:
  0.0 57.5 jit_solution(7485426258939689724)
XLA Ops:
  0.6 1.0 %reshape.11 = f32[2,128,64]{2,1,0:T(8,128)S(1)} reshape(f32[2,8192]{1,0:T(2,128)} %param.16) | data formatting | bytes 131072 | tf_op jit(solution)/shard_map/reshape | solution.py:397
  1.6 0.1 copy.19
  1.7 0.1 copy.20
  2.5 3.1 %collective-permute-start = (f32[1,136,128]{2,1,0:T(8,128)S(1)}, f32[1,136,128]{2,1,0:T(8,128)S(1)}, u32[]{:S(2)}, u32[]{:S(2)}) collective-permute-start(f32[1,136,128]{2,1,0:T(8,128)S(1)} %pad_bitcast_fusion), channel_id=1, source_target_pairs={{0,8},{1,9},{2,10},{3,11},{4,12},{5,13},{6,14},{7,15},{8,16},{9,17... | collective-permute-start | bytes 208904 | tf_op jit(solution)/shard_map/ppermute | solution.py:416
  5.6 2.6 %collective-permute-start.1 = (f32[1,136,128]{2,1,0:T(8,128)S(1)}, f32[1,136,128]{2,1,0:T(8,128)S(1)}, u32[]{:S(2)}, u32[]{:S(2)}) collective-permute-start(f32[1,136,128]{2,1,0:T(8,128)S(1)} %pad_bitcast_fusion), channel_id=1, source_target_pairs={{0,16},{1,17},{2,18},{3,19},{4,20},{5,21},{6,22},{7,23},{8,24},{9,... | collective-permute-start | bytes 208904 | tf_op jit(solution)/shard_map/ppermute | solution.py:416
  8.2 1.3 %collective-permute-start.2 = (f32[1,136,128]{2,1,0:T(8,128)S(1)}, f32[1,136,128]{2,1,0:T(8,128)S(1)}, u32[]{:S(2)}, u32[]{:S(2)}) collective-permute-start(f32[1,136,128]{2,1,0:T(8,128)S(1)} %pad_bitcast_fusion), channel_id=1, source_target_pairs={{0,24},{1,25},{2,26},{3,27},{4,28},{5,29},{6,30},{7,31},{8,0},{9,1... | collective-permute-start | bytes 208904 | tf_op jit(solution)/shard_map/ppermute | solution.py:416
  9.5 0.6 %collective-permute-done = f32[1,136,128]{2,1,0:T(8,128)S(1)} collective-permute-done((f32[1,136,128]{2,1,0:T(8,128)S(1)}, f32[1,136,128]{2,1,0:T(8,128)S(1)}, u32[]{:S(2)}, u32[]{:S(2)}) %collective-permute-start) | collective-permute-done | bytes 69664 | tf_op jit(solution)/shard_map/ppermute | solution.py:416
  10.1 2.7 %collective-permute-done.1 = f32[1,136,128]{2,1,0:T(8,128)S(1)} collective-permute-done((f32[1,136,128]{2,1,0:T(8,128)S(1)}, f32[1,136,128]{2,1,0:T(8,128)S(1)}, u32[]{:S(2)}, u32[]{:S(2)}) %collective-permute-start.1) | collective-permute-done | bytes 69664 | tf_op jit(solution)/shard_map/ppermute | solution.py:416
  12.9 0.2 collective-permute-done.2
  13.1 1.6 %collective-permute-start.4 = (f32[4,136,128]{2,1,0:T(8,128)S(1)}, f32[4,136,128]{2,1,0:T(8,128)S(1)}, u32[]{:S(2)}, u32[]{:S(2)}) collective-permute-start(f32[4,136,128]{2,1,0:T(8,128)S(1)} %pad_maximum_fusion.rest_0_), channel_id=1, source_target_pairs={{0,1},{1,0},{2,3},{3,2},{4,5},{5,4},{6,7},{7,6},{8,9},{9,8},{10,11... | collective-permute-start | bytes 835592 | tf_op jit(solution)/shard_map/ppermute | solution.py:416
  14.7 1.5 %collective-permute-start.3 = (f32[4,136,128]{2,1,0:T(8,128)S(1)}, f32[4,136,128]{2,1,0:T(8,128)S(1)}, u32[]{:S(2)}, u32[]{:S(2)}) collective-permute-start(f32[4,136,128]{2,1,0:T(8,128)S(1)} %pad_maximum_fusion.rest_0_), channel_id=1, source_target_pairs={{0,4},{1,5},{2,6},{3,7},{4,0},{5,1},{6,2},{7,3},{8,12},{9,13},{10,... | collective-permute-start | bytes 835592 | tf_op jit(solution)/shard_map/ppermute | solution.py:416
  16.2 5.2 %collective-permute-done.4.rest_1_ = f32[4,136,128]{2,1,0:T(8,128)S(1)} collective-permute-done((f32[4,136,128]{2,1,0:T(8,128)S(1)}, f32[4,136,128]{2,1,0:T(8,128)S(1)}, u32[]{:S(2)}, u32[]{:S(2)}) %collective-permute-start.4) | collective-permute-done | bytes 278560 | tf_op jit(solution)/shard_map/ppermute | solution.py:416
  21.4 1.3 %collective-permute-start.5 = (f32[4,136,128]{2,1,0:T(8,128)S(1)}, f32[4,136,128]{2,1,0:T(8,128)S(1)}, u32[]{:S(2)}, u32[]{:S(2)}) collective-permute-start(f32[4,136,128]{2,1,0:T(8,128)S(1)} %collective-permute-done.4.rest_1_), channel_id=1, source_target_pairs={{0,4},{1,5},{2,6},{3,7},{4,0},{5,1},{6,2},{7,3},{8,12},{9,13},{10,... | collective-permute-start | bytes 835592 | tf_op jit(solution)/shard_map/ppermute | solution.py:416
  22.7 0.0 collective-permute-start.8
  22.7 0.5 collective-permute-start.9
  23.2 0.0 copy-start.4
  23.2 0.0 copy-start.5
  23.3 0.8 %collective-permute-start.10 = (f32[4,8,128]{2,1,0:T(8,128)S(1)}, f32[4,8,128]{2,1,0:T(8,128)S(1)}, u32[]{:S(2)}, u32[]{:S(2)}) collective-permute-start(f32[4,8,128]{2,1,0:T(8,128)S(1)} %pad_maximum_fusion.1), channel_id=1, source_target_pairs={{0,4},{1,5},{2,6},{3,7},{4,0},{5,1},{6,2},{7,3},{8,12},{9,13},{10,... | collective-permute-start | bytes 49160 | tf_op jit(solution)/shard_map/ppermute | solution.py:416
  24.1 5.1 %collective-permute-done.10.rest_4_ = f32[4,8,128]{2,1,0:T(8,128)S(1)} collective-permute-done((f32[4,8,128]{2,1,0:T(8,128)S(1)}, f32[4,8,128]{2,1,0:T(8,128)S(1)}, u32[]{:S(2)}, u32[]{:S(2)}) %collective-permute-start.10) | collective-permute-done | bytes 16416 | tf_op jit(solution)/shard_map/ppermute | solution.py:416
  29.1 2.0 %collective-permute-start.11 = (f32[4,8,128]{2,1,0:T(8,128)S(1)}, f32[4,8,128]{2,1,0:T(8,128)S(1)}, u32[]{:S(2)}, u32[]{:S(2)}) collective-permute-start(f32[4,8,128]{2,1,0:T(8,128)S(1)} %pad_maximum_fusion.1), channel_id=1, source_target_pairs={{0,5},{1,4},{2,7},{3,6},{4,1},{5,0},{6,3},{7,2},{8,13},{9,12},{10,... | collective-permute-start | bytes 49160 | tf_op jit(solution)/shard_map/ppermute | solution.py:416
  31.2 2.6 %collective-permute-done.11.rest_5_ = f32[4,8,128]{2,1,0:T(8,128)S(1)} collective-permute-done((f32[4,8,128]{2,1,0:T(8,128)S(1)}, f32[4,8,128]{2,1,0:T(8,128)S(1)}, u32[]{:S(2)}, u32[]{:S(2)}) %collective-permute-start.11) | collective-permute-done | bytes 16416 | tf_op jit(solution)/shard_map/ppermute | solution.py:416
  33.8 3.2 %collective-permute-done.12.rest_6_ = f32[4,8,128]{2,1,0:T(8,128)S(1)} collective-permute-done((f32[4,8,128]{2,1,0:T(8,128)S(1)}, f32[4,8,128]{2,1,0:T(8,128)S(1)}, u32[]{:S(2)}, u32[]{:S(2)}) %collective-permute-start.12) | collective-permute-done | bytes 16416 | tf_op jit(solution)/shard_map/ppermute | solution.py:416
  36.9 0.5 collective-permute-start.13
  37.5 0.2 stack.287.plan_ref
  37.7 0.0 collective-permute-done.3.rest_0_
  37.7 1.7 %collective-permute-start.6 = (f32[4,136,128]{2,1,0:T(8,128)S(1)}, f32[4,136,128]{2,1,0:T(8,128)S(1)}, u32[]{:S(2)}, u32[]{:S(2)}) collective-permute-start(f32[4,136,128]{2,1,0:T(8,128)S(1)} %collective-permute-done.3.rest_0_), channel_id=1, source_target_pairs={{0,2},{1,3},{2,0},{3,1},{4,6},{5,7},{6,4},{7,5},{8,10},{9,11},{10,... | collective-permute-start | bytes 835592 | tf_op jit(solution)/shard_map/ppermute | solution.py:416
  39.3 0.0 collective-permute-done.5.rest_1_
  39.3 0.1 collective-permute-start.7
  39.4 1.6 %collective-permute-done.13.rest_7_ = f32[4,8,128]{2,1,0:T(8,128)S(1)} collective-permute-done((f32[4,8,128]{2,1,0:T(8,128)S(1)}, f32[4,8,128]{2,1,0:T(8,128)S(1)}, u32[]{:S(2)}, u32[]{:S(2)}) %collective-permute-start.13) | collective-permute-done | bytes 16416 | tf_op jit(solution)/shard_map/ppermute | solution.py:416
  41.1 7.9 %surfaces_first.1 = (f32[512,128]{1,0:T(8,128)S(1)}, f32[512,128]{1,0:T(8,128)S(1)}, f32[512,128]{1,0:T(8,128)S(1)}, f32[256,128]{1,0:T(8,128)S(1)}, f32[256,128]{1,0:T(8,128)S(1)}, /*index=5*/f32[4,8,128]{2,1,0:T(8,128)S(1)}) custom-call(s32[86]{0:T(128)S(1)} %stack.287.plan_ref, s32[3,16,128]{2,1,0:T(8,128)S(1)} %copy-done.4, s32[3,16,128]{2,1,0:T(8,128)S(1)} %copy-done.5, ...), custom_call_target="tpu_custom_call" | custom-call | flops 4831838208 | bytes 4194304 | tf_op jit(solution)/shard_map/surfaces_first/pallas_call | solution.py:367
  49.0 0.0 collective-permute-done.7.rest_3_
  49.0 8.5 %surfaces_last.1 = (f32[8,64,128]{2,1,0:T(8,128)}, f32[2,8,64,128]{3,2,1,0:T(8,128)}) custom-call(s32[86]{0:T(128)S(1)} %stack.287.plan_ref, s32[3,16,128]{2,1,0:T(8,128)S(1)} %copy-done.4, s32[3,16,128]{2,1,0:T(8,128)S(1)} %copy-done.5, f32[32,128]{1,0:T(8,128)S(1)} %copy-done.6, bf16[2,256,256]{2,1,0:T(8,128)(2,1)S(1)} %copy-done, ...), custom_call_target="tpu_custom_call" | custom-call | flops 4831838208 | bytes 4194304 | tf_op jit(solution)/shard_map/surfaces_last/pallas_call | solution.py:367
  (21 shorter events, 0.1 us)
Async XLA Ops:
  2.5 7.7 %collective-permute-start = (f32[1,136,128]{2,1,0:T(8,128)S(1)}, f32[1,136,128]{2,1,0:T(8,128)S(1)}, u32[]{:S(2)}, u32[]{:S(2)}) collective-permute-start(f32[1,136,128]{2,1,0:T(8,128)S(1)} %pad_bitcast_fusion), channel_id=1, source_target_pairs={{0,8},{1,9},{2,10},{3,11},{4,12},{5,13},{6,14},{7,15},{8,16},{9,17... | collective-permute-start | bytes 208904 | tf_op jit(solution)/shard_map/ppermute | solution.py:416
  5.6 7.3 %collective-permute-start.1 = (f32[1,136,128]{2,1,0:T(8,128)S(1)}, f32[1,136,128]{2,1,0:T(8,128)S(1)}, u32[]{:S(2)}, u32[]{:S(2)}) collective-permute-start(f32[1,136,128]{2,1,0:T(8,128)S(1)} %pad_bitcast_fusion), channel_id=1, source_target_pairs={{0,16},{1,17},{2,18},{3,19},{4,20},{5,21},{6,22},{7,23},{8,24},{9,... | collective-permute-start | bytes 208904 | tf_op jit(solution)/shard_map/ppermute | solution.py:416
  8.2 4.9 %collective-permute-start.2 = (f32[1,136,128]{2,1,0:T(8,128)S(1)}, f32[1,136,128]{2,1,0:T(8,128)S(1)}, u32[]{:S(2)}, u32[]{:S(2)}) collective-permute-start(f32[1,136,128]{2,1,0:T(8,128)S(1)} %pad_bitcast_fusion), channel_id=1, source_target_pairs={{0,24},{1,25},{2,26},{3,27},{4,28},{5,29},{6,30},{7,31},{8,0},{9,1... | collective-permute-start | bytes 208904 | tf_op jit(solution)/shard_map/ppermute | solution.py:416
  13.1 27.9 %copy-start.3 = (bf16[2,256,256]{2,1,0:T(8,128)(2,1)S(1)}, bf16[2,256,256]{2,1,0:T(8,128)(2,1)}, u32[]{:S(2)}) copy-start(bf16[2,256,256]{2,1,0:T(8,128)(2,1)} %constant.512.clone.odd_l) | copy-start | bytes 786436
  13.1 8.3 %collective-permute-start.4 = (f32[4,136,128]{2,1,0:T(8,128)S(1)}, f32[4,136,128]{2,1,0:T(8,128)S(1)}, u32[]{:S(2)}, u32[]{:S(2)}) collective-permute-start(f32[4,136,128]{2,1,0:T(8,128)S(1)} %pad_maximum_fusion.rest_0_), channel_id=1, source_target_pairs={{0,1},{1,0},{2,3},{3,2},{4,5},{5,4},{6,7},{7,6},{8,9},{9,8},{10,11... | collective-permute-start | bytes 835592 | tf_op jit(solution)/shard_map/ppermute | solution.py:416
  14.7 22.9 %collective-permute-start.3 = (f32[4,136,128]{2,1,0:T(8,128)S(1)}, f32[4,136,128]{2,1,0:T(8,128)S(1)}, u32[]{:S(2)}, u32[]{:S(2)}) collective-permute-start(f32[4,136,128]{2,1,0:T(8,128)S(1)} %pad_maximum_fusion.rest_0_), channel_id=1, source_target_pairs={{0,4},{1,5},{2,6},{3,7},{4,0},{5,1},{6,2},{7,3},{8,12},{9,13},{10,... | collective-permute-start | bytes 835592 | tf_op jit(solution)/shard_map/ppermute | solution.py:416
  21.4 17.9 %collective-permute-start.5 = (f32[4,136,128]{2,1,0:T(8,128)S(1)}, f32[4,136,128]{2,1,0:T(8,128)S(1)}, u32[]{:S(2)}, u32[]{:S(2)}) collective-permute-start(f32[4,136,128]{2,1,0:T(8,128)S(1)} %collective-permute-done.4.rest_1_), channel_id=1, source_target_pairs={{0,4},{1,5},{2,6},{3,7},{4,0},{5,1},{6,2},{7,3},{8,12},{9,13},{10,... | collective-permute-start | bytes 835592 | tf_op jit(solution)/shard_map/ppermute | solution.py:416
  22.7 18.3 %collective-permute-start.8 = (f32[4,136,128]{2,1,0:T(8,128)S(1)}, f32[4,136,128]{2,1,0:T(8,128)S(1)}, u32[]{:S(2)}, u32[]{:S(2)}) collective-permute-start(f32[4,136,128]{2,1,0:T(8,128)S(1)} %pad_maximum_fusion.rest_0_), channel_id=1, source_target_pairs={{0,2},{1,3},{2,0},{3,1},{4,6},{5,7},{6,4},{7,5},{8,10},{9,11},{10,... | collective-permute-start | bytes 835592 | tf_op jit(solution)/shard_map/ppermute | solution.py:416
  22.7 18.3 %collective-permute-start.9 = (f32[4,136,128]{2,1,0:T(8,128)S(1)}, f32[4,136,128]{2,1,0:T(8,128)S(1)}, u32[]{:S(2)}, u32[]{:S(2)}) collective-permute-start(f32[4,136,128]{2,1,0:T(8,128)S(1)} %collective-permute-done.4.rest_1_), channel_id=1, source_target_pairs={{0,2},{1,3},{2,0},{3,1},{4,6},{5,7},{6,4},{7,5},{8,10},{9,11},{10,... | collective-permute-start | bytes 835592 | tf_op jit(solution)/shard_map/ppermute | solution.py:416
  23.2 17.8 %copy-start.6 = (f32[32,128]{1,0:T(8,128)S(1)}, f32[32,128]{1,0:T(8,128)}, u32[]{:S(2)}) copy-start(f32[32,128]{1,0:T(8,128)} %constant.508.clone.small_ref) | copy-start | bytes 49156
  23.2 17.8 %copy-start.4 = (s32[3,16,128]{2,1,0:T(8,128)S(1)}, s32[3,16,128]{2,1,0:T(8,128)}, u32[]{:S(2)}) copy-start(s32[3,16,128]{2,1,0:T(8,128)} %constant.506.clone.fixed_ref) | copy-start | bytes 73732
  23.2 17.8 %copy-start.5 = (s32[3,16,128]{2,1,0:T(8,128)S(1)}, s32[3,16,128]{2,1,0:T(8,128)}, u32[]{:S(2)}) copy-start(s32[3,16,128]{2,1,0:T(8,128)} %constant.507.clone.ticks_ref) | copy-start | bytes 73732
  23.3 5.9 %collective-permute-start.10 = (f32[4,8,128]{2,1,0:T(8,128)S(1)}, f32[4,8,128]{2,1,0:T(8,128)S(1)}, u32[]{:S(2)}, u32[]{:S(2)}) collective-permute-start(f32[4,8,128]{2,1,0:T(8,128)S(1)} %pad_maximum_fusion.1), channel_id=1, source_target_pairs={{0,4},{1,5},{2,6},{3,7},{4,0},{5,1},{6,2},{7,3},{8,12},{9,13},{10,... | collective-permute-start | bytes 49160 | tf_op jit(solution)/shard_map/ppermute | solution.py:416
  29.1 4.6 %collective-permute-start.11 = (f32[4,8,128]{2,1,0:T(8,128)S(1)}, f32[4,8,128]{2,1,0:T(8,128)S(1)}, u32[]{:S(2)}, u32[]{:S(2)}) collective-permute-start(f32[4,8,128]{2,1,0:T(8,128)S(1)} %pad_maximum_fusion.1), channel_id=1, source_target_pairs={{0,5},{1,4},{2,7},{3,6},{4,1},{5,0},{6,3},{7,2},{8,13},{9,12},{10,... | collective-permute-start | bytes 49160 | tf_op jit(solution)/shard_map/ppermute | solution.py:416
  33.8 3.2 %collective-permute-start.12 = (f32[4,8,128]{2,1,0:T(8,128)S(1)}, f32[4,8,128]{2,1,0:T(8,128)S(1)}, u32[]{:S(2)}, u32[]{:S(2)}) collective-permute-start(f32[4,8,128]{2,1,0:T(8,128)S(1)} %pad_maximum_fusion.1), channel_id=1, source_target_pairs={{0,6},{1,7},{2,4},{3,5},{4,2},{5,3},{6,0},{7,1},{8,14},{9,15},{10,... | collective-permute-start | bytes 49160 | tf_op jit(solution)/shard_map/ppermute | solution.py:416
  33.8 7.3 %copy-start.2 = (bf16[2,256,256]{2,1,0:T(8,128)(2,1)S(1)}, bf16[2,256,256]{2,1,0:T(8,128)(2,1)}, u32[]{:S(2)}) copy-start(bf16[2,256,256]{2,1,0:T(8,128)(2,1)} %constant.511.clone.odd_h) | copy-start | bytes 786436
  36.9 4.1 %collective-permute-start.13 = (f32[4,8,128]{2,1,0:T(8,128)S(1)}, f32[4,8,128]{2,1,0:T(8,128)S(1)}, u32[]{:S(2)}, u32[]{:S(2)}) collective-permute-start(f32[4,8,128]{2,1,0:T(8,128)S(1)} %pad_maximum_fusion.1), channel_id=1, source_target_pairs={{0,7},{1,6},{2,5},{3,4},{4,3},{5,2},{6,1},{7,0},{8,15},{9,14},{10,... | collective-permute-start | bytes 49160 | tf_op jit(solution)/shard_map/ppermute | solution.py:416
  37.5 3.6 %copy-start.1 = (bf16[2,256,256]{2,1,0:T(8,128)(2,1)S(1)}, bf16[2,256,256]{2,1,0:T(8,128)(2,1)}, u32[]{:S(2)}) copy-start(bf16[2,256,256]{2,1,0:T(8,128)(2,1)} %constant.510.clone.even_l) | copy-start | bytes 786436
  37.5 3.6 %copy-start = (bf16[2,256,256]{2,1,0:T(8,128)(2,1)S(1)}, bf16[2,256,256]{2,1,0:T(8,128)(2,1)}, u32[]{:S(2)}) copy-start(bf16[2,256,256]{2,1,0:T(8,128)(2,1)} %constant.509.clone.even_h) | copy-start | bytes 786436
  37.7 11.3 %collective-permute-start.6 = (f32[4,136,128]{2,1,0:T(8,128)S(1)}, f32[4,136,128]{2,1,0:T(8,128)S(1)}, u32[]{:S(2)}, u32[]{:S(2)}) collective-permute-start(f32[4,136,128]{2,1,0:T(8,128)S(1)} %collective-permute-done.3.rest_0_), channel_id=1, source_target_pairs={{0,2},{1,3},{2,0},{3,1},{4,6},{5,7},{6,4},{7,5},{8,10},{9,11},{10,... | collective-permute-start | bytes 835592 | tf_op jit(solution)/shard_map/ppermute | solution.py:416
  39.3 9.6 %collective-permute-start.7 = (f32[4,136,128]{2,1,0:T(8,128)S(1)}, f32[4,136,128]{2,1,0:T(8,128)S(1)}, u32[]{:S(2)}, u32[]{:S(2)}) collective-permute-start(f32[4,136,128]{2,1,0:T(8,128)S(1)} %collective-permute-done.5.rest_1_), channel_id=1, source_target_pairs={{0,2},{1,3},{2,0},{3,1},{4,6},{5,7},{6,4},{7,5},{8,10},{9,11},{10,... | collective-permute-start | bytes 835592 | tf_op jit(solution)/shard_map/ppermute | solution.py:416

commit v3 on v2

--- a/solution.py
+++ b/solution.py
@@ -158,8 +158,8 @@
     norm = 1.0 / math.sqrt(Q)
     blend = 1.0 / math.sqrt(slabs * BLOCKS)
     opening = carried is None
-    inputs = arrays + len(notes) + (0 if opening else 6)
-    outputs = 6 if opening else 2
+    inputs = arrays + len(notes) + (0 if opening else 5)
+    outputs = 5 if opening else 2
 
     def kernel(plan_ref, fixed_ref, ticks_ref, small_ref, even_h, even_l, odd_h, odd_l, *rest):
         piece_refs = rest[:arrays]
@@ -167,16 +167,18 @@
         out_refs = rest[inputs : inputs + outputs]
         rest = rest[inputs + outputs :] if opening else rest[arrays:]
         if opening:
-            acc_re, acc_im, acc_sq, cos_ref, sin_ref, tails = out_refs
+            acc_re, acc_im, acc_sq, stamps, tails = out_refs
             frames, drops = rest[:2]
             scratch = rest[2:]
         else:
-            old_re, old_im, old_sq, cos_ref, sin_ref, tails = rest[:6]
+            old_re, old_im, old_sq, stamps, tails = rest[:5]
             held_ref, coherent_ref = out_refs
-            frames, acc_re, acc_im, acc_sq = rest[8:12]
-            scratch = rest[12:]
+            frames, acc_re, acc_im, acc_sq = rest[7:11]
+            scratch = rest[11:]
         slots = ((scratch[0:4], scratch[4:8]), (scratch[8:12], scratch[12:16]))
-        slab = plan_ref[0]
+        turns = (scratch[16:18], scratch[18:20])
+        base = fixed_ref[0] + plan_ref[0] * fixed_ref[1] + plan_ref[1] * fixed_ref[2]
+        rate = ticks_ref[0] + plan_ref[0] * ticks_ref[1] + plan_ref[1] * ticks_ref[2]
         group = plan_ref[1]
         frames[pl.ds(0, PAD), :] = jnp.zeros((PAD, LANES), jnp.float32)
         for array in range(arrays):
@@ -200,19 +202,12 @@
             else:
                 frames[at, :] = tails[item]
 
-        def make_turns():
-            base = fixed_ref[0] + slab * fixed_ref[1] + group * fixed_ref[2]
-            rate = ticks_ref[0] + slab * ticks_ref[1] + group * ticks_ref[2]
-
+        def make_stamps():
             def stamp_step(n, total):
-                dropped = drops[pl.ds(pl.multiple_of(n * PAD, 8), PAD), :][0:1]
-                dropped = jnp.broadcast_to(dropped, (PAD, LANES)).astype(jnp.int32)
+                at = pl.ds(pl.multiple_of(n * PAD, 8), PAD)
+                dropped = jnp.broadcast_to(drops[at, :][0:1], (PAD, LANES)).astype(jnp.int32)
                 total = (total + dropped) & (PERIOD - 1)
-                wide = jnp.concatenate([total] * (rows // PAD), axis=0)
-                cosine, sine = cos_sin((base + rate * wide) & (TURN - 1))
-                at = pl.ds(pl.multiple_of(n * rows, 8), rows)
-                cos_ref[at, :] = cosine
-                sin_ref[at, :] = sine
+                stamps[at, :] = total
                 return total
 
             start = jnp.zeros((PAD, LANES), jnp.int32)
@@ -222,7 +217,7 @@
             acc_re[...] = jnp.zeros_like(acc_re)
             acc_im[...] = jnp.zeros_like(acc_im)
             acc_sq[...] = jnp.zeros_like(acc_sq)
-            make_turns()
+            make_stamps()
         else:
             acc_re[...] = old_re[...]
             acc_im[...] = old_im[...]
@@ -230,7 +225,13 @@
         lane = lax.broadcasted_iota(jnp.int32, (Q, LANES), 1)
         left_half = lane < LANES // 2
 
-        def channelize(places, targets):
+        def channelize(places, side):
+            targets = slots[side]
+            at = pl.ds(pl.multiple_of((places[0] // BLOCKS) * PAD, 8), PAD)
+            wide = jnp.concatenate([stamps[at, :]] * (rows // PAD), axis=0)
+            cos_rows, sin_rows = cos_sin((base + rate * wide) & (TURN - 1))
+            turns[side][0][...] = cos_rows
+            turns[side][1][...] = sin_rows
             evens = []
             odds = []
             for place in places:
@@ -245,15 +246,12 @@
             both_odd = split(jnp.concatenate(odds, axis=0))
             from_even = dot3(both_even, (even_h[group], even_l[group]))
             from_odd = dot3(both_odd, (odd_h[group], odd_l[group]))
-            for index, (place, slot) in enumerate(zip(places, targets)):
+            for index, slot in enumerate(targets):
                 part = slice(index * Q, (index + 1) * Q)
-                finish(place, slot, from_even[part], from_odd[part])
-
-        def finish(place, slot, from_even, from_odd):
+                finish(cos_rows, sin_rows, slot, from_even[part], from_odd[part])
+
+        def finish(cos_rows, sin_rows, slot, from_even, from_odd):
             rhs_h, rhs_l, center_re, center_im = slot
-            turn = pl.multiple_of((place // BLOCKS) * rows, 8)
-            cos_rows = cos_ref[pl.ds(turn, rows), :]
-            sin_rows = sin_ref[pl.ds(turn, rows), :]
             row_k, row_l = 4 + pairs, 5 + pairs
             low_cos = cos_rows[row_k : row_k + 1]
             low_sin = sin_rows[row_k : row_k + 1] * small_ref[24:25]
@@ -284,11 +282,10 @@
                 center_re[at] = low_re[at] * c + low_im[at] * s
                 center_im[at] = low_im[at] * c - low_re[at] * s
 
-        def correlate(place, slot):
+        def correlate(turn, slot):
             rhs_h, rhs_l, center_re, center_im = slot
-            turn = pl.multiple_of((place // BLOCKS) * rows, 8)
-            cos_rows = cos_ref[pl.ds(turn, rows), :]
-            sin_rows = sin_ref[pl.ds(turn, rows), :]
+            cos_rows = turn[0][...]
+            sin_rows = turn[1][...]
             right = (rhs_h[...], rhs_l[...])
             group_size = min(pairs, 4)
             for base_pair in range(0, pairs, group_size):
@@ -319,16 +316,16 @@
 
         def work(first, side, more):
             if more:
-                channelize((block_at(first + 2), block_at(first + 3)), slots[1 - side])
+                channelize((block_at(first + 2), block_at(first + 3)), 1 - side)
             for item in range(2):
-                correlate(block_at(first + item), slots[side][item])
+                correlate(turns[side], slots[side][item])
 
         def step(index, carry):
             work(4 * index, 0, True)
             work(4 * index + 2, 1, True)
             return carry
 
-        channelize((block_at(0), block_at(1)), slots[0])
+        channelize((block_at(0), block_at(1)), 0)
         lax.fori_loop(0, count // 4 - 1, step, 0)
         work(count - 4, 0, True)
         work(count - 2, 1, False)
@@ -358,7 +355,7 @@
     ]
     sums = [(bins * width, LW)] * 3
     if opening:
-        shapes = sums + [(slabs * rows, LANES)] * 2 + [(depth, PAD, LANES)]
+        shapes = sums + [(slabs * PAD, LANES), (depth, PAD, LANES)]
         scratch = [(PAD + blocks * Q, LANES), (slabs * PAD, LANES)]
     else:
         shapes = [(bins, width, LW), (2, bins, width, LW)]
@@ -368,8 +365,13 @@
         kernel,
         in_specs=[pl.BlockSpec(memory_space=pltpu.SMEM)] + [vmem] * (7 + inputs),
         out_specs=[vmem] * outputs,
-        scratch_shapes=[pltpu.VMEM(shape, jnp.float32) for shape in scratch] + slot * 4,
-        out_shape=[jax.ShapeDtypeStruct(shape, jnp.float32) for shape in shapes],
+        scratch_shapes=[pltpu.VMEM(shape, jnp.float32) for shape in scratch]
+        + slot * 4
+        + [pltpu.VMEM((rows, LANES), jnp.float32)] * 4,
+        out_shape=[
+            jax.ShapeDtypeStruct(shape, jnp.int32 if opening and index == 3 else jnp.float32)
+            for index, shape in enumerate(shapes)
+        ],
         compiler_params=pltpu.CompilerParams(vmem_limit_bytes=(PAD + blocks * Q) * 4 * LANES + 12 * 1024 * 1024),
         cost_estimate=pl.CostEstimate(flops=work, transcendentals=0, bytes_accessed=4 * 1024 * 1024),
         name="surfaces_first" if opening else "surfaces_last",

time: 57.7 us -> 59 us (1.023)
  waiting for transfers between devices: 21.3 us -> 23.2 us
    ppermute x14, waiting for transfers between devices: 21.3 us -> 23.2 us  [moved(): return lax.ppermute(array, axes, pairs)]
  transfers between devices with their start and end apart: 14 -> 14, of which waited for: 8 -> 7; matrix products, arithmetic and copies ran while one was open for 0% -> 0% of each run, Pallas kernels for 14% -> 13%
where the time goes in v3:
time: 59 us; the launch traced here: 58.9 us
  waiting for transfers between devices  23.2 us (39%)
  starting transfers between devices  16.8 us (28%)
  Pallas kernels  16.1 us (27%)
  between operations  1.43 us (2%)
  local copies, waits for them, and re-layouts  1.37 us (2%)
    ppermute x14, waiting for transfers between devices, moved(): return lax.ppermute(array, axes, pairs)  23.2 us
    ppermute x14, starting transfers between devices, moved(): return lax.ppermute(array, axes, pairs)  16.8 us
    pallas_call x2, Pallas kernels, surfaces(): pl.pallas_call(kernel, in_specs=[pl.BlockSpec(memory_space=pltpu.SMEM)] +...  16.1 us
  transfers between devices with their start and end apart: 14, of which 7 were waited for; matrix products, arithmetic and copies ran while one was open for 0% of the time, Pallas kernels for 13%

profile of v3, /device:TPU:0, one launch (start us, length us, event | category | flops | bytes accessed | tf_op | source)
XLA Modules:
  0.0 58.9 jit_solution(4856173969463201850)
XLA Ops:
  1.3 1.0 %reshape.11 = f32[2,128,64]{2,1,0:T(8,128)S(1)} reshape(f32[2,8192]{1,0:T(2,128)} %param.16) | data formatting | bytes 131072 | tf_op jit(solution)/shard_map/reshape | solution.py:399
  2.3 0.1 copy.19
  2.3 0.1 copy.20
  2.5 5.1 %collective-permute-start.2 = (f32[1,136,128]{2,1,0:T(8,128)S(1)}, f32[1,136,128]{2,1,0:T(8,128)S(1)}, u32[]{:S(2)}, u32[]{:S(2)}) collective-permute-start(f32[1,136,128]{2,1,0:T(8,128)S(1)} %pad_bitcast_fusion), channel_id=1, source_target_pairs={{0,24},{1,25},{2,26},{3,27},{4,28},{5,29},{6,30},{7,31},{8,0},{9,1... | collective-permute-start | bytes 208904 | tf_op jit(solution)/shard_map/ppermute | solution.py:418
  7.6 0.0 collective-permute-start.1
  7.6 1.0 %collective-permute-start = (f32[1,136,128]{2,1,0:T(8,128)S(1)}, f32[1,136,128]{2,1,0:T(8,128)S(1)}, u32[]{:S(2)}, u32[]{:S(2)}) collective-permute-start(f32[1,136,128]{2,1,0:T(8,128)S(1)} %pad_bitcast_fusion), channel_id=1, source_target_pairs={{0,8},{1,9},{2,10},{3,11},{4,12},{5,13},{6,14},{7,15},{8,16},{9,17... | collective-permute-start | bytes 208904 | tf_op jit(solution)/shard_map/ppermute | solution.py:418
  8.6 1.6 %collective-permute-done.2 = f32[1,136,128]{2,1,0:T(8,128)S(1)} collective-permute-done((f32[1,136,128]{2,1,0:T(8,128)S(1)}, f32[1,136,128]{2,1,0:T(8,128)S(1)}, u32[]{:S(2)}, u32[]{:S(2)}) %collective-permute-start.2) | collective-permute-done | bytes 69664 | tf_op jit(solution)/shard_map/ppermute | solution.py:418
  10.2 4.2 %collective-permute-done.1 = f32[1,136,128]{2,1,0:T(8,128)S(1)} collective-permute-done((f32[1,136,128]{2,1,0:T(8,128)S(1)}, f32[1,136,128]{2,1,0:T(8,128)S(1)}, u32[]{:S(2)}, u32[]{:S(2)}) %collective-permute-start.1) | collective-permute-done | bytes 69664 | tf_op jit(solution)/shard_map/ppermute | solution.py:418
  14.4 0.0 collective-permute-done
  14.4 1.6 %collective-permute-start.4 = (f32[4,136,128]{2,1,0:T(8,128)S(1)}, f32[4,136,128]{2,1,0:T(8,128)S(1)}, u32[]{:S(2)}, u32[]{:S(2)}) collective-permute-start(f32[4,136,128]{2,1,0:T(8,128)S(1)} %pad_maximum_fusion.rest_0_), channel_id=1, source_target_pairs={{0,1},{1,0},{2,3},{3,2},{4,5},{5,4},{6,7},{7,6},{8,9},{9,8},{10,11... | collective-permute-start | bytes 835592 | tf_op jit(solution)/shard_map/ppermute | solution.py:418
  16.0 1.5 %collective-permute-start.3 = (f32[4,136,128]{2,1,0:T(8,128)S(1)}, f32[4,136,128]{2,1,0:T(8,128)S(1)}, u32[]{:S(2)}, u32[]{:S(2)}) collective-permute-start(f32[4,136,128]{2,1,0:T(8,128)S(1)} %pad_maximum_fusion.rest_0_), channel_id=1, source_target_pairs={{0,4},{1,5},{2,6},{3,7},{4,0},{5,1},{6,2},{7,3},{8,12},{9,13},{10,... | collective-permute-start | bytes 835592 | tf_op jit(solution)/shard_map/ppermute | solution.py:418
  17.5 5.5 %collective-permute-done.4.rest_1_ = f32[4,136,128]{2,1,0:T(8,128)S(1)} collective-permute-done((f32[4,136,128]{2,1,0:T(8,128)S(1)}, f32[4,136,128]{2,1,0:T(8,128)S(1)}, u32[]{:S(2)}, u32[]{:S(2)}) %collective-permute-start.4) | collective-permute-done | bytes 278560 | tf_op jit(solution)/shard_map/ppermute | solution.py:418
  23.0 1.5 %collective-permute-start.5 = (f32[4,136,128]{2,1,0:T(8,128)S(1)}, f32[4,136,128]{2,1,0:T(8,128)S(1)}, u32[]{:S(2)}, u32[]{:S(2)}) collective-permute-start(f32[4,136,128]{2,1,0:T(8,128)S(1)} %collective-permute-done.4.rest_1_), channel_id=1, source_target_pairs={{0,4},{1,5},{2,6},{3,7},{4,0},{5,1},{6,2},{7,3},{8,12},{9,13},{10,... | collective-permute-start | bytes 835592 | tf_op jit(solution)/shard_map/ppermute | solution.py:418
  24.5 0.5 collective-permute-start.9
  25.0 0.0 copy-start.4
  25.0 0.0 copy-start.5
  25.0 1.2 %collective-permute-start.13 = (f32[4,8,128]{2,1,0:T(8,128)S(1)}, f32[4,8,128]{2,1,0:T(8,128)S(1)}, u32[]{:S(2)}, u32[]{:S(2)}) collective-permute-start(f32[4,8,128]{2,1,0:T(8,128)S(1)} %pad_maximum_fusion.1), channel_id=1, source_target_pairs={{0,7},{1,6},{2,5},{3,4},{4,3},{5,2},{6,1},{7,0},{8,15},{9,14},{10,... | collective-permute-start | bytes 49160 | tf_op jit(solution)/shard_map/ppermute | solution.py:418
  26.2 3.9 %collective-permute-done.13.rest_7_ = f32[4,8,128]{2,1,0:T(8,128)S(1)} collective-permute-done((f32[4,8,128]{2,1,0:T(8,128)S(1)}, f32[4,8,128]{2,1,0:T(8,128)S(1)}, u32[]{:S(2)}, u32[]{:S(2)}) %collective-permute-start.13) | collective-permute-done | bytes 16416 | tf_op jit(solution)/shard_map/ppermute | solution.py:418
  30.1 2.8 %collective-permute-start.12 = (f32[4,8,128]{2,1,0:T(8,128)S(1)}, f32[4,8,128]{2,1,0:T(8,128)S(1)}, u32[]{:S(2)}, u32[]{:S(2)}) collective-permute-start(f32[4,8,128]{2,1,0:T(8,128)S(1)} %pad_maximum_fusion.1), channel_id=1, source_target_pairs={{0,6},{1,7},{2,4},{3,5},{4,2},{5,3},{6,0},{7,1},{8,14},{9,15},{10,... | collective-permute-start | bytes 49160 | tf_op jit(solution)/shard_map/ppermute | solution.py:418
  32.9 1.4 %collective-permute-done.12.rest_6_ = f32[4,8,128]{2,1,0:T(8,128)S(1)} collective-permute-done((f32[4,8,128]{2,1,0:T(8,128)S(1)}, f32[4,8,128]{2,1,0:T(8,128)S(1)}, u32[]{:S(2)}, u32[]{:S(2)}) %collective-permute-start.12) | collective-permute-done | bytes 16416 | tf_op jit(solution)/shard_map/ppermute | solution.py:418
  34.3 0.5 collective-permute-start.11
  34.8 4.2 %collective-permute-done.11.rest_5_ = f32[4,8,128]{2,1,0:T(8,128)S(1)} collective-permute-done((f32[4,8,128]{2,1,0:T(8,128)S(1)}, f32[4,8,128]{2,1,0:T(8,128)S(1)}, u32[]{:S(2)}, u32[]{:S(2)}) %collective-permute-start.11) | collective-permute-done | bytes 16416 | tf_op jit(solution)/shard_map/ppermute | solution.py:418
  38.9 0.5 collective-permute-start.10
  39.5 0.2 stack.287.plan_ref
  39.7 0.2 collective-permute-start.6
  39.9 0.0 collective-permute-done.5.rest_1_
  39.9 0.4 collective-permute-start.7
  40.3 2.4 %collective-permute-done.10.rest_4_ = f32[4,8,128]{2,1,0:T(8,128)S(1)} collective-permute-done((f32[4,8,128]{2,1,0:T(8,128)S(1)}, f32[4,8,128]{2,1,0:T(8,128)S(1)}, u32[]{:S(2)}, u32[]{:S(2)}) %collective-permute-start.10) | collective-permute-done | bytes 16416 | tf_op jit(solution)/shard_map/ppermute | solution.py:418
  42.7 0.0 collective-permute-done.9.rest_3_
  42.8 7.6 %surfaces_first.1 = (f32[512,128]{1,0:T(8,128)S(1)}, f32[512,128]{1,0:T(8,128)S(1)}, f32[512,128]{1,0:T(8,128)S(1)}, s32[128,128]{1,0:T(8,128)S(1)}, f32[4,8,128]{2,1,0:T(8,128)S(1)}) custom-call(s32[86]{0:T(128)S(1)} %stack.287.plan_ref, s32[3,16,128]{2,1,0:T(8,128)S(1)} %copy-done.5, s32[3,16,128]{2,1,0:T(8,128)S(1)} %copy-done.4, ...), custom_call_target="tpu_custom_call" | custom-call | flops 4831838208 | bytes 4194304 | tf_op jit(solution)/shard_map/surfaces_first/pallas_call | solution.py:364
  50.4 0.0 collective-permute-done.7.rest_3_
  50.4 8.5 %surfaces_last.1 = (f32[8,64,128]{2,1,0:T(8,128)}, f32[2,8,64,128]{3,2,1,0:T(8,128)}) custom-call(s32[86]{0:T(128)S(1)} %stack.287.plan_ref, s32[3,16,128]{2,1,0:T(8,128)S(1)} %copy-done.5, s32[3,16,128]{2,1,0:T(8,128)S(1)} %copy-done.4, f32[32,128]{1,0:T(8,128)S(1)} %copy-done.6, bf16[2,256,256]{2,1,0:T(8,128)(2,1)S(1)} %copy-done.3, ...), custom_call_target="tpu_custom_call" | custom-call | flops 4831838208 | bytes 4194304 | tf_op jit(solution)/shard_map/surfaces_last/pallas_call | solution.py:364
  (21 shorter events, 0.1 us)
Async XLA Ops:
  2.5 7.7 %collective-permute-start.2 = (f32[1,136,128]{2,1,0:T(8,128)S(1)}, f32[1,136,128]{2,1,0:T(8,128)S(1)}, u32[]{:S(2)}, u32[]{:S(2)}) collective-permute-start(f32[1,136,128]{2,1,0:T(8,128)S(1)} %pad_bitcast_fusion), channel_id=1, source_target_pairs={{0,24},{1,25},{2,26},{3,27},{4,28},{5,29},{6,30},{7,31},{8,0},{9,1... | collective-permute-start | bytes 208904 | tf_op jit(solution)/shard_map/ppermute | solution.py:418
  7.6 6.8 %collective-permute-start.1 = (f32[1,136,128]{2,1,0:T(8,128)S(1)}, f32[1,136,128]{2,1,0:T(8,128)S(1)}, u32[]{:S(2)}, u32[]{:S(2)}) collective-permute-start(f32[1,136,128]{2,1,0:T(8,128)S(1)} %pad_bitcast_fusion), channel_id=1, source_target_pairs={{0,16},{1,17},{2,18},{3,19},{4,20},{5,21},{6,22},{7,23},{8,24},{9,... | collective-permute-start | bytes 208904 | tf_op jit(solution)/shard_map/ppermute | solution.py:418
  7.6 6.8 %collective-permute-start = (f32[1,136,128]{2,1,0:T(8,128)S(1)}, f32[1,136,128]{2,1,0:T(8,128)S(1)}, u32[]{:S(2)}, u32[]{:S(2)}) collective-permute-start(f32[1,136,128]{2,1,0:T(8,128)S(1)} %pad_bitcast_fusion), channel_id=1, source_target_pairs={{0,8},{1,9},{2,10},{3,11},{4,12},{5,13},{6,14},{7,15},{8,16},{9,17... | collective-permute-start | bytes 208904 | tf_op jit(solution)/shard_map/ppermute | solution.py:418
  14.4 28.3 %copy-start.3 = (bf16[2,256,256]{2,1,0:T(8,128)(2,1)S(1)}, bf16[2,256,256]{2,1,0:T(8,128)(2,1)}, u32[]{:S(2)}) copy-start(bf16[2,256,256]{2,1,0:T(8,128)(2,1)} %constant.509.clone.even_h) | copy-start | bytes 786436
  14.4 8.6 %collective-permute-start.4 = (f32[4,136,128]{2,1,0:T(8,128)S(1)}, f32[4,136,128]{2,1,0:T(8,128)S(1)}, u32[]{:S(2)}, u32[]{:S(2)}) collective-permute-start(f32[4,136,128]{2,1,0:T(8,128)S(1)} %pad_maximum_fusion.rest_0_), channel_id=1, source_target_pairs={{0,1},{1,0},{2,3},{3,2},{4,5},{5,4},{6,7},{7,6},{8,9},{9,8},{10,11... | collective-permute-start | bytes 835592 | tf_op jit(solution)/shard_map/ppermute | solution.py:418
  16.0 23.7 %collective-permute-start.3 = (f32[4,136,128]{2,1,0:T(8,128)S(1)}, f32[4,136,128]{2,1,0:T(8,128)S(1)}, u32[]{:S(2)}, u32[]{:S(2)}) collective-permute-start(f32[4,136,128]{2,1,0:T(8,128)S(1)} %pad_maximum_fusion.rest_0_), channel_id=1, source_target_pairs={{0,4},{1,5},{2,6},{3,7},{4,0},{5,1},{6,2},{7,3},{8,12},{9,13},{10,... | collective-permute-start | bytes 835592 | tf_op jit(solution)/shard_map/ppermute | solution.py:418
  23.0 16.9 %collective-permute-start.5 = (f32[4,136,128]{2,1,0:T(8,128)S(1)}, f32[4,136,128]{2,1,0:T(8,128)S(1)}, u32[]{:S(2)}, u32[]{:S(2)}) collective-permute-start(f32[4,136,128]{2,1,0:T(8,128)S(1)} %collective-permute-done.4.rest_1_), channel_id=1, source_target_pairs={{0,4},{1,5},{2,6},{3,7},{4,0},{5,1},{6,2},{7,3},{8,12},{9,13},{10,... | collective-permute-start | bytes 835592 | tf_op jit(solution)/shard_map/ppermute | solution.py:418
  24.5 18.2 %collective-permute-start.8 = (f32[4,136,128]{2,1,0:T(8,128)S(1)}, f32[4,136,128]{2,1,0:T(8,128)S(1)}, u32[]{:S(2)}, u32[]{:S(2)}) collective-permute-start(f32[4,136,128]{2,1,0:T(8,128)S(1)} %pad_maximum_fusion.rest_0_), channel_id=1, source_target_pairs={{0,2},{1,3},{2,0},{3,1},{4,6},{5,7},{6,4},{7,5},{8,10},{9,11},{10,... | collective-permute-start | bytes 835592 | tf_op jit(solution)/shard_map/ppermute | solution.py:418
  24.5 18.2 %collective-permute-start.9 = (f32[4,136,128]{2,1,0:T(8,128)S(1)}, f32[4,136,128]{2,1,0:T(8,128)S(1)}, u32[]{:S(2)}, u32[]{:S(2)}) collective-permute-start(f32[4,136,128]{2,1,0:T(8,128)S(1)} %collective-permute-done.4.rest_1_), channel_id=1, source_target_pairs={{0,2},{1,3},{2,0},{3,1},{4,6},{5,7},{6,4},{7,5},{8,10},{9,11},{10,... | collective-permute-start | bytes 835592 | tf_op jit(solution)/shard_map/ppermute | solution.py:418
  25.0 17.7 %copy-start.6 = (f32[32,128]{1,0:T(8,128)S(1)}, f32[32,128]{1,0:T(8,128)}, u32[]{:S(2)}) copy-start(f32[32,128]{1,0:T(8,128)} %constant.508.clone.small_ref) | copy-start | bytes 49156
  25.0 17.7 %copy-start.4 = (s32[3,16,128]{2,1,0:T(8,128)S(1)}, s32[3,16,128]{2,1,0:T(8,128)}, u32[]{:S(2)}) copy-start(s32[3,16,128]{2,1,0:T(8,128)} %constant.507.clone.ticks_ref) | copy-start | bytes 73732
  25.0 17.7 %copy-start.5 = (s32[3,16,128]{2,1,0:T(8,128)S(1)}, s32[3,16,128]{2,1,0:T(8,128)}, u32[]{:S(2)}) copy-start(s32[3,16,128]{2,1,0:T(8,128)} %constant.506.clone.fixed_ref) | copy-start | bytes 73732
  25.0 5.0 %collective-permute-start.13 = (f32[4,8,128]{2,1,0:T(8,128)S(1)}, f32[4,8,128]{2,1,0:T(8,128)S(1)}, u32[]{:S(2)}, u32[]{:S(2)}) collective-permute-start(f32[4,8,128]{2,1,0:T(8,128)S(1)} %pad_maximum_fusion.1), channel_id=1, source_target_pairs={{0,7},{1,6},{2,5},{3,4},{4,3},{5,2},{6,1},{7,0},{8,15},{9,14},{10,... | collective-permute-start | bytes 49160 | tf_op jit(solution)/shard_map/ppermute | solution.py:418
  30.1 4.2 %collective-permute-start.12 = (f32[4,8,128]{2,1,0:T(8,128)S(1)}, f32[4,8,128]{2,1,0:T(8,128)S(1)}, u32[]{:S(2)}, u32[]{:S(2)}) collective-permute-start(f32[4,8,128]{2,1,0:T(8,128)S(1)} %pad_maximum_fusion.1), channel_id=1, source_target_pairs={{0,6},{1,7},{2,4},{3,5},{4,2},{5,3},{6,0},{7,1},{8,14},{9,15},{10,... | collective-permute-start | bytes 49160 | tf_op jit(solution)/shard_map/ppermute | solution.py:418
  34.3 4.6 %collective-permute-start.11 = (f32[4,8,128]{2,1,0:T(8,128)S(1)}, f32[4,8,128]{2,1,0:T(8,128)S(1)}, u32[]{:S(2)}, u32[]{:S(2)}) collective-permute-start(f32[4,8,128]{2,1,0:T(8,128)S(1)} %pad_maximum_fusion.1), channel_id=1, source_target_pairs={{0,5},{1,4},{2,7},{3,6},{4,1},{5,0},{6,3},{7,2},{8,13},{9,12},{10,... | collective-permute-start | bytes 49160 | tf_op jit(solution)/shard_map/ppermute | solution.py:418
  34.8 7.9 %copy-start.2 = (bf16[2,256,256]{2,1,0:T(8,128)(2,1)S(1)}, bf16[2,256,256]{2,1,0:T(8,128)(2,1)}, u32[]{:S(2)}) copy-start(bf16[2,256,256]{2,1,0:T(8,128)(2,1)} %constant.510.clone.even_l) | copy-start | bytes 786436
  38.9 3.7 %collective-permute-start.10 = (f32[4,8,128]{2,1,0:T(8,128)S(1)}, f32[4,8,128]{2,1,0:T(8,128)S(1)}, u32[]{:S(2)}, u32[]{:S(2)}) collective-permute-start(f32[4,8,128]{2,1,0:T(8,128)S(1)} %pad_maximum_fusion.1), channel_id=1, source_target_pairs={{0,4},{1,5},{2,6},{3,7},{4,0},{5,1},{6,2},{7,3},{8,12},{9,13},{10,... | collective-permute-start | bytes 49160 | tf_op jit(solution)/shard_map/ppermute | solution.py:418
  39.5 3.3 %copy-start.1 = (bf16[2,256,256]{2,1,0:T(8,128)(2,1)S(1)}, bf16[2,256,256]{2,1,0:T(8,128)(2,1)}, u32[]{:S(2)}) copy-start(bf16[2,256,256]{2,1,0:T(8,128)(2,1)} %constant.511.clone.odd_h) | copy-start | bytes 786436
  39.5 3.3 %copy-start = (bf16[2,256,256]{2,1,0:T(8,128)(2,1)S(1)}, bf16[2,256,256]{2,1,0:T(8,128)(2,1)}, u32[]{:S(2)}) copy-start(bf16[2,256,256]{2,1,0:T(8,128)(2,1)} %constant.512.clone.odd_l) | copy-start | bytes 786436
  39.7 10.7 %collective-permute-start.6 = (f32[4,136,128]{2,1,0:T(8,128)S(1)}, f32[4,136,128]{2,1,0:T(8,128)S(1)}, u32[]{:S(2)}, u32[]{:S(2)}) collective-permute-start(f32[4,136,128]{2,1,0:T(8,128)S(1)} %collective-permute-done.3.rest_0_), channel_id=1, source_target_pairs={{0,2},{1,3},{2,0},{3,1},{4,6},{5,7},{6,4},{7,5},{8,10},{9,11},{10,... | collective-permute-start | bytes 835592 | tf_op jit(solution)/shard_map/ppermute | solution.py:418
  39.9 10.5 %collective-permute-start.7 = (f32[4,136,128]{2,1,0:T(8,128)S(1)}, f32[4,136,128]{2,1,0:T(8,128)S(1)}, u32[]{:S(2)}, u32[]{:S(2)}) collective-permute-start(f32[4,136,128]{2,1,0:T(8,128)S(1)} %collective-permute-done.5.rest_1_), channel_id=1, source_target_pairs={{0,2},{1,3},{2,0},{3,1},{4,6},{5,7},{6,4},{7,5},{8,10},{9,11},{10,... | collective-permute-start | bytes 835592 | tf_op jit(solution)/shard_map/ppermute | solution.py:418

commit v4 on v3

--- a/solution.py
+++ b/solution.py
@@ -172,9 +172,10 @@
             scratch = rest[2:]
         else:
             old_re, old_im, old_sq, stamps, tails = rest[:5]
-            held_ref, coherent_ref = out_refs
+            held_out, coherent_out = out_refs
             frames, acc_re, acc_im, acc_sq = rest[7:11]
             scratch = rest[11:]
+            held_ref, coherent_ref, sems = scratch[20:23]
         slots = ((scratch[0:4], scratch[4:8]), (scratch[8:12], scratch[12:16]))
         turns = (scratch[16:18], scratch[18:20])
         base = fixed_ref[0] + plan_ref[0] * fixed_ref[1] + plan_ref[1] * fixed_ref[2]
@@ -337,6 +338,7 @@
         def natural(value):
             return jnp.take_along_axis(value, source, axis=1, mode="promise_in_bounds")
 
+        copies = []
         for bin_index in range(bins):
             for part, kappa in enumerate((0, 2, 1, 3)):
                 first = bin_index * width + part * quarter
@@ -345,6 +347,15 @@
                 held_ref[bin_index, put, :] = natural(jnp.sqrt(acc_sq[take]))
                 coherent_ref[0, bin_index, put, :] = natural(acc_re[take] * blend)
                 coherent_ref[1, bin_index, put, :] = natural(acc_im[take] * blend)
+            pairs_out = [(held_ref.at[bin_index], held_out.at[bin_index])]
+            for plane in range(2):
+                pairs_out.append((coherent_ref.at[plane, bin_index], coherent_out.at[plane, bin_index]))
+            for lane_index, (source_ref, target_ref) in enumerate(pairs_out):
+                copy = pltpu.make_async_copy(source_ref, target_ref, sems.at[lane_index, bin_index])
+                copy.start()
+                copies.append(copy)
+        for copy in copies:
+            copy.wait()
 
     vmem = pl.BlockSpec(memory_space=pltpu.VMEM)
     slot = [
@@ -357,17 +368,21 @@
     if opening:
         shapes = sums + [(slabs * PAD, LANES), (depth, PAD, LANES)]
         scratch = [(PAD + blocks * Q, LANES), (slabs * PAD, LANES)]
+        ending = []
     else:
         shapes = [(bins, width, LW), (2, bins, width, LW)]
         scratch = [(PAD + blocks * Q, LANES)] + sums
+        ending = [pltpu.VMEM(shape, jnp.float32) for shape in shapes]
+        ending += [pltpu.SemaphoreType.DMA((3, bins))]
     work = 2 * 3 * count * NCH * NCH * (2 * Q + 2 * bins * width // 2)
     return pl.pallas_call(
         kernel,
         in_specs=[pl.BlockSpec(memory_space=pltpu.SMEM)] + [vmem] * (7 + inputs),
-        out_specs=[vmem] * outputs,
+        out_specs=[vmem if opening else pl.BlockSpec(memory_space=pl.ANY)] * outputs,
         scratch_shapes=[pltpu.VMEM(shape, jnp.float32) for shape in scratch]
         + slot * 4
-        + [pltpu.VMEM((rows, LANES), jnp.float32)] * 4,
+        + [pltpu.VMEM((rows, LANES), jnp.float32)] * 4
+        + ending,
         out_shape=[
             jax.ShapeDtypeStruct(shape, jnp.int32 if opening and index == 3 else jnp.float32)
             for index, shape in enumerate(shapes)
@@ -420,14 +435,19 @@
     line = [own]
     for step in range(1, outer):
         line.append(moved(own, (step, 0, 0, 0)))
+    own_near = [moved(own, (0, 0, 0, member)) for member in range(1, groups)]
+    own_far = moved(own, (0, 1, 0, 0))
+    rest = jnp.concatenate(line[1:], axis=0)
     line = jnp.concatenate(line, axis=0)
     tiles = jnp.concatenate([line[:, hops : hops + PAD - lead], line[:, hops - lead : hops]], axis=1)
     note_steps = [(1, core, member) for core in range(2) for member in range(groups)]
     notes = []
     for by in note_steps:
         notes.append(moved(tiles, (0,) + by))
-    near = [line] + [moved(line, (0, 0, 0, member)) for member in range(1, groups)]
-    far = [moved(line, (0, 1, 0, 0))]
+    near = [moved(rest, (0, 0, 0, member)) for member in range(1, groups)]
+    far = [moved(rest, (0, 1, 0, 0))]
+    near = [line] + [jnp.concatenate(pair, axis=0) for pair in zip(own_near, near)]
+    far = [jnp.concatenate([own_far, far[0]], axis=0)]
     far += [moved(piece, (0, 1, 0, 0)) for piece in near[1:]]
     near_steps = [(0, 0, member) for member in range(groups)]
     far_steps = [(1, 0, member) for member in range(groups)]

time: 59 us -> 55.7 us (0.944); the launches traced: 58.9 us -> 54.8 us
  waiting for transfers between devices: 23.2 us -> 14.6 us
  starting transfers between devices: 16.8 us -> 20.7 us
    ppermute x14 -> x16, waiting for transfers between devices: 23.2 us -> 14.6 us  [moved(): return lax.ppermute(array, axes, pairs)]
    ppermute x14 -> x16, starting transfers between devices: 16.8 us -> 20.7 us  [moved(): return lax.ppermute(array, axes, pairs)]
  transfers between devices with their start and end apart: 14 -> 16, of which waited for: 7 -> 7; matrix products, arithmetic and copies ran while one was open for 0% -> 1% of each run, Pallas kernels for 13% -> 14%
where the time goes in v4:
time: 55.7 us; the launch traced here: 54.8 us
  starting transfers between devices  20.7 us (37%)
  Pallas kernels  16.4 us (29%)
  waiting for transfers between devices  14.6 us (26%)
  between operations  1.62 us (3%)
  local copies, waits for them, and re-layouts  1.43 us (3%)
    ppermute x16, starting transfers between devices, moved(): return lax.ppermute(array, axes, pairs)  20.7 us
    pallas_call x2, Pallas kernels, surfaces(): pl.pallas_call(kernel, in_specs=[pl.BlockSpec(memory_space=pltpu.SMEM)] +...  16.4 us
    ppermute x16, waiting for transfers between devices, moved(): return lax.ppermute(array, axes, pairs)  14.6 us
  transfers between devices with their start and end apart: 16, of which 7 were waited for; matrix products, arithmetic and copies ran while one was open for 1% of the time, Pallas kernels for 14%

profile of v4, /device:TPU:0, one launch (start us, length us, event | category | flops | bytes accessed | tf_op | source)
XLA Modules:
  0.0 54.8 jit_solution(13668452797961173211)
XLA Ops:
  0.6 1.0 %reshape.11 = f32[2,128,64]{2,1,0:T(8,128)S(1)} reshape(f32[2,8192]{1,0:T(2,128)} %param.16) | data formatting | bytes 131072 | tf_op jit(solution)/shard_map/reshape | solution.py:414
  1.6 0.1 copy.19
  1.7 0.1 copy.20
  2.5 3.1 %collective-permute-start.1 = (f32[1,136,128]{2,1,0:T(8,128)S(1)}, f32[1,136,128]{2,1,0:T(8,128)S(1)}, u32[]{:S(2)}, u32[]{:S(2)}) collective-permute-start(f32[1,136,128]{2,1,0:T(8,128)S(1)} %pad_bitcast_fusion), channel_id=1, source_target_pairs={{0,8},{1,9},{2,10},{3,11},{4,12},{5,13},{6,14},{7,15},{8,16},{9,17... | collective-permute-start | bytes 208904 | tf_op jit(solution)/shard_map/ppermute | solution.py:433
  5.6 2.6 %collective-permute-start.2 = (f32[1,136,128]{2,1,0:T(8,128)S(1)}, f32[1,136,128]{2,1,0:T(8,128)S(1)}, u32[]{:S(2)}, u32[]{:S(2)}) collective-permute-start(f32[1,136,128]{2,1,0:T(8,128)S(1)} %pad_bitcast_fusion), channel_id=1, source_target_pairs={{0,16},{1,17},{2,18},{3,19},{4,20},{5,21},{6,22},{7,23},{8,24},{9,... | collective-permute-start | bytes 208904 | tf_op jit(solution)/shard_map/ppermute | solution.py:433
  8.2 1.3 %collective-permute-start.3 = (f32[1,136,128]{2,1,0:T(8,128)S(1)}, f32[1,136,128]{2,1,0:T(8,128)S(1)}, u32[]{:S(2)}, u32[]{:S(2)}) collective-permute-start(f32[1,136,128]{2,1,0:T(8,128)S(1)} %pad_bitcast_fusion), channel_id=1, source_target_pairs={{0,24},{1,25},{2,26},{3,27},{4,28},{5,29},{6,30},{7,31},{8,0},{9,1... | collective-permute-start | bytes 208904 | tf_op jit(solution)/shard_map/ppermute | solution.py:433
  9.5 1.5 %collective-permute-start.5 = (f32[1,136,128]{2,1,0:T(8,128)S(1)}, f32[1,136,128]{2,1,0:T(8,128)S(1)}, u32[]{:S(2)}, u32[]{:S(2)}) collective-permute-start(f32[1,136,128]{2,1,0:T(8,128)S(1)} %pad_bitcast_fusion), channel_id=1, source_target_pairs={{0,1},{1,0},{2,3},{3,2},{4,5},{5,4},{6,7},{7,6},{8,9},{9,8},{10,11... | collective-permute-start | bytes 208904 | tf_op jit(solution)/shard_map/ppermute | solution.py:433
  11.0 1.5 %collective-permute-start = (f32[1,136,128]{2,1,0:T(8,128)S(1)}, f32[1,136,128]{2,1,0:T(8,128)S(1)}, u32[]{:S(2)}, u32[]{:S(2)}) collective-permute-start(f32[1,136,128]{2,1,0:T(8,128)S(1)} %pad_bitcast_fusion), channel_id=1, source_target_pairs={{0,4},{1,5},{2,6},{3,7},{4,0},{5,1},{6,2},{7,3},{8,12},{9,13},{10,... | collective-permute-start | bytes 208904 | tf_op jit(solution)/shard_map/ppermute | solution.py:433
  12.5 0.3 collective-permute-done.2
  12.9 0.2 collective-permute-done.3
  13.1 1.6 %collective-permute-start.6 = (f32[3,136,128]{2,1,0:T(8,128)S(1)}, f32[3,136,128]{2,1,0:T(8,128)S(1)}, u32[]{:S(2)}, u32[]{:S(2)}) collective-permute-start(f32[3,136,128]{2,1,0:T(8,128)S(1)} %constant_dynamic-update-slice_fusion), channel_id=1, source_target_pairs={{0,1},{1,0},{2,3},{3,2},{4,5},{5,4},{6,7},{7,6},{8,9},{9,8},{10,11... | collective-permute-start | bytes 626696 | tf_op jit(solution)/shard_map/ppermute | solution.py:433
  14.7 0.1 collective-permute-start.10
  14.8 1.6 %collective-permute-start.4 = (f32[3,136,128]{2,1,0:T(8,128)S(1)}, f32[3,136,128]{2,1,0:T(8,128)S(1)}, u32[]{:S(2)}, u32[]{:S(2)}) collective-permute-start(f32[3,136,128]{2,1,0:T(8,128)S(1)} %constant_dynamic-update-slice_fusion), channel_id=1, source_target_pairs={{0,4},{1,5},{2,6},{3,7},{4,0},{5,1},{6,2},{7,3},{8,12},{9,13},{10,... | collective-permute-start | bytes 626696 | tf_op jit(solution)/shard_map/ppermute | solution.py:433
  16.4 0.0 collective-permute-done.5
  16.4 3.5 %collective-permute-done.6 = f32[3,136,128]{2,1,0:T(8,128)S(1)} collective-permute-done((f32[3,136,128]{2,1,0:T(8,128)S(1)}, f32[3,136,128]{2,1,0:T(8,128)S(1)}, u32[]{:S(2)}, u32[]{:S(2)}) %collective-permute-start.6) | collective-permute-done | bytes 208928 | tf_op jit(solution)/shard_map/ppermute | solution.py:433
  19.9 0.1 collective-permute-start.11
  20.0 1.3 %collective-permute-start.7 = (f32[4,136,128]{2,1,0:T(8,128)S(1)}, f32[4,136,128]{2,1,0:T(8,128)S(1)}, u32[]{:S(2)}, u32[]{:S(2)}) collective-permute-start(f32[4,136,128]{2,1,0:T(8,128)S(1)} %constant_dynamic-update-slice_fusion.5.rest_1_), channel_id=1, source_target_pairs={{0,4},{1,5},{2,6},{3,7},{4,0},{5,1},{6,2},{7,3},{8,12},{9,13},{10,... | collective-permute-start | bytes 835592 | tf_op jit(solution)/shard_map/ppermute | solution.py:433
  21.4 0.0 collective-permute-done
  21.4 0.8 %collective-permute-start.12 = (f32[4,8,128]{2,1,0:T(8,128)S(1)}, f32[4,8,128]{2,1,0:T(8,128)S(1)}, u32[]{:S(2)}, u32[]{:S(2)}) collective-permute-start(f32[4,8,128]{2,1,0:T(8,128)S(1)} %pad_maximum_fusion.1), channel_id=1, source_target_pairs={{0,4},{1,5},{2,6},{3,7},{4,0},{5,1},{6,2},{7,3},{8,12},{9,13},{10,... | collective-permute-start | bytes 49160 | tf_op jit(solution)/shard_map/ppermute | solution.py:433
  22.3 0.0 copy-start.2
  22.4 0.2 stack.287.plan_ref
  22.5 0.0 copy-start
  22.5 0.0 copy-start.1
  22.6 6.9 %collective-permute-done.12.rest_4_ = f32[4,8,128]{2,1,0:T(8,128)S(1)} collective-permute-done((f32[4,8,128]{2,1,0:T(8,128)S(1)}, f32[4,8,128]{2,1,0:T(8,128)S(1)}, u32[]{:S(2)}, u32[]{:S(2)}) %collective-permute-start.12) | collective-permute-done | bytes 16416 | tf_op jit(solution)/shard_map/ppermute | solution.py:433
  29.4 2.2 %collective-permute-start.13 = (f32[4,8,128]{2,1,0:T(8,128)S(1)}, f32[4,8,128]{2,1,0:T(8,128)S(1)}, u32[]{:S(2)}, u32[]{:S(2)}) collective-permute-start(f32[4,8,128]{2,1,0:T(8,128)S(1)} %pad_maximum_fusion.1), channel_id=1, source_target_pairs={{0,5},{1,4},{2,7},{3,6},{4,1},{5,0},{6,3},{7,2},{8,13},{9,12},{10,... | collective-permute-start | bytes 49160 | tf_op jit(solution)/shard_map/ppermute | solution.py:433
  31.7 2.4 %collective-permute-done.13.rest_5_ = f32[4,8,128]{2,1,0:T(8,128)S(1)} collective-permute-done((f32[4,8,128]{2,1,0:T(8,128)S(1)}, f32[4,8,128]{2,1,0:T(8,128)S(1)}, u32[]{:S(2)}, u32[]{:S(2)}) %collective-permute-start.13) | collective-permute-done | bytes 16416 | tf_op jit(solution)/shard_map/ppermute | solution.py:433
  34.1 2.5 %collective-permute-start.15 = (f32[4,8,128]{2,1,0:T(8,128)S(1)}, f32[4,8,128]{2,1,0:T(8,128)S(1)}, u32[]{:S(2)}, u32[]{:S(2)}) collective-permute-start(f32[4,8,128]{2,1,0:T(8,128)S(1)} %pad_maximum_fusion.1), channel_id=1, source_target_pairs={{0,7},{1,6},{2,5},{3,4},{4,3},{5,2},{6,1},{7,0},{8,15},{9,14},{10,... | collective-permute-start | bytes 49160 | tf_op jit(solution)/shard_map/ppermute | solution.py:433
  36.6 0.7 %collective-permute-done.14.rest_6_ = f32[4,8,128]{2,1,0:T(8,128)S(1)} collective-permute-done((f32[4,8,128]{2,1,0:T(8,128)S(1)}, f32[4,8,128]{2,1,0:T(8,128)S(1)}, u32[]{:S(2)}, u32[]{:S(2)}) %collective-permute-start.14) | collective-permute-done | bytes 16416 | tf_op jit(solution)/shard_map/ppermute | solution.py:433
  37.2 0.5 collective-permute-start.9
  37.8 0.6 %collective-permute-done.15.rest_7_ = f32[4,8,128]{2,1,0:T(8,128)S(1)} collective-permute-done((f32[4,8,128]{2,1,0:T(8,128)S(1)}, f32[4,8,128]{2,1,0:T(8,128)S(1)}, u32[]{:S(2)}, u32[]{:S(2)}) %collective-permute-start.15) | collective-permute-done | bytes 16416 | tf_op jit(solution)/shard_map/ppermute | solution.py:433
  38.4 7.7 %surfaces_first.1 = (f32[512,128]{1,0:T(8,128)S(1)}, f32[512,128]{1,0:T(8,128)S(1)}, f32[512,128]{1,0:T(8,128)S(1)}, s32[128,128]{1,0:T(8,128)S(1)}, f32[4,8,128]{2,1,0:T(8,128)S(1)}) custom-call(s32[86]{0:T(128)S(1)} %stack.287.plan_ref, s32[3,16,128]{2,1,0:T(8,128)S(1)} %copy-done.4, s32[3,16,128]{2,1,0:T(8,128)S(1)} %copy-done.5, ...), custom_call_target="tpu_custom_call" | custom-call | flops 4831838208 | bytes 4194304 | tf_op jit(solution)/shard_map/surfaces_first/pallas_call | solution.py:378
  46.1 8.7 %surfaces_last.1 = (f32[8,64,128]{2,1,0:T(8,128)}, f32[2,8,64,128]{3,2,1,0:T(8,128)}) custom-call(s32[86]{0:T(128)S(1)} %stack.287.plan_ref, s32[3,16,128]{2,1,0:T(8,128)S(1)} %copy-done.4, s32[3,16,128]{2,1,0:T(8,128)S(1)} %copy-done.5, f32[32,128]{1,0:T(8,128)S(1)} %copy-done.6, bf16[2,256,256]{2,1,0:T(8,128)(2,1)S(1)} %copy-done, ...), custom_call_target="tpu_custom_call" | custom-call | flops 4831838208 | bytes 4194304 | tf_op jit(solution)/shard_map/surfaces_last/pallas_call | solution.py:378
  (32 shorter events, 0.2 us)
Async XLA Ops:
  2.5 10.1 %collective-permute-start.1 = (f32[1,136,128]{2,1,0:T(8,128)S(1)}, f32[1,136,128]{2,1,0:T(8,128)S(1)}, u32[]{:S(2)}, u32[]{:S(2)}) collective-permute-start(f32[1,136,128]{2,1,0:T(8,128)S(1)} %pad_bitcast_fusion), channel_id=1, source_target_pairs={{0,8},{1,9},{2,10},{3,11},{4,12},{5,13},{6,14},{7,15},{8,16},{9,17... | collective-permute-start | bytes 208904 | tf_op jit(solution)/shard_map/ppermute | solution.py:433
  5.6 7.3 %collective-permute-start.2 = (f32[1,136,128]{2,1,0:T(8,128)S(1)}, f32[1,136,128]{2,1,0:T(8,128)S(1)}, u32[]{:S(2)}, u32[]{:S(2)}) collective-permute-start(f32[1,136,128]{2,1,0:T(8,128)S(1)} %pad_bitcast_fusion), channel_id=1, source_target_pairs={{0,16},{1,17},{2,18},{3,19},{4,20},{5,21},{6,22},{7,23},{8,24},{9,... | collective-permute-start | bytes 208904 | tf_op jit(solution)/shard_map/ppermute | solution.py:433
  8.2 4.9 %collective-permute-start.3 = (f32[1,136,128]{2,1,0:T(8,128)S(1)}, f32[1,136,128]{2,1,0:T(8,128)S(1)}, u32[]{:S(2)}, u32[]{:S(2)}) collective-permute-start(f32[1,136,128]{2,1,0:T(8,128)S(1)} %pad_bitcast_fusion), channel_id=1, source_target_pairs={{0,24},{1,25},{2,26},{3,27},{4,28},{5,29},{6,30},{7,31},{8,0},{9,1... | collective-permute-start | bytes 208904 | tf_op jit(solution)/shard_map/ppermute | solution.py:433
  9.5 6.9 %collective-permute-start.5 = (f32[1,136,128]{2,1,0:T(8,128)S(1)}, f32[1,136,128]{2,1,0:T(8,128)S(1)}, u32[]{:S(2)}, u32[]{:S(2)}) collective-permute-start(f32[1,136,128]{2,1,0:T(8,128)S(1)} %pad_bitcast_fusion), channel_id=1, source_target_pairs={{0,1},{1,0},{2,3},{3,2},{4,5},{5,4},{6,7},{7,6},{8,9},{9,8},{10,11... | collective-permute-start | bytes 208904 | tf_op jit(solution)/shard_map/ppermute | solution.py:433
  11.0 10.3 %collective-permute-start = (f32[1,136,128]{2,1,0:T(8,128)S(1)}, f32[1,136,128]{2,1,0:T(8,128)S(1)}, u32[]{:S(2)}, u32[]{:S(2)}) collective-permute-start(f32[1,136,128]{2,1,0:T(8,128)S(1)} %pad_bitcast_fusion), channel_id=1, source_target_pairs={{0,4},{1,5},{2,6},{3,7},{4,0},{5,1},{6,2},{7,3},{8,12},{9,13},{10,... | collective-permute-start | bytes 208904 | tf_op jit(solution)/shard_map/ppermute | solution.py:433
  13.1 6.8 %collective-permute-start.6 = (f32[3,136,128]{2,1,0:T(8,128)S(1)}, f32[3,136,128]{2,1,0:T(8,128)S(1)}, u32[]{:S(2)}, u32[]{:S(2)}) collective-permute-start(f32[3,136,128]{2,1,0:T(8,128)S(1)} %constant_dynamic-update-slice_fusion), channel_id=1, source_target_pairs={{0,1},{1,0},{2,3},{3,2},{4,5},{5,4},{6,7},{7,6},{8,9},{9,8},{10,11... | collective-permute-start | bytes 626696 | tf_op jit(solution)/shard_map/ppermute | solution.py:433
  14.7 23.6 %collective-permute-start.10 = (f32[4,136,128]{2,1,0:T(8,128)S(1)}, f32[4,136,128]{2,1,0:T(8,128)S(1)}, u32[]{:S(2)}, u32[]{:S(2)}) collective-permute-start(f32[4,136,128]{2,1,0:T(8,128)S(1)} %pad_maximum_fusion.rest_0_), channel_id=1, source_target_pairs={{0,2},{1,3},{2,0},{3,1},{4,6},{5,7},{6,4},{7,5},{8,10},{9,11},{10,... | collective-permute-start | bytes 835592 | tf_op jit(solution)/shard_map/ppermute | solution.py:433
  14.8 19.3 %collective-permute-start.4 = (f32[3,136,128]{2,1,0:T(8,128)S(1)}, f32[3,136,128]{2,1,0:T(8,128)S(1)}, u32[]{:S(2)}, u32[]{:S(2)}) collective-permute-start(f32[3,136,128]{2,1,0:T(8,128)S(1)} %constant_dynamic-update-slice_fusion), channel_id=1, source_target_pairs={{0,4},{1,5},{2,6},{3,7},{4,0},{5,1},{6,2},{7,3},{8,12},{9,13},{10,... | collective-permute-start | bytes 626696 | tf_op jit(solution)/shard_map/ppermute | solution.py:433
  19.9 18.4 %collective-permute-start.11 = (f32[4,136,128]{2,1,0:T(8,128)S(1)}, f32[4,136,128]{2,1,0:T(8,128)S(1)}, u32[]{:S(2)}, u32[]{:S(2)}) collective-permute-start(f32[4,136,128]{2,1,0:T(8,128)S(1)} %constant_dynamic-update-slice_fusion.5.rest_1_), channel_id=1, source_target_pairs={{0,2},{1,3},{2,0},{3,1},{4,6},{5,7},{6,4},{7,5},{8,10},{9,11},{10,... | collective-permute-start | bytes 835592 | tf_op jit(solution)/shard_map/ppermute | solution.py:433
  20.0 17.2 %collective-permute-start.7 = (f32[4,136,128]{2,1,0:T(8,128)S(1)}, f32[4,136,128]{2,1,0:T(8,128)S(1)}, u32[]{:S(2)}, u32[]{:S(2)}) collective-permute-start(f32[4,136,128]{2,1,0:T(8,128)S(1)} %constant_dynamic-update-slice_fusion.5.rest_1_), channel_id=1, source_target_pairs={{0,4},{1,5},{2,6},{3,7},{4,0},{5,1},{6,2},{7,3},{8,12},{9,13},{10,... | collective-permute-start | bytes 835592 | tf_op jit(solution)/shard_map/ppermute | solution.py:433
  21.4 8.1 %collective-permute-start.12 = (f32[4,8,128]{2,1,0:T(8,128)S(1)}, f32[4,8,128]{2,1,0:T(8,128)S(1)}, u32[]{:S(2)}, u32[]{:S(2)}) collective-permute-start(f32[4,8,128]{2,1,0:T(8,128)S(1)} %pad_maximum_fusion.1), channel_id=1, source_target_pairs={{0,4},{1,5},{2,6},{3,7},{4,0},{5,1},{6,2},{7,3},{8,12},{9,13},{10,... | collective-permute-start | bytes 49160 | tf_op jit(solution)/shard_map/ppermute | solution.py:433
  22.2 16.1 %copy-start.5 = (s32[3,16,128]{2,1,0:T(8,128)S(1)}, s32[3,16,128]{2,1,0:T(8,128)}, u32[]{:S(2)}) copy-start(s32[3,16,128]{2,1,0:T(8,128)} %constant.507.clone.ticks_ref) | copy-start | bytes 73732
  22.2 16.1 %copy-start.6 = (f32[32,128]{1,0:T(8,128)S(1)}, f32[32,128]{1,0:T(8,128)}, u32[]{:S(2)}) copy-start(f32[32,128]{1,0:T(8,128)} %constant.508.clone.small_ref) | copy-start | bytes 49156
  22.2 16.1 %copy-start.4 = (s32[3,16,128]{2,1,0:T(8,128)S(1)}, s32[3,16,128]{2,1,0:T(8,128)}, u32[]{:S(2)}) copy-start(s32[3,16,128]{2,1,0:T(8,128)} %constant.506.clone.fixed_ref) | copy-start | bytes 73732
  22.2 16.2 %copy-start.3 = (bf16[2,256,256]{2,1,0:T(8,128)(2,1)S(1)}, bf16[2,256,256]{2,1,0:T(8,128)(2,1)}, u32[]{:S(2)}) copy-start(bf16[2,256,256]{2,1,0:T(8,128)(2,1)} %constant.512.clone.odd_l) | copy-start | bytes 786436
  22.3 16.0 %copy-start.2 = (bf16[2,256,256]{2,1,0:T(8,128)(2,1)S(1)}, bf16[2,256,256]{2,1,0:T(8,128)(2,1)}, u32[]{:S(2)}) copy-start(bf16[2,256,256]{2,1,0:T(8,128)(2,1)} %constant.511.clone.odd_h) | copy-start | bytes 786436
  22.5 15.8 %copy-start = (bf16[2,256,256]{2,1,0:T(8,128)(2,1)S(1)}, bf16[2,256,256]{2,1,0:T(8,128)(2,1)}, u32[]{:S(2)}) copy-start(bf16[2,256,256]{2,1,0:T(8,128)(2,1)} %constant.509.clone.even_h) | copy-start | bytes 786436
  22.5 15.8 %copy-start.1 = (bf16[2,256,256]{2,1,0:T(8,128)(2,1)S(1)}, bf16[2,256,256]{2,1,0:T(8,128)(2,1)}, u32[]{:S(2)}) copy-start(bf16[2,256,256]{2,1,0:T(8,128)(2,1)} %constant.510.clone.even_l) | copy-start | bytes 786436
  29.4 4.6 %collective-permute-start.13 = (f32[4,8,128]{2,1,0:T(8,128)S(1)}, f32[4,8,128]{2,1,0:T(8,128)S(1)}, u32[]{:S(2)}, u32[]{:S(2)}) collective-permute-start(f32[4,8,128]{2,1,0:T(8,128)S(1)} %pad_maximum_fusion.1), channel_id=1, source_target_pairs={{0,5},{1,4},{2,7},{3,6},{4,1},{5,0},{6,3},{7,2},{8,13},{9,12},{10,... | collective-permute-start | bytes 49160 | tf_op jit(solution)/shard_map/ppermute | solution.py:433
  34.1 3.2 %collective-permute-start.14 = (f32[4,8,128]{2,1,0:T(8,128)S(1)}, f32[4,8,128]{2,1,0:T(8,128)S(1)}, u32[]{:S(2)}, u32[]{:S(2)}) collective-permute-start(f32[4,8,128]{2,1,0:T(8,128)S(1)} %pad_maximum_fusion.1), channel_id=1, source_target_pairs={{0,6},{1,7},{2,4},{3,5},{4,2},{5,3},{6,0},{7,1},{8,14},{9,15},{10,... | collective-permute-start | bytes 49160 | tf_op jit(solution)/shard_map/ppermute | solution.py:433
  34.1 4.2 %collective-permute-start.15 = (f32[4,8,128]{2,1,0:T(8,128)S(1)}, f32[4,8,128]{2,1,0:T(8,128)S(1)}, u32[]{:S(2)}, u32[]{:S(2)}) collective-permute-start(f32[4,8,128]{2,1,0:T(8,128)S(1)} %pad_maximum_fusion.1), channel_id=1, source_target_pairs={{0,7},{1,6},{2,5},{3,4},{4,3},{5,2},{6,1},{7,0},{8,15},{9,14},{10,... | collective-permute-start | bytes 49160 | tf_op jit(solution)/shard_map/ppermute | solution.py:433
  37.2 8.8 %collective-permute-start.8 = (f32[4,136,128]{2,1,0:T(8,128)S(1)}, f32[4,136,128]{2,1,0:T(8,128)S(1)}, u32[]{:S(2)}, u32[]{:S(2)}) collective-permute-start(f32[4,136,128]{2,1,0:T(8,128)S(1)} %constant_dynamic-update-slice_fusion.3.rest_0_), channel_id=1, source_target_pairs={{0,2},{1,3},{2,0},{3,1},{4,6},{5,7},{6,4},{7,5},{8,10},{9,11},{10,... | collective-permute-start | bytes 835592 | tf_op jit(solution)/shard_map/ppermute | solution.py:433
  37.2 8.8 %collective-permute-start.9 = (f32[4,136,128]{2,1,0:T(8,128)S(1)}, f32[4,136,128]{2,1,0:T(8,128)S(1)}, u32[]{:S(2)}, u32[]{:S(2)}) collective-permute-start(f32[4,136,128]{2,1,0:T(8,128)S(1)} %collective-permute-done.7.rest_1_), channel_id=1, source_target_pairs={{0,2},{1,3},{2,0},{3,1},{4,6},{5,7},{6,4},{7,5},{8,10},{9,11},{10,... | collective-permute-start | bytes 835592 | tf_op jit(solution)/shard_map/ppermute | solution.py:433

commit v5 on v3

--- a/solution.py
+++ b/solution.py
@@ -326,7 +326,7 @@
             return carry
 
         channelize((block_at(0), block_at(1)), 0)
-        lax.fori_loop(0, count // 4 - 1, step, 0)
+        lax.fori_loop(0, count // 4 - 1, step, 0, unroll=count <= 16)
         work(count - 4, 0, True)
         work(count - 2, 1, False)
         if opening:
@@ -420,14 +420,19 @@
     line = [own]
     for step in range(1, outer):
         line.append(moved(own, (step, 0, 0, 0)))
+    own_near = [moved(own, (0, 0, 0, member)) for member in range(1, groups)]
+    own_far = moved(own, (0, 1, 0, 0))
+    rest = jnp.concatenate(line[1:], axis=0)
     line = jnp.concatenate(line, axis=0)
     tiles = jnp.concatenate([line[:, hops : hops + PAD - lead], line[:, hops - lead : hops]], axis=1)
     note_steps = [(1, core, member) for core in range(2) for member in range(groups)]
     notes = []
     for by in note_steps:
         notes.append(moved(tiles, (0,) + by))
-    near = [line] + [moved(line, (0, 0, 0, member)) for member in range(1, groups)]
-    far = [moved(line, (0, 1, 0, 0))]
+    near = [moved(rest, (0, 0, 0, member)) for member in range(1, groups)]
+    far = [moved(rest, (0, 1, 0, 0))]
+    near = [line] + [jnp.concatenate(pair, axis=0) for pair in zip(own_near, near)]
+    far = [jnp.concatenate([own_far, far[0]], axis=0)]
     far += [moved(piece, (0, 1, 0, 0)) for piece in near[1:]]
     near_steps = [(0, 0, member) for member in range(groups)]
     far_steps = [(1, 0, member) for member in range(groups)]

time: 59 us -> 54.4 us (0.922); the launches traced: 58.9 us -> 53.5 us
  waiting for transfers between devices: 23.2 us -> 14.6 us
  starting transfers between devices: 16.8 us -> 20.7 us
  Pallas kernels: 16.1 us -> 15.1 us
    ppermute x14 -> x16, waiting for transfers between devices: 23.2 us -> 14.6 us  [moved(): return lax.ppermute(array, axes, pairs)]
    ppermute x14 -> x16, starting transfers between devices: 16.8 us -> 20.7 us  [moved(): return lax.ppermute(array, axes, pairs)]
    pallas_call x2, Pallas kernels: 16.1 us -> 15.1 us  [surfaces(): pl.pallas_call(kernel, in_specs=[pl.BlockSpec(memory_space=pltpu.SMEM)] +...]
  transfers between devices with their start and end apart: 14 -> 16, of which waited for: 7 -> 7; matrix products, arithmetic and copies ran while one was open for 0% -> 1% of each run, Pallas kernels for 13% -> 13%
where the time goes in v5:
time: 54.4 us; the launch traced here: 53.5 us
  starting transfers between devices  20.7 us (38%)
  Pallas kernels  15.1 us (28%)
  waiting for transfers between devices  14.6 us (27%)
  between operations  1.62 us (3%)
  local copies, waits for them, and re-layouts  1.43 us (3%)
    ppermute x16, starting transfers between devices, moved(): return lax.ppermute(array, axes, pairs)  20.7 us
    pallas_call x2, Pallas kernels, surfaces(): pl.pallas_call(kernel, in_specs=[pl.BlockSpec(memory_space=pltpu.SMEM)] +...  15.1 us
    ppermute x16, waiting for transfers between devices, moved(): return lax.ppermute(array, axes, pairs)  14.6 us
  transfers between devices with their start and end apart: 16, of which 7 were waited for; matrix products, arithmetic and copies ran while one was open for 1% of the time, Pallas kernels for 13%

profile of v5, /device:TPU:0, one launch (start us, length us, event | category | flops | bytes accessed | tf_op | source)
XLA Modules:
  0.0 53.5 jit_solution(12852644418202000950)
XLA Ops:
  0.6 1.0 %reshape.11 = f32[2,128,64]{2,1,0:T(8,128)S(1)} reshape(f32[2,8192]{1,0:T(2,128)} %param.16) | data formatting | bytes 131072 | tf_op jit(solution)/shard_map/reshape | solution.py:399
  1.6 0.1 copy.19
  1.7 0.1 copy.20
  2.5 3.1 %collective-permute-start.1 = (f32[1,136,128]{2,1,0:T(8,128)S(1)}, f32[1,136,128]{2,1,0:T(8,128)S(1)}, u32[]{:S(2)}, u32[]{:S(2)}) collective-permute-start(f32[1,136,128]{2,1,0:T(8,128)S(1)} %pad_bitcast_fusion), channel_id=1, source_target_pairs={{0,8},{1,9},{2,10},{3,11},{4,12},{5,13},{6,14},{7,15},{8,16},{9,17... | collective-permute-start | bytes 208904 | tf_op jit(solution)/shard_map/ppermute | solution.py:418
  5.6 2.6 %collective-permute-start.2 = (f32[1,136,128]{2,1,0:T(8,128)S(1)}, f32[1,136,128]{2,1,0:T(8,128)S(1)}, u32[]{:S(2)}, u32[]{:S(2)}) collective-permute-start(f32[1,136,128]{2,1,0:T(8,128)S(1)} %pad_bitcast_fusion), channel_id=1, source_target_pairs={{0,16},{1,17},{2,18},{3,19},{4,20},{5,21},{6,22},{7,23},{8,24},{9,... | collective-permute-start | bytes 208904 | tf_op jit(solution)/shard_map/ppermute | solution.py:418
  8.2 1.3 %collective-permute-start.3 = (f32[1,136,128]{2,1,0:T(8,128)S(1)}, f32[1,136,128]{2,1,0:T(8,128)S(1)}, u32[]{:S(2)}, u32[]{:S(2)}) collective-permute-start(f32[1,136,128]{2,1,0:T(8,128)S(1)} %pad_bitcast_fusion), channel_id=1, source_target_pairs={{0,24},{1,25},{2,26},{3,27},{4,28},{5,29},{6,30},{7,31},{8,0},{9,1... | collective-permute-start | bytes 208904 | tf_op jit(solution)/shard_map/ppermute | solution.py:418
  9.5 1.5 %collective-permute-start.5 = (f32[1,136,128]{2,1,0:T(8,128)S(1)}, f32[1,136,128]{2,1,0:T(8,128)S(1)}, u32[]{:S(2)}, u32[]{:S(2)}) collective-permute-start(f32[1,136,128]{2,1,0:T(8,128)S(1)} %pad_bitcast_fusion), channel_id=1, source_target_pairs={{0,1},{1,0},{2,3},{3,2},{4,5},{5,4},{6,7},{7,6},{8,9},{9,8},{10,11... | collective-permute-start | bytes 208904 | tf_op jit(solution)/shard_map/ppermute | solution.py:418
  11.0 1.5 %collective-permute-start = (f32[1,136,128]{2,1,0:T(8,128)S(1)}, f32[1,136,128]{2,1,0:T(8,128)S(1)}, u32[]{:S(2)}, u32[]{:S(2)}) collective-permute-start(f32[1,136,128]{2,1,0:T(8,128)S(1)} %pad_bitcast_fusion), channel_id=1, source_target_pairs={{0,4},{1,5},{2,6},{3,7},{4,0},{5,1},{6,2},{7,3},{8,12},{9,13},{10,... | collective-permute-start | bytes 208904 | tf_op jit(solution)/shard_map/ppermute | solution.py:418
  12.5 0.3 collective-permute-done.2
  12.9 0.2 collective-permute-done.3
  13.1 1.6 %collective-permute-start.6 = (f32[3,136,128]{2,1,0:T(8,128)S(1)}, f32[3,136,128]{2,1,0:T(8,128)S(1)}, u32[]{:S(2)}, u32[]{:S(2)}) collective-permute-start(f32[3,136,128]{2,1,0:T(8,128)S(1)} %constant_dynamic-update-slice_fusion), channel_id=1, source_target_pairs={{0,1},{1,0},{2,3},{3,2},{4,5},{5,4},{6,7},{7,6},{8,9},{9,8},{10,11... | collective-permute-start | bytes 626696 | tf_op jit(solution)/shard_map/ppermute | solution.py:418
  14.7 0.1 collective-permute-start.10
  14.8 1.6 %collective-permute-start.4 = (f32[3,136,128]{2,1,0:T(8,128)S(1)}, f32[3,136,128]{2,1,0:T(8,128)S(1)}, u32[]{:S(2)}, u32[]{:S(2)}) collective-permute-start(f32[3,136,128]{2,1,0:T(8,128)S(1)} %constant_dynamic-update-slice_fusion), channel_id=1, source_target_pairs={{0,4},{1,5},{2,6},{3,7},{4,0},{5,1},{6,2},{7,3},{8,12},{9,13},{10,... | collective-permute-start | bytes 626696 | tf_op jit(solution)/shard_map/ppermute | solution.py:418
  16.4 0.0 collective-permute-done.5
  16.4 3.5 %collective-permute-done.6 = f32[3,136,128]{2,1,0:T(8,128)S(1)} collective-permute-done((f32[3,136,128]{2,1,0:T(8,128)S(1)}, f32[3,136,128]{2,1,0:T(8,128)S(1)}, u32[]{:S(2)}, u32[]{:S(2)}) %collective-permute-start.6) | collective-permute-done | bytes 208928 | tf_op jit(solution)/shard_map/ppermute | solution.py:418
  19.9 0.1 collective-permute-start.11
  20.0 1.3 %collective-permute-start.7 = (f32[4,136,128]{2,1,0:T(8,128)S(1)}, f32[4,136,128]{2,1,0:T(8,128)S(1)}, u32[]{:S(2)}, u32[]{:S(2)}) collective-permute-start(f32[4,136,128]{2,1,0:T(8,128)S(1)} %constant_dynamic-update-slice_fusion.5.rest_1_), channel_id=1, source_target_pairs={{0,4},{1,5},{2,6},{3,7},{4,0},{5,1},{6,2},{7,3},{8,12},{9,13},{10,... | collective-permute-start | bytes 835592 | tf_op jit(solution)/shard_map/ppermute | solution.py:418
  21.4 0.0 collective-permute-done
  21.4 0.8 %collective-permute-start.12 = (f32[4,8,128]{2,1,0:T(8,128)S(1)}, f32[4,8,128]{2,1,0:T(8,128)S(1)}, u32[]{:S(2)}, u32[]{:S(2)}) collective-permute-start(f32[4,8,128]{2,1,0:T(8,128)S(1)} %pad_maximum_fusion.1), channel_id=1, source_target_pairs={{0,4},{1,5},{2,6},{3,7},{4,0},{5,1},{6,2},{7,3},{8,12},{9,13},{10,... | collective-permute-start | bytes 49160 | tf_op jit(solution)/shard_map/ppermute | solution.py:418
  22.3 0.0 copy-start.2
  22.4 0.2 stack.287.plan_ref
  22.5 0.0 copy-start
  22.5 0.0 copy-start.1
  22.6 6.9 %collective-permute-done.12.rest_4_ = f32[4,8,128]{2,1,0:T(8,128)S(1)} collective-permute-done((f32[4,8,128]{2,1,0:T(8,128)S(1)}, f32[4,8,128]{2,1,0:T(8,128)S(1)}, u32[]{:S(2)}, u32[]{:S(2)}) %collective-permute-start.12) | collective-permute-done | bytes 16416 | tf_op jit(solution)/shard_map/ppermute | solution.py:418
  29.4 2.2 %collective-permute-start.13 = (f32[4,8,128]{2,1,0:T(8,128)S(1)}, f32[4,8,128]{2,1,0:T(8,128)S(1)}, u32[]{:S(2)}, u32[]{:S(2)}) collective-permute-start(f32[4,8,128]{2,1,0:T(8,128)S(1)} %pad_maximum_fusion.1), channel_id=1, source_target_pairs={{0,5},{1,4},{2,7},{3,6},{4,1},{5,0},{6,3},{7,2},{8,13},{9,12},{10,... | collective-permute-start | bytes 49160 | tf_op jit(solution)/shard_map/ppermute | solution.py:418
  31.7 2.4 %collective-permute-done.13.rest_5_ = f32[4,8,128]{2,1,0:T(8,128)S(1)} collective-permute-done((f32[4,8,128]{2,1,0:T(8,128)S(1)}, f32[4,8,128]{2,1,0:T(8,128)S(1)}, u32[]{:S(2)}, u32[]{:S(2)}) %collective-permute-start.13) | collective-permute-done | bytes 16416 | tf_op jit(solution)/shard_map/ppermute | solution.py:418
  34.1 2.5 %collective-permute-start.15 = (f32[4,8,128]{2,1,0:T(8,128)S(1)}, f32[4,8,128]{2,1,0:T(8,128)S(1)}, u32[]{:S(2)}, u32[]{:S(2)}) collective-permute-start(f32[4,8,128]{2,1,0:T(8,128)S(1)} %pad_maximum_fusion.1), channel_id=1, source_target_pairs={{0,7},{1,6},{2,5},{3,4},{4,3},{5,2},{6,1},{7,0},{8,15},{9,14},{10,... | collective-permute-start | bytes 49160 | tf_op jit(solution)/shard_map/ppermute | solution.py:418
  36.6 0.7 %collective-permute-done.14.rest_6_ = f32[4,8,128]{2,1,0:T(8,128)S(1)} collective-permute-done((f32[4,8,128]{2,1,0:T(8,128)S(1)}, f32[4,8,128]{2,1,0:T(8,128)S(1)}, u32[]{:S(2)}, u32[]{:S(2)}) %collective-permute-start.14) | collective-permute-done | bytes 16416 | tf_op jit(solution)/shard_map/ppermute | solution.py:418
  37.2 0.5 collective-permute-start.9
  37.8 0.6 %collective-permute-done.15.rest_7_ = f32[4,8,128]{2,1,0:T(8,128)S(1)} collective-permute-done((f32[4,8,128]{2,1,0:T(8,128)S(1)}, f32[4,8,128]{2,1,0:T(8,128)S(1)}, u32[]{:S(2)}, u32[]{:S(2)}) %collective-permute-start.15) | collective-permute-done | bytes 16416 | tf_op jit(solution)/shard_map/ppermute | solution.py:418
  38.4 7.1 %surfaces_first.1 = (f32[512,128]{1,0:T(8,128)S(1)}, f32[512,128]{1,0:T(8,128)S(1)}, f32[512,128]{1,0:T(8,128)S(1)}, s32[128,128]{1,0:T(8,128)S(1)}, f32[4,8,128]{2,1,0:T(8,128)S(1)}) custom-call(s32[86]{0:T(128)S(1)} %stack.287.plan_ref, s32[3,16,128]{2,1,0:T(8,128)S(1)} %copy-done.4, s32[3,16,128]{2,1,0:T(8,128)S(1)} %copy-done.5, ...), custom_call_target="tpu_custom_call" | custom-call | flops 4831838208 | bytes 4194304 | tf_op jit(solution)/shard_map/surfaces_first/pallas_call | solution.py:364
  45.5 8.0 %surfaces_last.1 = (f32[8,64,128]{2,1,0:T(8,128)}, f32[2,8,64,128]{3,2,1,0:T(8,128)}) custom-call(s32[86]{0:T(128)S(1)} %stack.287.plan_ref, s32[3,16,128]{2,1,0:T(8,128)S(1)} %copy-done.4, s32[3,16,128]{2,1,0:T(8,128)S(1)} %copy-done.5, f32[32,128]{1,0:T(8,128)S(1)} %copy-done.6, bf16[2,256,256]{2,1,0:T(8,128)(2,1)S(1)} %copy-done, ...), custom_call_target="tpu_custom_call" | custom-call | flops 4831838208 | bytes 4194304 | tf_op jit(solution)/shard_map/surfaces_last/pallas_call | solution.py:364
  (32 shorter events, 0.2 us)
Async XLA Ops:
  2.5 10.1 %collective-permute-start.1 = (f32[1,136,128]{2,1,0:T(8,128)S(1)}, f32[1,136,128]{2,1,0:T(8,128)S(1)}, u32[]{:S(2)}, u32[]{:S(2)}) collective-permute-start(f32[1,136,128]{2,1,0:T(8,128)S(1)} %pad_bitcast_fusion), channel_id=1, source_target_pairs={{0,8},{1,9},{2,10},{3,11},{4,12},{5,13},{6,14},{7,15},{8,16},{9,17... | collective-permute-start | bytes 208904 | tf_op jit(solution)/shard_map/ppermute | solution.py:418
  5.6 7.3 %collective-permute-start.2 = (f32[1,136,128]{2,1,0:T(8,128)S(1)}, f32[1,136,128]{2,1,0:T(8,128)S(1)}, u32[]{:S(2)}, u32[]{:S(2)}) collective-permute-start(f32[1,136,128]{2,1,0:T(8,128)S(1)} %pad_bitcast_fusion), channel_id=1, source_target_pairs={{0,16},{1,17},{2,18},{3,19},{4,20},{5,21},{6,22},{7,23},{8,24},{9,... | collective-permute-start | bytes 208904 | tf_op jit(solution)/shard_map/ppermute | solution.py:418
  8.2 4.9 %collective-permute-start.3 = (f32[1,136,128]{2,1,0:T(8,128)S(1)}, f32[1,136,128]{2,1,0:T(8,128)S(1)}, u32[]{:S(2)}, u32[]{:S(2)}) collective-permute-start(f32[1,136,128]{2,1,0:T(8,128)S(1)} %pad_bitcast_fusion), channel_id=1, source_target_pairs={{0,24},{1,25},{2,26},{3,27},{4,28},{5,29},{6,30},{7,31},{8,0},{9,1... | collective-permute-start | bytes 208904 | tf_op jit(solution)/shard_map/ppermute | solution.py:418
  9.5 6.9 %collective-permute-start.5 = (f32[1,136,128]{2,1,0:T(8,128)S(1)}, f32[1,136,128]{2,1,0:T(8,128)S(1)}, u32[]{:S(2)}, u32[]{:S(2)}) collective-permute-start(f32[1,136,128]{2,1,0:T(8,128)S(1)} %pad_bitcast_fusion), channel_id=1, source_target_pairs={{0,1},{1,0},{2,3},{3,2},{4,5},{5,4},{6,7},{7,6},{8,9},{9,8},{10,11... | collective-permute-start | bytes 208904 | tf_op jit(solution)/shard_map/ppermute | solution.py:418
  11.0 10.3 %collective-permute-start = (f32[1,136,128]{2,1,0:T(8,128)S(1)}, f32[1,136,128]{2,1,0:T(8,128)S(1)}, u32[]{:S(2)}, u32[]{:S(2)}) collective-permute-start(f32[1,136,128]{2,1,0:T(8,128)S(1)} %pad_bitcast_fusion), channel_id=1, source_target_pairs={{0,4},{1,5},{2,6},{3,7},{4,0},{5,1},{6,2},{7,3},{8,12},{9,13},{10,... | collective-permute-start | bytes 208904 | tf_op jit(solution)/shard_map/ppermute | solution.py:418
  13.1 6.8 %collective-permute-start.6 = (f32[3,136,128]{2,1,0:T(8,128)S(1)}, f32[3,136,128]{2,1,0:T(8,128)S(1)}, u32[]{:S(2)}, u32[]{:S(2)}) collective-permute-start(f32[3,136,128]{2,1,0:T(8,128)S(1)} %constant_dynamic-update-slice_fusion), channel_id=1, source_target_pairs={{0,1},{1,0},{2,3},{3,2},{4,5},{5,4},{6,7},{7,6},{8,9},{9,8},{10,11... | collective-permute-start | bytes 626696 | tf_op jit(solution)/shard_map/ppermute | solution.py:418
  14.7 23.6 %collective-permute-start.10 = (f32[4,136,128]{2,1,0:T(8,128)S(1)}, f32[4,136,128]{2,1,0:T(8,128)S(1)}, u32[]{:S(2)}, u32[]{:S(2)}) collective-permute-start(f32[4,136,128]{2,1,0:T(8,128)S(1)} %pad_maximum_fusion.rest_0_), channel_id=1, source_target_pairs={{0,2},{1,3},{2,0},{3,1},{4,6},{5,7},{6,4},{7,5},{8,10},{9,11},{10,... | collective-permute-start | bytes 835592 | tf_op jit(solution)/shard_map/ppermute | solution.py:418
  14.8 19.3 %collective-permute-start.4 = (f32[3,136,128]{2,1,0:T(8,128)S(1)}, f32[3,136,128]{2,1,0:T(8,128)S(1)}, u32[]{:S(2)}, u32[]{:S(2)}) collective-permute-start(f32[3,136,128]{2,1,0:T(8,128)S(1)} %constant_dynamic-update-slice_fusion), channel_id=1, source_target_pairs={{0,4},{1,5},{2,6},{3,7},{4,0},{5,1},{6,2},{7,3},{8,12},{9,13},{10,... | collective-permute-start | bytes 626696 | tf_op jit(solution)/shard_map/ppermute | solution.py:418
  19.9 18.4 %collective-permute-start.11 = (f32[4,136,128]{2,1,0:T(8,128)S(1)}, f32[4,136,128]{2,1,0:T(8,128)S(1)}, u32[]{:S(2)}, u32[]{:S(2)}) collective-permute-start(f32[4,136,128]{2,1,0:T(8,128)S(1)} %constant_dynamic-update-slice_fusion.5.rest_1_), channel_id=1, source_target_pairs={{0,2},{1,3},{2,0},{3,1},{4,6},{5,7},{6,4},{7,5},{8,10},{9,11},{10,... | collective-permute-start | bytes 835592 | tf_op jit(solution)/shard_map/ppermute | solution.py:418
  20.0 17.2 %collective-permute-start.7 = (f32[4,136,128]{2,1,0:T(8,128)S(1)}, f32[4,136,128]{2,1,0:T(8,128)S(1)}, u32[]{:S(2)}, u32[]{:S(2)}) collective-permute-start(f32[4,136,128]{2,1,0:T(8,128)S(1)} %constant_dynamic-update-slice_fusion.5.rest_1_), channel_id=1, source_target_pairs={{0,4},{1,5},{2,6},{3,7},{4,0},{5,1},{6,2},{7,3},{8,12},{9,13},{10,... | collective-permute-start | bytes 835592 | tf_op jit(solution)/shard_map/ppermute | solution.py:418
  21.4 8.1 %collective-permute-start.12 = (f32[4,8,128]{2,1,0:T(8,128)S(1)}, f32[4,8,128]{2,1,0:T(8,128)S(1)}, u32[]{:S(2)}, u32[]{:S(2)}) collective-permute-start(f32[4,8,128]{2,1,0:T(8,128)S(1)} %pad_maximum_fusion.1), channel_id=1, source_target_pairs={{0,4},{1,5},{2,6},{3,7},{4,0},{5,1},{6,2},{7,3},{8,12},{9,13},{10,... | collective-permute-start | bytes 49160 | tf_op jit(solution)/shard_map/ppermute | solution.py:418
  22.2 16.1 %copy-start.5 = (s32[3,16,128]{2,1,0:T(8,128)S(1)}, s32[3,16,128]{2,1,0:T(8,128)}, u32[]{:S(2)}) copy-start(s32[3,16,128]{2,1,0:T(8,128)} %constant.507.clone.ticks_ref) | copy-start | bytes 73732
  22.2 16.1 %copy-start.6 = (f32[32,128]{1,0:T(8,128)S(1)}, f32[32,128]{1,0:T(8,128)}, u32[]{:S(2)}) copy-start(f32[32,128]{1,0:T(8,128)} %constant.508.clone.small_ref) | copy-start | bytes 49156
  22.2 16.1 %copy-start.4 = (s32[3,16,128]{2,1,0:T(8,128)S(1)}, s32[3,16,128]{2,1,0:T(8,128)}, u32[]{:S(2)}) copy-start(s32[3,16,128]{2,1,0:T(8,128)} %constant.506.clone.fixed_ref) | copy-start | bytes 73732
  22.2 16.2 %copy-start.3 = (bf16[2,256,256]{2,1,0:T(8,128)(2,1)S(1)}, bf16[2,256,256]{2,1,0:T(8,128)(2,1)}, u32[]{:S(2)}) copy-start(bf16[2,256,256]{2,1,0:T(8,128)(2,1)} %constant.512.clone.odd_l) | copy-start | bytes 786436
  22.3 16.0 %copy-start.2 = (bf16[2,256,256]{2,1,0:T(8,128)(2,1)S(1)}, bf16[2,256,256]{2,1,0:T(8,128)(2,1)}, u32[]{:S(2)}) copy-start(bf16[2,256,256]{2,1,0:T(8,128)(2,1)} %constant.511.clone.odd_h) | copy-start | bytes 786436
  22.5 15.8 %copy-start = (bf16[2,256,256]{2,1,0:T(8,128)(2,1)S(1)}, bf16[2,256,256]{2,1,0:T(8,128)(2,1)}, u32[]{:S(2)}) copy-start(bf16[2,256,256]{2,1,0:T(8,128)(2,1)} %constant.509.clone.even_h) | copy-start | bytes 786436
  22.5 15.8 %copy-start.1 = (bf16[2,256,256]{2,1,0:T(8,128)(2,1)S(1)}, bf16[2,256,256]{2,1,0:T(8,128)(2,1)}, u32[]{:S(2)}) copy-start(bf16[2,256,256]{2,1,0:T(8,128)(2,1)} %constant.510.clone.even_l) | copy-start | bytes 786436
  29.4 4.6 %collective-permute-start.13 = (f32[4,8,128]{2,1,0:T(8,128)S(1)}, f32[4,8,128]{2,1,0:T(8,128)S(1)}, u32[]{:S(2)}, u32[]{:S(2)}) collective-permute-start(f32[4,8,128]{2,1,0:T(8,128)S(1)} %pad_maximum_fusion.1), channel_id=1, source_target_pairs={{0,5},{1,4},{2,7},{3,6},{4,1},{5,0},{6,3},{7,2},{8,13},{9,12},{10,... | collective-permute-start | bytes 49160 | tf_op jit(solution)/shard_map/ppermute | solution.py:418
  34.1 3.2 %collective-permute-start.14 = (f32[4,8,128]{2,1,0:T(8,128)S(1)}, f32[4,8,128]{2,1,0:T(8,128)S(1)}, u32[]{:S(2)}, u32[]{:S(2)}) collective-permute-start(f32[4,8,128]{2,1,0:T(8,128)S(1)} %pad_maximum_fusion.1), channel_id=1, source_target_pairs={{0,6},{1,7},{2,4},{3,5},{4,2},{5,3},{6,0},{7,1},{8,14},{9,15},{10,... | collective-permute-start | bytes 49160 | tf_op jit(solution)/shard_map/ppermute | solution.py:418
  34.1 4.2 %collective-permute-start.15 = (f32[4,8,128]{2,1,0:T(8,128)S(1)}, f32[4,8,128]{2,1,0:T(8,128)S(1)}, u32[]{:S(2)}, u32[]{:S(2)}) collective-permute-start(f32[4,8,128]{2,1,0:T(8,128)S(1)} %pad_maximum_fusion.1), channel_id=1, source_target_pairs={{0,7},{1,6},{2,5},{3,4},{4,3},{5,2},{6,1},{7,0},{8,15},{9,14},{10,... | collective-permute-start | bytes 49160 | tf_op jit(solution)/shard_map/ppermute | solution.py:418
  37.2 8.3 %collective-permute-start.8 = (f32[4,136,128]{2,1,0:T(8,128)S(1)}, f32[4,136,128]{2,1,0:T(8,128)S(1)}, u32[]{:S(2)}, u32[]{:S(2)}) collective-permute-start(f32[4,136,128]{2,1,0:T(8,128)S(1)} %constant_dynamic-update-slice_fusion.3.rest_0_), channel_id=1, source_target_pairs={{0,2},{1,3},{2,0},{3,1},{4,6},{5,7},{6,4},{7,5},{8,10},{9,11},{10,... | collective-permute-start | bytes 835592 | tf_op jit(solution)/shard_map/ppermute | solution.py:418
  37.2 8.3 %collective-permute-start.9 = (f32[4,136,128]{2,1,0:T(8,128)S(1)}, f32[4,136,128]{2,1,0:T(8,128)S(1)}, u32[]{:S(2)}, u32[]{:S(2)}) collective-permute-start(f32[4,136,128]{2,1,0:T(8,128)S(1)} %collective-permute-done.7.rest_1_), channel_id=1, source_target_pairs={{0,2},{1,3},{2,0},{3,1},{4,6},{5,7},{6,4},{7,5},{8,10},{9,11},{10,... | collective-permute-start | bytes 835592 | tf_op jit(solution)/shard_map/ppermute | solution.py:418

commit v6 on v5

--- a/solution.py
+++ b/solution.py
@@ -213,12 +213,14 @@
             start = jnp.zeros((PAD, LANES), jnp.int32)
             lax.fori_loop(0, slabs, stamp_step, start, unroll=min(slabs, 16))
 
+        flat = count <= 16
         if opening:
-            acc_re[...] = jnp.zeros_like(acc_re)
-            acc_im[...] = jnp.zeros_like(acc_im)
-            acc_sq[...] = jnp.zeros_like(acc_sq)
+            if not flat:
+                acc_re[...] = jnp.zeros_like(acc_re)
+                acc_im[...] = jnp.zeros_like(acc_im)
+                acc_sq[...] = jnp.zeros_like(acc_sq)
             make_stamps()
-        else:
+        elif not flat:
             acc_re[...] = old_re[...]
             acc_im[...] = old_im[...]
             acc_sq[...] = old_sq[...]
@@ -282,7 +284,7 @@
                 center_re[at] = low_re[at] * c + low_im[at] * s
                 center_im[at] = low_im[at] * c - low_re[at] * s
 
-        def correlate(turn, slot):
+        def correlate(turn, slot, fresh):
             rhs_h, rhs_l, center_re, center_im = slot
             cos_rows = turn[0][...]
             sin_rows = turn[1][...]
@@ -307,18 +309,23 @@
                     put = slice(at, at + width)
                     re = total[index * width : (index + 1) * width, :LW]
                     im = total[index * width : (index + 1) * width, LW:]
-                    acc_re[put] = acc_re[put] + re
-                    acc_im[put] = acc_im[put] + im
-                    acc_sq[put] = jnp.maximum(acc_sq[put], re * re + im * im)
+                    square = re * re + im * im
+                    if fresh and opening:
+                        acc_re[put], acc_im[put], acc_sq[put] = re, im, square
+                        continue
+                    held = (old_re, old_im, old_sq) if fresh else (acc_re, acc_im, acc_sq)
+                    acc_re[put] = held[0][put] + re
+                    acc_im[put] = held[1][put] + im
+                    acc_sq[put] = jnp.maximum(held[2][put], square)
 
         def block_at(index):
             return plan_ref[first_block + index]
 
-        def work(first, side, more):
+        def work(first, side, more, start=False):
             if more:
                 channelize((block_at(first + 2), block_at(first + 3)), 1 - side)
             for item in range(2):
-                correlate(turns[side], slots[side][item])
+                correlate(turns[side], slots[side][item], start and item == 0)
 
         def step(index, carry):
             work(4 * index, 0, True)
@@ -326,8 +333,12 @@
             return carry
 
         channelize((block_at(0), block_at(1)), 0)
-        lax.fori_loop(0, count // 4 - 1, step, 0, unroll=count <= 16)
-        work(count - 4, 0, True)
+        if flat:
+            for first in range(0, count - 4, 2):
+                work(first, first // 2 % 2, True, start=first == 0)
+        else:
+            lax.fori_loop(0, count // 4 - 1, step, 0)
+        work(count - 4, 0, True, start=flat and count == 4)
         work(count - 2, 1, False)
         if opening:
             return

time: 54.4 us -> 54.4 us (level)
  no operation moved by 1% of the time
where the time goes in v6:
time: 54.4 us; the launch traced here: 53.5 us
  starting transfers between devices  20.7 us (38%)
  Pallas kernels  15.1 us (28%)
  waiting for transfers between devices  14.6 us (27%)
  between operations  1.62 us (3%)
  local copies, waits for them, and re-layouts  1.43 us (3%)
    ppermute x16, starting transfers between devices, moved(): return lax.ppermute(array, axes, pairs)  20.7 us
    pallas_call x2, Pallas kernels, surfaces(): pl.pallas_call(kernel, in_specs=[pl.BlockSpec(memory_space=pltpu.SMEM)] +...  15.1 us
    ppermute x16, waiting for transfers between devices, moved(): return lax.ppermute(array, axes, pairs)  14.6 us
  transfers between devices with their start and end apart: 16, of which 7 were waited for; matrix products, arithmetic and copies ran while one was open for 1% of the time, Pallas kernels for 13%

profile of v6, /device:TPU:0, one launch (start us, length us, event | category | flops | bytes accessed | tf_op | source)
XLA Modules:
  0.0 53.5 jit_solution(18139601777859689058)
XLA Ops:
  0.6 1.0 %reshape.11 = f32[2,128,64]{2,1,0:T(8,128)S(1)} reshape(f32[2,8192]{1,0:T(2,128)} %param.16) | data formatting | bytes 131072 | tf_op jit(solution)/shard_map/reshape | solution.py:410
  1.6 0.1 copy.19
  1.7 0.1 copy.20
  2.5 3.1 %collective-permute-start.1 = (f32[1,136,128]{2,1,0:T(8,128)S(1)}, f32[1,136,128]{2,1,0:T(8,128)S(1)}, u32[]{:S(2)}, u32[]{:S(2)}) collective-permute-start(f32[1,136,128]{2,1,0:T(8,128)S(1)} %pad_bitcast_fusion), channel_id=1, source_target_pairs={{0,8},{1,9},{2,10},{3,11},{4,12},{5,13},{6,14},{7,15},{8,16},{9,17... | collective-permute-start | bytes 208904 | tf_op jit(solution)/shard_map/ppermute | solution.py:429
  5.6 2.6 %collective-permute-start.2 = (f32[1,136,128]{2,1,0:T(8,128)S(1)}, f32[1,136,128]{2,1,0:T(8,128)S(1)}, u32[]{:S(2)}, u32[]{:S(2)}) collective-permute-start(f32[1,136,128]{2,1,0:T(8,128)S(1)} %pad_bitcast_fusion), channel_id=1, source_target_pairs={{0,16},{1,17},{2,18},{3,19},{4,20},{5,21},{6,22},{7,23},{8,24},{9,... | collective-permute-start | bytes 208904 | tf_op jit(solution)/shard_map/ppermute | solution.py:429
  8.2 1.3 %collective-permute-start.3 = (f32[1,136,128]{2,1,0:T(8,128)S(1)}, f32[1,136,128]{2,1,0:T(8,128)S(1)}, u32[]{:S(2)}, u32[]{:S(2)}) collective-permute-start(f32[1,136,128]{2,1,0:T(8,128)S(1)} %pad_bitcast_fusion), channel_id=1, source_target_pairs={{0,24},{1,25},{2,26},{3,27},{4,28},{5,29},{6,30},{7,31},{8,0},{9,1... | collective-permute-start | bytes 208904 | tf_op jit(solution)/shard_map/ppermute | solution.py:429
  9.5 1.5 %collective-permute-start.5 = (f32[1,136,128]{2,1,0:T(8,128)S(1)}, f32[1,136,128]{2,1,0:T(8,128)S(1)}, u32[]{:S(2)}, u32[]{:S(2)}) collective-permute-start(f32[1,136,128]{2,1,0:T(8,128)S(1)} %pad_bitcast_fusion), channel_id=1, source_target_pairs={{0,1},{1,0},{2,3},{3,2},{4,5},{5,4},{6,7},{7,6},{8,9},{9,8},{10,11... | collective-permute-start | bytes 208904 | tf_op jit(solution)/shard_map/ppermute | solution.py:429
  11.0 1.5 %collective-permute-start = (f32[1,136,128]{2,1,0:T(8,128)S(1)}, f32[1,136,128]{2,1,0:T(8,128)S(1)}, u32[]{:S(2)}, u32[]{:S(2)}) collective-permute-start(f32[1,136,128]{2,1,0:T(8,128)S(1)} %pad_bitcast_fusion), channel_id=1, source_target_pairs={{0,4},{1,5},{2,6},{3,7},{4,0},{5,1},{6,2},{7,3},{8,12},{9,13},{10,... | collective-permute-start | bytes 208904 | tf_op jit(solution)/shard_map/ppermute | solution.py:429
  12.5 0.3 collective-permute-done.2
  12.9 0.2 collective-permute-done.3
  13.1 1.6 %collective-permute-start.6 = (f32[3,136,128]{2,1,0:T(8,128)S(1)}, f32[3,136,128]{2,1,0:T(8,128)S(1)}, u32[]{:S(2)}, u32[]{:S(2)}) collective-permute-start(f32[3,136,128]{2,1,0:T(8,128)S(1)} %constant_dynamic-update-slice_fusion), channel_id=1, source_target_pairs={{0,1},{1,0},{2,3},{3,2},{4,5},{5,4},{6,7},{7,6},{8,9},{9,8},{10,11... | collective-permute-start | bytes 626696 | tf_op jit(solution)/shard_map/ppermute | solution.py:429
  14.7 0.1 collective-permute-start.10
  14.8 1.6 %collective-permute-start.4 = (f32[3,136,128]{2,1,0:T(8,128)S(1)}, f32[3,136,128]{2,1,0:T(8,128)S(1)}, u32[]{:S(2)}, u32[]{:S(2)}) collective-permute-start(f32[3,136,128]{2,1,0:T(8,128)S(1)} %constant_dynamic-update-slice_fusion), channel_id=1, source_target_pairs={{0,4},{1,5},{2,6},{3,7},{4,0},{5,1},{6,2},{7,3},{8,12},{9,13},{10,... | collective-permute-start | bytes 626696 | tf_op jit(solution)/shard_map/ppermute | solution.py:429
  16.4 0.0 collective-permute-done.5
  16.4 3.5 %collective-permute-done.6 = f32[3,136,128]{2,1,0:T(8,128)S(1)} collective-permute-done((f32[3,136,128]{2,1,0:T(8,128)S(1)}, f32[3,136,128]{2,1,0:T(8,128)S(1)}, u32[]{:S(2)}, u32[]{:S(2)}) %collective-permute-start.6) | collective-permute-done | bytes 208928 | tf_op jit(solution)/shard_map/ppermute | solution.py:429
  19.9 0.1 collective-permute-start.11
  20.0 1.3 %collective-permute-start.7 = (f32[4,136,128]{2,1,0:T(8,128)S(1)}, f32[4,136,128]{2,1,0:T(8,128)S(1)}, u32[]{:S(2)}, u32[]{:S(2)}) collective-permute-start(f32[4,136,128]{2,1,0:T(8,128)S(1)} %constant_dynamic-update-slice_fusion.5.rest_1_), channel_id=1, source_target_pairs={{0,4},{1,5},{2,6},{3,7},{4,0},{5,1},{6,2},{7,3},{8,12},{9,13},{10,... | collective-permute-start | bytes 835592 | tf_op jit(solution)/shard_map/ppermute | solution.py:429
  21.4 0.0 collective-permute-done
  21.4 0.8 %collective-permute-start.12 = (f32[4,8,128]{2,1,0:T(8,128)S(1)}, f32[4,8,128]{2,1,0:T(8,128)S(1)}, u32[]{:S(2)}, u32[]{:S(2)}) collective-permute-start(f32[4,8,128]{2,1,0:T(8,128)S(1)} %pad_maximum_fusion.1), channel_id=1, source_target_pairs={{0,4},{1,5},{2,6},{3,7},{4,0},{5,1},{6,2},{7,3},{8,12},{9,13},{10,... | collective-permute-start | bytes 49160 | tf_op jit(solution)/shard_map/ppermute | solution.py:429
  22.3 0.0 copy-start.2
  22.4 0.2 stack.287.plan_ref
  22.5 0.0 copy-start
  22.5 0.0 copy-start.1
  22.6 6.9 %collective-permute-done.12.rest_4_ = f32[4,8,128]{2,1,0:T(8,128)S(1)} collective-permute-done((f32[4,8,128]{2,1,0:T(8,128)S(1)}, f32[4,8,128]{2,1,0:T(8,128)S(1)}, u32[]{:S(2)}, u32[]{:S(2)}) %collective-permute-start.12) | collective-permute-done | bytes 16416 | tf_op jit(solution)/shard_map/ppermute | solution.py:429
  29.4 2.2 %collective-permute-start.13 = (f32[4,8,128]{2,1,0:T(8,128)S(1)}, f32[4,8,128]{2,1,0:T(8,128)S(1)}, u32[]{:S(2)}, u32[]{:S(2)}) collective-permute-start(f32[4,8,128]{2,1,0:T(8,128)S(1)} %pad_maximum_fusion.1), channel_id=1, source_target_pairs={{0,5},{1,4},{2,7},{3,6},{4,1},{5,0},{6,3},{7,2},{8,13},{9,12},{10,... | collective-permute-start | bytes 49160 | tf_op jit(solution)/shard_map/ppermute | solution.py:429
  31.7 2.4 %collective-permute-done.13.rest_5_ = f32[4,8,128]{2,1,0:T(8,128)S(1)} collective-permute-done((f32[4,8,128]{2,1,0:T(8,128)S(1)}, f32[4,8,128]{2,1,0:T(8,128)S(1)}, u32[]{:S(2)}, u32[]{:S(2)}) %collective-permute-start.13) | collective-permute-done | bytes 16416 | tf_op jit(solution)/shard_map/ppermute | solution.py:429
  34.1 2.5 %collective-permute-start.15 = (f32[4,8,128]{2,1,0:T(8,128)S(1)}, f32[4,8,128]{2,1,0:T(8,128)S(1)}, u32[]{:S(2)}, u32[]{:S(2)}) collective-permute-start(f32[4,8,128]{2,1,0:T(8,128)S(1)} %pad_maximum_fusion.1), channel_id=1, source_target_pairs={{0,7},{1,6},{2,5},{3,4},{4,3},{5,2},{6,1},{7,0},{8,15},{9,14},{10,... | collective-permute-start | bytes 49160 | tf_op jit(solution)/shard_map/ppermute | solution.py:429
  36.6 0.7 %collective-permute-done.14.rest_6_ = f32[4,8,128]{2,1,0:T(8,128)S(1)} collective-permute-done((f32[4,8,128]{2,1,0:T(8,128)S(1)}, f32[4,8,128]{2,1,0:T(8,128)S(1)}, u32[]{:S(2)}, u32[]{:S(2)}) %collective-permute-start.14) | collective-permute-done | bytes 16416 | tf_op jit(solution)/shard_map/ppermute | solution.py:429
  37.2 0.5 collective-permute-start.9
  37.8 0.6 %collective-permute-done.15.rest_7_ = f32[4,8,128]{2,1,0:T(8,128)S(1)} collective-permute-done((f32[4,8,128]{2,1,0:T(8,128)S(1)}, f32[4,8,128]{2,1,0:T(8,128)S(1)}, u32[]{:S(2)}, u32[]{:S(2)}) %collective-permute-start.15) | collective-permute-done | bytes 16416 | tf_op jit(solution)/shard_map/ppermute | solution.py:429
  38.4 7.1 %surfaces_first.1 = (f32[512,128]{1,0:T(8,128)S(1)}, f32[512,128]{1,0:T(8,128)S(1)}, f32[512,128]{1,0:T(8,128)S(1)}, s32[128,128]{1,0:T(8,128)S(1)}, f32[4,8,128]{2,1,0:T(8,128)S(1)}) custom-call(s32[86]{0:T(128)S(1)} %stack.287.plan_ref, s32[3,16,128]{2,1,0:T(8,128)S(1)} %copy-done.4, s32[3,16,128]{2,1,0:T(8,128)S(1)} %copy-done.5, ...), custom_call_target="tpu_custom_call" | custom-call | flops 4831838208 | bytes 4194304 | tf_op jit(solution)/shard_map/surfaces_first/pallas_call | solution.py:375
  45.5 8.0 %surfaces_last.1 = (f32[8,64,128]{2,1,0:T(8,128)}, f32[2,8,64,128]{3,2,1,0:T(8,128)}) custom-call(s32[86]{0:T(128)S(1)} %stack.287.plan_ref, s32[3,16,128]{2,1,0:T(8,128)S(1)} %copy-done.4, s32[3,16,128]{2,1,0:T(8,128)S(1)} %copy-done.5, f32[32,128]{1,0:T(8,128)S(1)} %copy-done.6, bf16[2,256,256]{2,1,0:T(8,128)(2,1)S(1)} %copy-done, ...), custom_call_target="tpu_custom_call" | custom-call | flops 4831838208 | bytes 4194304 | tf_op jit(solution)/shard_map/surfaces_last/pallas_call | solution.py:375
  (32 shorter events, 0.2 us)
Async XLA Ops:
  2.5 10.1 %collective-permute-start.1 = (f32[1,136,128]{2,1,0:T(8,128)S(1)}, f32[1,136,128]{2,1,0:T(8,128)S(1)}, u32[]{:S(2)}, u32[]{:S(2)}) collective-permute-start(f32[1,136,128]{2,1,0:T(8,128)S(1)} %pad_bitcast_fusion), channel_id=1, source_target_pairs={{0,8},{1,9},{2,10},{3,11},{4,12},{5,13},{6,14},{7,15},{8,16},{9,17... | collective-permute-start | bytes 208904 | tf_op jit(solution)/shard_map/ppermute | solution.py:429
  5.6 7.3 %collective-permute-start.2 = (f32[1,136,128]{2,1,0:T(8,128)S(1)}, f32[1,136,128]{2,1,0:T(8,128)S(1)}, u32[]{:S(2)}, u32[]{:S(2)}) collective-permute-start(f32[1,136,128]{2,1,0:T(8,128)S(1)} %pad_bitcast_fusion), channel_id=1, source_target_pairs={{0,16},{1,17},{2,18},{3,19},{4,20},{5,21},{6,22},{7,23},{8,24},{9,... | collective-permute-start | bytes 208904 | tf_op jit(solution)/shard_map/ppermute | solution.py:429
  8.2 4.9 %collective-permute-start.3 = (f32[1,136,128]{2,1,0:T(8,128)S(1)}, f32[1,136,128]{2,1,0:T(8,128)S(1)}, u32[]{:S(2)}, u32[]{:S(2)}) collective-permute-start(f32[1,136,128]{2,1,0:T(8,128)S(1)} %pad_bitcast_fusion), channel_id=1, source_target_pairs={{0,24},{1,25},{2,26},{3,27},{4,28},{5,29},{6,30},{7,31},{8,0},{9,1... | collective-permute-start | bytes 208904 | tf_op jit(solution)/shard_map/ppermute | solution.py:429
  9.5 6.9 %collective-permute-start.5 = (f32[1,136,128]{2,1,0:T(8,128)S(1)}, f32[1,136,128]{2,1,0:T(8,128)S(1)}, u32[]{:S(2)}, u32[]{:S(2)}) collective-permute-start(f32[1,136,128]{2,1,0:T(8,128)S(1)} %pad_bitcast_fusion), channel_id=1, source_target_pairs={{0,1},{1,0},{2,3},{3,2},{4,5},{5,4},{6,7},{7,6},{8,9},{9,8},{10,11... | collective-permute-start | bytes 208904 | tf_op jit(solution)/shard_map/ppermute | solution.py:429
  11.0 10.3 %collective-permute-start = (f32[1,136,128]{2,1,0:T(8,128)S(1)}, f32[1,136,128]{2,1,0:T(8,128)S(1)}, u32[]{:S(2)}, u32[]{:S(2)}) collective-permute-start(f32[1,136,128]{2,1,0:T(8,128)S(1)} %pad_bitcast_fusion), channel_id=1, source_target_pairs={{0,4},{1,5},{2,6},{3,7},{4,0},{5,1},{6,2},{7,3},{8,12},{9,13},{10,... | collective-permute-start | bytes 208904 | tf_op jit(solution)/shard_map/ppermute | solution.py:429
  13.1 6.8 %collective-permute-start.6 = (f32[3,136,128]{2,1,0:T(8,128)S(1)}, f32[3,136,128]{2,1,0:T(8,128)S(1)}, u32[]{:S(2)}, u32[]{:S(2)}) collective-permute-start(f32[3,136,128]{2,1,0:T(8,128)S(1)} %constant_dynamic-update-slice_fusion), channel_id=1, source_target_pairs={{0,1},{1,0},{2,3},{3,2},{4,5},{5,4},{6,7},{7,6},{8,9},{9,8},{10,11... | collective-permute-start | bytes 626696 | tf_op jit(solution)/shard_map/ppermute | solution.py:429
  14.7 23.6 %collective-permute-start.10 = (f32[4,136,128]{2,1,0:T(8,128)S(1)}, f32[4,136,128]{2,1,0:T(8,128)S(1)}, u32[]{:S(2)}, u32[]{:S(2)}) collective-permute-start(f32[4,136,128]{2,1,0:T(8,128)S(1)} %pad_maximum_fusion.rest_0_), channel_id=1, source_target_pairs={{0,2},{1,3},{2,0},{3,1},{4,6},{5,7},{6,4},{7,5},{8,10},{9,11},{10,... | collective-permute-start | bytes 835592 | tf_op jit(solution)/shard_map/ppermute | solution.py:429
  14.8 19.3 %collective-permute-start.4 = (f32[3,136,128]{2,1,0:T(8,128)S(1)}, f32[3,136,128]{2,1,0:T(8,128)S(1)}, u32[]{:S(2)}, u32[]{:S(2)}) collective-permute-start(f32[3,136,128]{2,1,0:T(8,128)S(1)} %constant_dynamic-update-slice_fusion), channel_id=1, source_target_pairs={{0,4},{1,5},{2,6},{3,7},{4,0},{5,1},{6,2},{7,3},{8,12},{9,13},{10,... | collective-permute-start | bytes 626696 | tf_op jit(solution)/shard_map/ppermute | solution.py:429
  19.9 18.4 %collective-permute-start.11 = (f32[4,136,128]{2,1,0:T(8,128)S(1)}, f32[4,136,128]{2,1,0:T(8,128)S(1)}, u32[]{:S(2)}, u32[]{:S(2)}) collective-permute-start(f32[4,136,128]{2,1,0:T(8,128)S(1)} %constant_dynamic-update-slice_fusion.5.rest_1_), channel_id=1, source_target_pairs={{0,2},{1,3},{2,0},{3,1},{4,6},{5,7},{6,4},{7,5},{8,10},{9,11},{10,... | collective-permute-start | bytes 835592 | tf_op jit(solution)/shard_map/ppermute | solution.py:429
  20.0 17.2 %collective-permute-start.7 = (f32[4,136,128]{2,1,0:T(8,128)S(1)}, f32[4,136,128]{2,1,0:T(8,128)S(1)}, u32[]{:S(2)}, u32[]{:S(2)}) collective-permute-start(f32[4,136,128]{2,1,0:T(8,128)S(1)} %constant_dynamic-update-slice_fusion.5.rest_1_), channel_id=1, source_target_pairs={{0,4},{1,5},{2,6},{3,7},{4,0},{5,1},{6,2},{7,3},{8,12},{9,13},{10,... | collective-permute-start | bytes 835592 | tf_op jit(solution)/shard_map/ppermute | solution.py:429
  21.4 8.1 %collective-permute-start.12 = (f32[4,8,128]{2,1,0:T(8,128)S(1)}, f32[4,8,128]{2,1,0:T(8,128)S(1)}, u32[]{:S(2)}, u32[]{:S(2)}) collective-permute-start(f32[4,8,128]{2,1,0:T(8,128)S(1)} %pad_maximum_fusion.1), channel_id=1, source_target_pairs={{0,4},{1,5},{2,6},{3,7},{4,0},{5,1},{6,2},{7,3},{8,12},{9,13},{10,... | collective-permute-start | bytes 49160 | tf_op jit(solution)/shard_map/ppermute | solution.py:429
  22.2 16.1 %copy-start.5 = (s32[3,16,128]{2,1,0:T(8,128)S(1)}, s32[3,16,128]{2,1,0:T(8,128)}, u32[]{:S(2)}) copy-start(s32[3,16,128]{2,1,0:T(8,128)} %constant.507.clone.ticks_ref) | copy-start | bytes 73732
  22.2 16.1 %copy-start.6 = (f32[32,128]{1,0:T(8,128)S(1)}, f32[32,128]{1,0:T(8,128)}, u32[]{:S(2)}) copy-start(f32[32,128]{1,0:T(8,128)} %constant.508.clone.small_ref) | copy-start | bytes 49156
  22.2 16.1 %copy-start.4 = (s32[3,16,128]{2,1,0:T(8,128)S(1)}, s32[3,16,128]{2,1,0:T(8,128)}, u32[]{:S(2)}) copy-start(s32[3,16,128]{2,1,0:T(8,128)} %constant.506.clone.fixed_ref) | copy-start | bytes 73732
  22.2 16.2 %copy-start.3 = (bf16[2,256,256]{2,1,0:T(8,128)(2,1)S(1)}, bf16[2,256,256]{2,1,0:T(8,128)(2,1)}, u32[]{:S(2)}) copy-start(bf16[2,256,256]{2,1,0:T(8,128)(2,1)} %constant.512.clone.odd_l) | copy-start | bytes 786436
  22.3 16.0 %copy-start.2 = (bf16[2,256,256]{2,1,0:T(8,128)(2,1)S(1)}, bf16[2,256,256]{2,1,0:T(8,128)(2,1)}, u32[]{:S(2)}) copy-start(bf16[2,256,256]{2,1,0:T(8,128)(2,1)} %constant.511.clone.odd_h) | copy-start | bytes 786436
  22.5 15.8 %copy-start = (bf16[2,256,256]{2,1,0:T(8,128)(2,1)S(1)}, bf16[2,256,256]{2,1,0:T(8,128)(2,1)}, u32[]{:S(2)}) copy-start(bf16[2,256,256]{2,1,0:T(8,128)(2,1)} %constant.509.clone.even_h) | copy-start | bytes 786436
  22.5 15.8 %copy-start.1 = (bf16[2,256,256]{2,1,0:T(8,128)(2,1)S(1)}, bf16[2,256,256]{2,1,0:T(8,128)(2,1)}, u32[]{:S(2)}) copy-start(bf16[2,256,256]{2,1,0:T(8,128)(2,1)} %constant.510.clone.even_l) | copy-start | bytes 786436
  29.4 4.6 %collective-permute-start.13 = (f32[4,8,128]{2,1,0:T(8,128)S(1)}, f32[4,8,128]{2,1,0:T(8,128)S(1)}, u32[]{:S(2)}, u32[]{:S(2)}) collective-permute-start(f32[4,8,128]{2,1,0:T(8,128)S(1)} %pad_maximum_fusion.1), channel_id=1, source_target_pairs={{0,5},{1,4},{2,7},{3,6},{4,1},{5,0},{6,3},{7,2},{8,13},{9,12},{10,... | collective-permute-start | bytes 49160 | tf_op jit(solution)/shard_map/ppermute | solution.py:429
  34.1 3.2 %collective-permute-start.14 = (f32[4,8,128]{2,1,0:T(8,128)S(1)}, f32[4,8,128]{2,1,0:T(8,128)S(1)}, u32[]{:S(2)}, u32[]{:S(2)}) collective-permute-start(f32[4,8,128]{2,1,0:T(8,128)S(1)} %pad_maximum_fusion.1), channel_id=1, source_target_pairs={{0,6},{1,7},{2,4},{3,5},{4,2},{5,3},{6,0},{7,1},{8,14},{9,15},{10,... | collective-permute-start | bytes 49160 | tf_op jit(solution)/shard_map/ppermute | solution.py:429
  34.1 4.2 %collective-permute-start.15 = (f32[4,8,128]{2,1,0:T(8,128)S(1)}, f32[4,8,128]{2,1,0:T(8,128)S(1)}, u32[]{:S(2)}, u32[]{:S(2)}) collective-permute-start(f32[4,8,128]{2,1,0:T(8,128)S(1)} %pad_maximum_fusion.1), channel_id=1, source_target_pairs={{0,7},{1,6},{2,5},{3,4},{4,3},{5,2},{6,1},{7,0},{8,15},{9,14},{10,... | collective-permute-start | bytes 49160 | tf_op jit(solution)/shard_map/ppermute | solution.py:429
  37.2 8.2 %collective-permute-start.8 = (f32[4,136,128]{2,1,0:T(8,128)S(1)}, f32[4,136,128]{2,1,0:T(8,128)S(1)}, u32[]{:S(2)}, u32[]{:S(2)}) collective-permute-start(f32[4,136,128]{2,1,0:T(8,128)S(1)} %constant_dynamic-update-slice_fusion.3.rest_0_), channel_id=1, source_target_pairs={{0,2},{1,3},{2,0},{3,1},{4,6},{5,7},{6,4},{7,5},{8,10},{9,11},{10,... | collective-permute-start | bytes 835592 | tf_op jit(solution)/shard_map/ppermute | solution.py:429
  37.2 8.3 %collective-permute-start.9 = (f32[4,136,128]{2,1,0:T(8,128)S(1)}, f32[4,136,128]{2,1,0:T(8,128)S(1)}, u32[]{:S(2)}, u32[]{:S(2)}) collective-permute-start(f32[4,136,128]{2,1,0:T(8,128)S(1)} %collective-permute-done.7.rest_1_), channel_id=1, source_target_pairs={{0,2},{1,3},{2,0},{3,1},{4,6},{5,7},{6,4},{7,5},{8,10},{9,11},{10,... | collective-permute-start | bytes 835592 | tf_op jit(solution)/shard_map/ppermute | solution.py:429
